TPU v7x, 32 devices: a whole 2x2x4 slice. The times are simulated.
32 devices in a mesh: groups: 2 (over y), heads: 4 (over x, core), tm: 4 (over z).
Axes of the slice: x: 2, y: 2, z: 4, core: 2. Of those that a mesh axis runs over, the one named last changes fastest.
Arguments:
- queries: bfloat16 [256, 8192], P('groups', 'heads'), parts along dimension 0, may hold values from -6 to 6
- cache_keys: bfloat16 [8192, 8192], P(('groups', 'tm'), 'heads'), parts along dimension 0, may hold values from -650 to 650
- cache_values: bfloat16 [8192, 8192], P(('groups', 'tm'), 'heads'), parts along dimension 0, may hold values from -6 to 6
- residual: bfloat16 [256, 8192], P('groups', 'tm'), parts along dimension 0, may hold values from -20 to 20
- out_weight: bfloat16 [8192, 8192], P('heads', 'tm'), may hold values from -0.0625 to 0.0625
- norm_gain: float32 [8192], P('tm'), may hold values from 0.1 to 1.9
- cond_weight: bfloat16 [8192, 1536], P('tm', 'heads'), may hold values from -0.0625 to 0.0625
- in_weight: bfloat16 [1152, 1536], replicated, may hold values from -0.1875 to 0.1875
- head_out: bfloat16 [1536, 1152], replicated, may hold values from -0.15625 to 0.15625
- start_state: float32 [256, 1152], P(('groups', 'heads')), parts along dimension 0, may hold values from -6 to 6
- noise_draws: bfloat16 [256, 8, 1152], P(('groups', 'heads'), 'tm'), parts along dimension 0, may hold values from -6 to 6
- positions: int32 [256], P('groups'), parts along dimension 0, may hold values from 0 to 4095
- cache_length: int32 [2], P('groups'), parts along dimension 0, may hold values from 2048 to 4096
- plan: int32 [9], replicated, may hold values from 0 to 1000, as said below
Outputs:
- states: float32 [256, 8, 1152], P(('groups', 'heads'), 'tm'), parts along dimension 0
There are 2 independent parts, one for each index of `groups`. A program takes and returns all parts, laid end to end along the dimension named above; an argument that names none is the same for every part. Nothing has to cross between parts.
Inputs may be any that keep to these rules, and one draw needn't show every extreme that they name: `plan`: strictly decreasing; the first entry is 1000 and the last is 0.
All inputs are finite; a program needn't handle non-finite values.
Results may differ from a plain program's by a relative error of at most 0.0028.
Values may be sent and summed in bfloat16 or wider, within the bound.
No kernel may reach another device: no remote copies, remote signals or barrier semaphores. Data moves between devices by JAX's collectives and lax.ppermute only.
A program may use at most 128 MiB of HBM per device.

v0:
```python
import math

import jax
import jax.numpy as jnp
from jax import lax
from jax.sharding import PartitionSpec as P

D = 8192
HD = 128
WIDTH = 1536
CHAN = 1152
SWEEPS = 3


def merged(part, axis, combine):
    gathered = jax.tree.map(lambda a: lax.all_gather(a, axis), part)

    def take(source):
        return jax.tree.map(lambda a: lax.dynamic_index_in_dim(a, source, 0, False), gathered)

    return lax.fori_loop(
        1, lax.axis_size(axis), lambda source, state: combine(state, take(source)), take(0)
    )


def rotate(values, angle_pos):
    head_feature_width = values.shape[-1]
    half_dim = head_feature_width // 2
    frequencies = jnp.exp(
        -math.log(10000.0) * 2.0 * jnp.arange(half_dim, dtype=jnp.float32) / head_feature_width
    )
    angles = angle_pos[:, None] * frequencies[None, :]
    cosine = jnp.cos(angles)[:, None, :]
    sine_part = jnp.sin(angles)[:, None, :]
    paired = values.astype(jnp.float32).reshape(values.shape[0], values.shape[1], half_dim, 2)
    real_part = paired[..., 0]
    imag_part = paired[..., 1]
    turned = jnp.stack(
        [real_part * cosine - imag_part * sine_part, real_part * sine_part + imag_part * cosine],
        axis=-1,
    )
    return turned.reshape(values.shape).astype(jnp.bfloat16)


def time_terms(levels, hidden_width):
    half_width = hidden_width // 2
    frequencies = jnp.exp(
        -math.log(10000.0) * jnp.arange(half_width, dtype=jnp.float32) / half_width
    )
    angles = levels[:-1, None] * frequencies[None, :]
    embedding = jnp.concatenate([jnp.sin(angles), jnp.cos(angles)], axis=1)
    step_size = (levels[:-1] - levels[1:]) / 1000.0
    return (embedding, step_size, jnp.sqrt(step_size))


def block_attend(rotary_applied, block_key_rows, block_value_rows, valid_keys):
    head_feature_width = rotary_applied.shape[-1]
    attention_logits = jnp.einsum(
        "orp,brp->orb", rotary_applied, block_key_rows, preferred_element_type=jnp.float32
    ) * (1.0 / math.sqrt(head_feature_width))
    masked = jnp.where(valid_keys[None, None, :], attention_logits, jnp.float32(-1e30))
    block_max = jnp.max(masked, axis=2)
    weights = jnp.where(
        valid_keys[None, None, :], jnp.exp(masked - block_max[:, :, None]), jnp.float32(0.0)
    )
    block_total = jnp.sum(weights, axis=2)
    block_output_part = jnp.einsum(
        "pzu,uzx->pzx",
        weights.astype(jnp.bfloat16),
        block_value_rows,
        preferred_element_type=jnp.float32,
    )
    return (block_max, block_total, block_output_part)


def combine(earlier, latter):
    max_one, total_one, out_one = earlier
    max_two, total_two, out_two = latter
    highest = jnp.maximum(max_one, max_two)
    scale_one = jnp.exp(max_one - highest)
    scale_two = jnp.exp(max_two - highest)
    merged_total = total_one * scale_one + total_two * scale_two
    merged_out = out_one * scale_one[:, :, None] + out_two * scale_two[:, :, None]
    return (highest, merged_total, merged_out)


def prefix_sum(totals):
    gathered = lax.all_gather(totals[None], "tm", axis=0, tiled=True)
    lower_mask = (jnp.arange(gathered.shape[0], dtype=jnp.int32) < lax.axis_index("tm")).astype(
        jnp.float32
    )
    return jnp.sum(gathered * lower_mask[:, None, None], axis=0)


def shards(
    queries,
    cache_keys,
    cache_values,
    residual,
    out_weight,
    norm_gain,
    cond_weight,
    in_weight,
    head_out,
    start_state,
    noise_draws,
    positions,
    cache_length,
    plan,
):
    row_total = queries.shape[0]
    local_heads = queries.shape[1] // HD
    key_count = cache_keys.shape[0]
    time_index = lax.axis_index("tm")
    head_index = lax.axis_index("heads")
    rotary_applied = rotate(
        queries.reshape(row_total, local_heads, HD), positions.astype(jnp.float32)
    )
    key_pos = time_index * key_count + jnp.arange(key_count, dtype=jnp.int32)
    valid_keys = key_pos < cache_length[0]
    partial_value = block_attend(
        rotary_applied,
        cache_keys.reshape(key_count, local_heads, HD),
        cache_values.reshape(key_count, local_heads, HD),
        valid_keys,
    )
    merged_max, merged_total, merged_out = merged(partial_value, "tm", combine)
    attended = (
        (merged_out / merged_total[:, :, None])
        .reshape(row_total, local_heads * HD)
        .astype(jnp.bfloat16)
    )
    row_each = start_state.shape[0]
    first_row = head_index * row_each
    projected = lax.psum(jnp.dot(attended, out_weight, preferred_element_type=jnp.float32), "heads")
    hidden = residual.astype(jnp.float32) + projected
    hidden_rows = lax.dynamic_slice_in_dim(hidden, first_row, row_each, 0)
    squares = jnp.sum(hidden_rows * hidden_rows, axis=1)
    scaled = (hidden * norm_gain[None, :]).astype(jnp.bfloat16)
    cond_part = jnp.dot(scaled, cond_weight, preferred_element_type=jnp.float32)
    square_sum, cond_sum = lax.psum((squares, cond_part), "tm")
    inverse = lax.rsqrt(square_sum / D + 1e-06)
    condition = (
        lax.all_to_all(cond_sum, "heads", split_axis=0, concat_axis=1, tiled=True)
        * inverse[:, None]
    )
    time_each = noise_draws.shape[1]
    levels = lax.dynamic_slice_in_dim(plan, time_index * time_each, time_each + 1, 0).astype(
        jnp.float32
    )
    embedding, step_size, noise_scale = time_terms(levels, in_weight.shape[1])
    noise_term = noise_scale[None, :, None] * noise_draws.astype(jnp.float32)
    states = jnp.broadcast_to(start_state[:, None, :], noise_draws.shape)
    for sweep_index in range(SWEEPS):
        flat_states = states.astype(jnp.bfloat16).reshape(row_each * time_each, CHAN)
        preact = jnp.dot(flat_states, in_weight, preferred_element_type=jnp.float32).reshape(
            row_each, time_each, WIDTH
        )
        preact = preact + condition[:, None, :] + embedding[None]
        action = jax.nn.silu(preact).astype(jnp.bfloat16)
        drift_term = jnp.dot(
            action.reshape(row_each * time_each, WIDTH),
            head_out,
            preferred_element_type=jnp.float32,
        ).reshape(row_each, time_each, CHAN)
        increment = step_size[None, :, None] * drift_term + noise_term
        running = jnp.cumsum(increment, axis=1)
        before = prefix_sum(running[:, -1, :])
        states = start_state[:, None, :] + before[:, None, :] + (running - increment)
    return states


def solution(mesh):
    placed = (
        P("groups", "heads"),
        P(("groups", "tm"), "heads"),
        P(("groups", "tm"), "heads"),
        P("groups", "tm"),
        P("heads", "tm"),
        P("tm"),
        P("tm", "heads"),
        P(),
        P(),
        P(("groups", "heads"), None),
        P(("groups", "heads"), "tm", None),
        P("groups"),
        P("groups"),
        P(),
    )
    return jax.shard_map(
        shards,
        mesh=mesh,
        in_specs=placed,
        out_specs=P(("groups", "heads"), "tm", None),
        check_vma=False,
    )
```

profile of v0, /device:TPU:0, one launch (start us, length us, event | category | flops | bytes accessed | tf_op | source)
XLA Modules:
  0.0 314.8 jit_solution(7323992095895758402)
XLA Ops:
  12.9 2.9 subtract_convert_fusion
  17.1 4.3 %bitcast_reduce_fusion = (f32[128,16]{0,1:T(8,128)S(1)}, f32[16,128,1024]{2,1,0:T(8,128)S(1)}) fusion(pred[1024]{0:T(1024)(128)(4,1)S(1)} %add_compare_fusion, bf16[128,16,128]{0,2,1:T(8,128)(2,1)S(1)} %bitcast.134, bf16[1024,2048]{1,0:T(8,128)(2,1)} %param.17), kind=kOutput, calls=%fused_computation.10 | convolution fusion | flops 543160320 | bytes 13116416 | tf_op jit(solution)/shard_map/orp,brp->orb/dot_general | solution.py:58
  21.4 3.2 %copy-done.1 = f32[16,128,1024]{2,1,0:T(8,128)} copy-done((f32[16,128,1024]{2,1,0:T(8,128)}, f32[16,128,1024]{2,1,0:T(8,128)S(1)}, u32[]{:S(2)}) %copy-start.1) | copy-done | bytes 8388632
  24.6 3.5 %fusion.67 = f32[128,16,128]{2,0,1:T(8,128)} fusion(f32[16,128,1024]{2,1,0:T(8,128)S(1)} %get-tuple-element.228, f32[128,16]{0,1:T(8,128)S(1)} %get-tuple-element.227, pred[1024]{0:T(1024)(128)(4,1)S(1)} %add_compare_fusion, bf16[1024,2048]{1,0:T(8,128)(2,1)S(1)} %copy-done.9), kind=kOutput, calls=%fused_computation.52 | convolution fusion | flops 547356672 | bytes 13640704 | tf_op jit(solution)/shard_map/pzu,uzx->pzx/dot_general | solution.py:67
  28.2 14.8 %all-gather = f32[512,16]{0,1:T(8,128)S(1)} all-gather(f32[128,16]{0,1:T(8,128)S(1)} %get-tuple-element.227), channel_id=2, replica_groups=mesh['groups'=2,'heads'=4,'tm'=4] {'tm'}, dimensions={0}, use_global_device_ids=true | all-gather | bytes 40960 | tf_op jit(solution)/shard_map/all_gather | solution.py:16
  45.6 4.6 %fusion.5 = f32[128,16]{0,1:T(8,128)S(1)} fusion(f32[16,128,1024]{2,1,0:T(8,128)} %copy-done.1, f32[128,16]{0,1:T(8,128)S(1)} %get-tuple-element.227, pred[1024]{0:T(1024)(128)(4,1)S(1)} %add_compare_fusion), kind=kLoop, calls=%fused_computation.15 | loop fusion | flops 10483712 | bytes 8406016 | tf_op jit(solution)/shard_map/reduce_sum | solution.py:66
  50.3 13.7 %all-gather.1 = f32[512,16]{0,1:T(8,128)S(1)} all-gather(f32[128,16]{0,1:T(8,128)S(1)} %fusion.5), channel_id=3, replica_groups=mesh['groups'=2,'heads'=4,'tm'=4] {'tm'}, dimensions={0}, use_global_device_ids=true | all-gather | bytes 40960 | tf_op jit(solution)/shard_map/all_gather | solution.py:16
  69.3 42.9 %all-gather.8.cloned.1.call-done = f32[512,16,128]{2,0,1:T(8,128)} async-done(((f32[128,16,128]{2,0,1:T(8,128)}), f32[512,16,128]{2,0,1:T(8,128)}) %all-gather.8.cloned.1.call-update) | async-done | bytes 4194320 | tf_op jit(solution)/shard_map/all_gather | solution.py:16
  115.1 24.9 %while.19 = (s32[]{:T(128)}, f32[128,16]{0,1:T(8,128)}, f32[128,16]{0,1:T(8,128)}, f32[128,16,128]{2,1,0:T(8,128)}, f32[4,128,16]{1,0,2:T(4,128)}, /*index=5*/f3...) while((s32[]{:T(128)}, f32[128,16]{0,1:T(8,128)}, ...), condition=%wide.region_3.4_spmd, body=%wide.region_2.3_spmd.sunk | while | flops 798725 | bytes 5390479 | solution.py:21
  120.0 3.4 %fusion.123 = f32[128,16,128]{2,1,0:T(8,128)} fusion(f32[1,128,16,128]{3,1,0,2:T(8,128)S(1)} %constant_dynamic-slice_fusion.6, f32[128,16,128]{2,1,0:T(8,128)} %get-tuple-element.297, f32[128,16]{1,0:T(8,128)} %copy.79, f32[128,16]{1,0:T(8,128)} %copy.80), kind=kLoop, calls=%fused_computation.2.clone.1 | loop fusion | flops 786432 | bytes 3162112 | tf_op jit(solution)/shard_map/while/body/eval_jaxpr/add | solution.py:83
  128.3 3.4 %fusion.123 = f32[128,16,128]{2,1,0:T(8,128)} fusion(f32[1,128,16,128]{3,1,0,2:T(8,128)S(1)} %constant_dynamic-slice_fusion.6, f32[128,16,128]{2,1,0:T(8,128)} %get-tuple-element.297, f32[128,16]{1,0:T(8,128)} %copy.79, f32[128,16]{1,0:T(8,128)} %copy.80), kind=kLoop, calls=%fused_computation.2.clone.1 | loop fusion | flops 786432 | bytes 3162112 | tf_op jit(solution)/shard_map/while/body/eval_jaxpr/add | solution.py:83
  136.6 3.4 %fusion.123 = f32[128,16,128]{2,1,0:T(8,128)} fusion(f32[1,128,16,128]{3,1,0,2:T(8,128)S(1)} %constant_dynamic-slice_fusion.6, f32[128,16,128]{2,1,0:T(8,128)} %get-tuple-element.297, f32[128,16]{1,0:T(8,128)} %copy.79, f32[128,16]{1,0:T(8,128)} %copy.80), kind=kLoop, calls=%fused_computation.2.clone.1 | loop fusion | flops 786432 | bytes 3162112 | tf_op jit(solution)/shard_map/while/body/eval_jaxpr/add | solution.py:83
  143.0 5.7 %fusion.73 = f32[128,2048]{1,0:T(8,128)} fusion(bf16[2048,2048]{1,0:T(8,128)(2,1)} %param.20, bf16[16,8,16,128]{3,2,1,0:T(8,128)(2,1)S(1)} %bitcast.130), kind=kOutput, calls=%fused_computation.60 | convolution fusion | flops 1073741824 | bytes 9961472 | tf_op jit(solution)/shard_map/dot_general | solution.py:135
  150.4 33.3 %all-reduce.3.cloned.1.call-done = f32[128,2048]{1,0:T(8,128)} async-done(((f32[128,2048]{1,0:T(8,128)}), f32[128,2048]{1,0:T(8,128)}) %all-reduce.3.cloned.1.call-update) | async-done | bytes 1048592 | tf_op jit(solution)/shard_map/psum | solution.py:135
  191.1 12.3 %psum.23 = f32[32]{0:T(128)} all-reduce(f32[32]{0:T(128)} %multiply_reduce_fusion.3), channel_id=1, replica_groups=mesh['groups'=2,'heads'=4,'tm'=4] {'tm'}, use_global_device_ids=true, to_apply=%region_7.8 | all-reduce | flops 32 | bytes 256 | tf_op jit(solution)/shard_map/psum | solution.py:141
  203.4 21.0 %all-reduce.5.cloned.1.call-done = f32[4,32,384]{2,1,0:T(8,128)} async-done(((f32[4,32,384]{2,1,0:T(8,128)}), f32[4,32,384]{2,1,0:T(8,128)}) %all-reduce.5.cloned.1.call-update) | async-done | bytes 196624 | tf_op jit(solution)/shard_map/psum | solution.py:141
  224.4 4.0 %all-to-all-start = ((f32[4,32,384]{2,1,0:T(8,128)}), f32[4,32,384]{2,1,0:T(8,128)}, u32[]{:S(2)}, u32[]{:S(2)}) async-start(f32[4,32,384]{2,1,0:T(8,128)} %all-reduce.5.cloned.1.call-done), calls=%async_computation | async-start | bytes 393216 | tf_op jit(solution)/shard_map/all_to_all | solution.py:144
  229.5 4.2 %all-to-all-done = f32[4,32,384]{2,1,0:T(8,128)} async-done(((f32[4,32,384]{2,1,0:T(8,128)}), f32[4,32,384]{2,1,0:T(8,128)}, u32[]{:S(2)}, u32[]{:S(2)}) %all-to-all-start) | async-done | bytes 196640 | tf_op jit(solution)/shard_map/all_to_all | solution.py:144
  236.1 4.2 %fusion.46 = f32[32,2,1152]{2,0,1:T(8,128)} fusion(bf16[1536,1152]{1,0:T(8,128)(2,1)S(1)} %copy-done, bf16[1152,1536]{1,0:T(8,128)(2,1)} %param.23, f32[2,1536]{1,0:T(2,128)S(1)} %pad_maximum_fusion.1, f32[32,1536]{1,0:T(8,128)} %broadcast_multiply_fusion, f32[2]{0:T(128)S(1)} %get-tuple-element.216, f32[2]{0:T(128)} %get-tuple-element.217, ...), kind=kOutput, calls=%fused_computation.45 | convolution fusion | flops 453967872 | bytes 7802896 | tf_op jit(solution)/shard_map/dot_general | solution.py:161
  242.0 15.7 %all-gather.3 = f32[128,1,1152]{2,0,1:T(8,128)S(1)} all-gather(f32[32,1,1152]{2,0,1:T(8,128)S(1)} %slice.40), channel_id=5, replica_groups=mesh['groups'=2,'heads'=4,'tm'=4] {'tm'}, dimensions={0}, use_global_device_ids=true | all-gather | bytes 737280 | tf_op jit(solution)/shard_map/all_gather | solution.py:88
  260.1 4.4 %fusion.43 = f32[32,2,1152]{2,0,1:T(8,128)} fusion(bf16[1536,1152]{1,0:T(8,128)(2,1)S(1)} %copy-done, bf16[1152,1536]{1,0:T(8,128)(2,1)} %param.23, f32[2,1536]{1,0:T(2,128)S(1)} %pad_maximum_fusion.1, f32[32,1536]{1,0:T(8,128)} %broadcast_multiply_fusion, f32[32,2,1152]{2,0,1:T(8,128)} %copy-done.4, f32[32,2,1152]{2,0,1:T(8,128)} %fusion.46, ...), kind=kOutput, calls=%fused_computation.44 | convolution fusion | flops 454189056 | bytes 8466448 | tf_op jit(solution)/shard_map/dot_general | solution.py:161
  266.1 15.4 %all-gather.4 = f32[128,1,1152]{2,0,1:T(8,128)S(1)} all-gather(f32[32,1,1152]{2,0,1:T(8,128)S(1)} %slice.41), channel_id=6, replica_groups=mesh['groups'=2,'heads'=4,'tm'=4] {'tm'}, dimensions={0}, use_global_device_ids=true | all-gather | bytes 737280 | tf_op jit(solution)/shard_map/all_gather | solution.py:88
  283.9 4.4 %fusion.40 = f32[32,2,1152]{2,0,1:T(8,128)} fusion(bf16[1536,1152]{1,0:T(8,128)(2,1)S(1)} %copy-done, bf16[1152,1536]{1,0:T(8,128)(2,1)} %param.23, f32[2,1536]{1,0:T(2,128)S(1)} %pad_maximum_fusion.1, f32[32,1536]{1,0:T(8,128)} %broadcast_multiply_fusion, f32[32,2,1152]{2,0,1:T(8,128)} %copy-done.3, f32[32,2,1152]{2,0,1:T(8,128)} %fusion.43, ...), kind=kOutput, calls=%fused_computation.43 | convolution fusion | flops 454189056 | bytes 8466448 | tf_op jit(solution)/shard_map/dot_general | solution.py:161
  289.3 15.3 %all-gather.5 = f32[128,1,1152]{2,0,1:T(8,128)S(1)} all-gather(f32[32,1,1152]{2,0,1:T(8,128)S(1)} %slice.42), channel_id=7, replica_groups=mesh['groups'=2,'heads'=4,'tm'=4] {'tm'}, dimensions={0}, use_global_device_ids=true | all-gather | bytes 737280 | tf_op jit(solution)/shard_map/all_gather | solution.py:88
  (84 shorter events, 60.6 us)
Async XLA Ops:
  6.5 229.6 %copy-start = (bf16[1536,1152]{1,0:T(8,128)(2,1)S(1)}, bf16[1536,1152]{1,0:T(8,128)(2,1)}, u32[]{:S(2)}) copy-start(bf16[1536,1152]{1,0:T(8,128)(2,1)} %param.24) | copy-start | bytes 10616836
  6.5 105.6 %all-gather.8.cloned.1.call-start = ((), (), s32[]{:S(2)}) async-start(), calls=%async_computation.3 | async-start | bytes 5242880 | tf_op jit(solution)/shard_map/all_gather | solution.py:16
  17.0 7.6 %copy-start.9 = (bf16[1024,2048]{1,0:T(8,128)(2,1)S(1)}, bf16[1024,2048]{1,0:T(8,128)(2,1)}, u32[]{:S(2)}) copy-start(bf16[1024,2048]{1,0:T(8,128)(2,1)} %param.18) | copy-start | bytes 12582916
  21.4 3.2 %copy-start.1 = (f32[16,128,1024]{2,1,0:T(8,128)}, f32[16,128,1024]{2,1,0:T(8,128)S(1)}, u32[]{:S(2)}) copy-start(f32[16,128,1024]{2,1,0:T(8,128)S(1)} %get-tuple-element.228) | copy-start | bytes 25165828
  28.1 155.6 %all-reduce.3.cloned.1.call-start = ((), (), s32[]{:S(2)}) async-start(), calls=%async_computation.1 | async-start | bytes 2097152 | tf_op jit(solution)/shard_map/psum | solution.py:135
  43.0 0.6 copy-start.6
  64.0 0.6 copy-start.5
  142.9 6.0 %copy-start.10 = (s32[9]{0:T(128)S(1)}, s32[9]{0:T(128)}, u32[]{:S(2)}) copy-start(s32[9]{0:T(128)} %param.29) | copy-start | bytes 112
  143.0 6.7 %copy-start.7 = (f32[768]{0:T(1024)S(1)}, f32[768]{0:T(1024)}, u32[]{:S(2)}) copy-start(f32[768]{0:T(1024)} %multiply_exponential_fusion) | copy-start | bytes 9220
  143.0 43.2 %copy-start.8 = (f32[2048]{0:T(1024)S(1)}, f32[2048]{0:T(1024)}, u32[]{:S(2)}) copy-start(f32[2048]{0:T(1024)} %param.21) | copy-start | bytes 24580
  148.7 75.7 %all-reduce.5.cloned.1.call-start = ((), (), s32[]{:S(2)}) async-start(), calls=%async_computation.2 | async-start | bytes 393216 | tf_op jit(solution)/shard_map/psum | solution.py:141
  185.2 1.0 copy-start.2
  224.4 9.4 %all-to-all-start = ((f32[4,32,384]{2,1,0:T(8,128)}), f32[4,32,384]{2,1,0:T(8,128)}, u32[]{:S(2)}, u32[]{:S(2)}) async-start(f32[4,32,384]{2,1,0:T(8,128)} %all-reduce.5.cloned.1.call-done), calls=%async_computation | async-start | bytes 393216 | tf_op jit(solution)/shard_map/all_to_all | solution.py:144
  241.2 0.7 copy-start.4
  265.4 0.7 copy-start.3
Sparse Core Ops, SparseCore 0:
  28.3 83.8 all-gather.7
  148.8 34.8 all-reduce.2
  188.9 35.4 all-reduce.4
where the time goes:
time: 316 us; the launch traced here: 315 us
  waiting for transfers between devices  101 us (32%)
  blocking collectives  87.3 us (28%)
  other arithmetic  49 us (16%)
  local copies, waits for them, and re-layouts  29.8 us (9%)
  matrix products  28.9 us (9%)
  between operations  14.1 us (4%)
  starting transfers between devices  4.26 us (1%)
    all_gather x3, blocking collectives, prefix_sum(): gathered = lax.all_gather(totals[None], 'tm', axis=0, tiled=True)  46.4 us
    all_gather x1, waiting for transfers between devices, merged(): gathered = jax.tree.map(lambda a: lax.all_gather(a, axis), part)  42.9 us
    psum x1, waiting for transfers between devices, shards(): lax.psum(jnp.dot(attended, out_weight, preferred_element_type=jnp.float32...  33.3 us
    all_gather x2, blocking collectives, merged(): gathered = jax.tree.map(lambda a: lax.all_gather(a, axis), part)  28.6 us
    psum x1, waiting for transfers between devices, shards(): square_sum, cond_sum = lax.psum((squares, cond_part), 'tm')  21 us
    dot_general x3, matrix products, shards(): jnp.dot(action.reshape(row_each * time_each, WIDTH), head_out, preferred_...  12.9 us
    psum x1, blocking collectives, shards(): square_sum, cond_sum = lax.psum((squares, cond_part), 'tm')  12.3 us
    add x3, other arithmetic, combine(): out_one * scale_one[:, :, None] + out_two * scale_two[:, :, None]  10.2 us
  transfers between devices with their start and end apart: 4, of which 4 were waited for; matrix products, arithmetic and copies ran while one was open for 5% of the time, Pallas kernels for 0%

commit v1 on v0

v1 whole, which is shorter than its diff:
```python
import functools
import math

import jax
import jax.numpy as jnp
from jax import lax
from jax.experimental import pallas as pl
from jax.experimental.pallas import tpu as pltpu
from jax.sharding import PartitionSpec as P

HD = 128
SWEEPS = 3
LANES = 128


def swap(values, axis, distance):
    size = lax.axis_size(axis)
    return lax.ppermute(values, axis, [(i, i ^ distance) for i in range(size)])


def pick(values, index):
    return lax.dynamic_index_in_dim(values, index, 0, False)


def whole(shape):
    return pl.BlockSpec(shape, lambda *_: (0,) * len(shape))


def cost(flops, transcendentals, *arrays):
    moved = sum(math.prod(a.shape) * jnp.dtype(a.dtype).itemsize for a in arrays)
    return pl.CostEstimate(flops=flops, bytes_accessed=moved, transcendentals=transcendentals)


def rotation_tables(positions):
    pair = jnp.arange(HD, dtype=jnp.int32) // 2
    frequencies = jnp.exp(-math.log(10000.0) * 2.0 * pair.astype(jnp.float32) / HD)
    angles = positions.astype(jnp.float32)[:, None] * frequencies[None, :]
    sign = jnp.where(jnp.arange(HD) % 2 == 0, -1.0, 1.0).astype(jnp.float32)
    return jnp.cos(angles), jnp.sin(angles) * sign[None, :]


def attend_kernel(groups, share, step_heads, info, q_ref, k_ref, v_ref, cos_ref, sin_ref, *refs):
    outs, stats, table = refs[:groups], refs[groups : 2 * groups], refs[2 * groups]
    step = pl.program_id(0)
    group_steps = share // step_heads
    rows, keys = q_ref.shape[0], k_ref.shape[0]
    valid = lax.broadcasted_iota(jnp.int32, (1, keys), 1) < info[1]
    even = lax.broadcasted_iota(jnp.int32, (rows, HD), 1) % 2 == 0
    lane = lax.broadcasted_iota(jnp.int32, (rows, LANES), 1)
    scale = 1.0 / math.sqrt(HD)
    results = []
    for i in range(step_heads):
        at = slice(i * HD, (i + 1) * HD)
        wide = q_ref[:, at].astype(jnp.float32)
        partner = jnp.where(even, pltpu.roll(wide, HD - 1, 1), pltpu.roll(wide, 1, 1))
        rotated = (wide * cos_ref[...] + partner * sin_ref[...]).astype(jnp.bfloat16)
        scores = lax.dot_general(
            rotated, k_ref[:, at], (((1,), (1,)), ((), ())), preferred_element_type=jnp.float32
        )
        masked = jnp.where(valid, scores * scale, jnp.float32(-1e30))
        block_max = jnp.max(masked, axis=1, keepdims=True)
        weights = jnp.where(valid, jnp.exp(masked - block_max), 0.0)
        block_total = jnp.sum(weights, axis=1, keepdims=True)
        block_out = jnp.dot(
            weights.astype(jnp.bfloat16), v_ref[:, at], preferred_element_type=jnp.float32
        )
        results.append((block_max, block_total, block_out.astype(jnp.bfloat16)))
    for group in range(groups):
        for part in range(group_steps):

            @pl.when(step == group * group_steps + part)
            def _(group=group, part=part):
                held = table[...] if part else jnp.zeros((rows, LANES), jnp.float32)
                for i, (block_max, block_total, block_out) in enumerate(results):
                    head = part * step_heads + i
                    outs[group][:, head * HD : (head + 1) * HD] = block_out
                    held = jnp.where(lane == head, block_max, held)
                    held = jnp.where(lane == share + head, block_total, held)
                if part == group_steps - 1:
                    stats[group][...] = held.T[: 2 * share]
                else:
                    table[...] = held


def attend(queries, keys, values, cosine, sine, first, valid_count, groups, share):
    rows = queries.shape[0]
    key_count = keys.shape[0]
    step_heads = 2 if share % 2 == 0 else 1
    per = share // step_heads
    width = step_heads * HD
    info = jnp.stack([first, valid_count]).astype(jnp.int32)

    def column(step, info):
        a = jnp.int32(0)
        for g, value in enumerate(groups):
            a = jnp.where(step // per == g, value, a)
        return (0, (info[0] ^ a) * per + step % per)

    n = len(groups)
    result = pl.pallas_call(
        functools.partial(attend_kernel, n, share, step_heads),
        grid_spec=pltpu.PrefetchScalarGridSpec(
            num_scalar_prefetch=1,
            grid=(n * per,),
            in_specs=[
                pl.BlockSpec((rows, width), column),
                pl.BlockSpec((key_count, width), column),
                pl.BlockSpec((key_count, width), column),
                whole((rows, HD)),
                whole((rows, HD)),
            ],
            out_specs=[whole((rows, share * HD))] * n + [whole((2 * share, rows))] * n,
            scratch_shapes=[pltpu.VMEM((rows, LANES), jnp.float32)],
        ),
        out_shape=[jax.ShapeDtypeStruct((rows, share * HD), jnp.bfloat16)] * n
        + [jax.ShapeDtypeStruct((2 * share, rows), jnp.float32)] * n,
        cost_estimate=pl.CostEstimate(
            flops=4 * n * share * rows * key_count * HD,
            bytes_accessed=4 * n * share * key_count * HD,
            transcendentals=n * share * rows * key_count,
        ),
        name="attend",
    )(info, queries, keys, values, cosine, sine)
    return list(zip(result[:n], result[n:]))


def merge_kernel(count, share, *refs):
    outs, stats, out_ref = refs[:count], refs[count : 2 * count], refs[2 * count]
    rows = out_ref.shape[0]
    maxima = [s[:share] for s in stats]
    totals = [s[share:] for s in stats]
    top = functools.reduce(jnp.maximum, maxima)
    factors = [jnp.exp(m - top) for m in maxima]
    total = sum(f * s for f, s in zip(factors, totals))
    scales = [f / total for f in factors]
    pad = -(count * share) % LANES
    table = jnp.concatenate(scales + [jnp.zeros((pad, rows), jnp.float32)], axis=0).T
    for head in range(share):
        at = slice(head * HD, (head + 1) * HD)
        value = sum(
            o[:, at].astype(jnp.float32) * table[:, i * share + head : i * share + head + 1]
            for i, o in enumerate(outs)
        )
        out_ref[:, at] = value.astype(jnp.bfloat16)


def merge(outs, stats, share):
    rows, width = outs[0].shape
    return pl.pallas_call(
        functools.partial(merge_kernel, len(outs), share),
        out_shape=jax.ShapeDtypeStruct((rows, width), jnp.bfloat16),
        cost_estimate=cost(4 * len(outs) * rows * width, 0, *outs, *stats),
        name="merge",
    )(*outs, *stats)


def project_kernel(chained, info, a_ref, w_ref, *refs):
    value = jnp.dot(a_ref[...], w_ref[...], preferred_element_type=jnp.float32)
    if chained:
        value = value + refs[0][...]
    refs[-1][...] = value


def project(part, weight, block, total):
    rows, depth = part.shape
    columns = weight.shape[1]
    tile = min(columns, 512)
    chained = total is not None
    spec = pl.BlockSpec((rows, tile), lambda i, info: (0, i))
    return pl.pallas_call(
        functools.partial(project_kernel, chained),
        grid_spec=pltpu.PrefetchScalarGridSpec(
            num_scalar_prefetch=1,
            grid=(columns // tile,),
            in_specs=[
                whole((rows, depth)),
                pl.BlockSpec((depth, tile), lambda i, info: (info[0], i)),
            ]
            + [spec] * chained,
            out_specs=spec,
        ),
        out_shape=jax.ShapeDtypeStruct((rows, columns), jnp.float32),
        cost_estimate=pl.CostEstimate(
            flops=2 * rows * depth * columns, bytes_accessed=2 * depth * columns, transcendentals=0
        ),
        name="project",
    )(block.astype(jnp.int32)[None], part, weight, *([total] if chained else []))


def condition_kernel(shards, own_rows, info, mine_ref, residual_ref, gain_ref, *refs):
    weights, out_ref = refs[:shards], refs[shards]
    hidden = residual_ref[...].astype(jnp.float32) + mine_ref[...]
    squares = jnp.sum(hidden * hidden, axis=1, keepdims=True)
    scaled = (hidden * gain_ref[...]).astype(jnp.bfloat16)
    width = weights[0].shape[1]
    for s, weight in enumerate(weights):
        part = jnp.dot(scaled, weight[...], preferred_element_type=jnp.float32)
        start = (info[0] ^ s) * width
        if width % LANES == 0:
            out_ref[:, pl.ds(pl.multiple_of(start, LANES), width)] = part
        else:
            out_ref[:, s * width : (s + 1) * width] = part
    out_ref[:, shards * width :] = jnp.broadcast_to(squares, (squares.shape[0], LANES))


def condition_part(mine, residual, gain, weights, own_rows, h):
    rows, depth = mine.shape
    width = weights[0].shape[1] * len(weights)
    return pl.pallas_call(
        functools.partial(condition_kernel, len(weights), own_rows),
        grid_spec=pltpu.PrefetchScalarGridSpec(
            num_scalar_prefetch=1,
            grid=(1,),
            in_specs=[
                whole((rows, depth)),
                pl.BlockSpec((rows, depth), lambda i, info: (info[0], 0)),
                whole((1, depth)),
            ]
            + [whole(w.shape) for w in weights],
            out_specs=whole((rows, width + LANES)),
        ),
        out_shape=jax.ShapeDtypeStruct((rows, width + LANES), jnp.float32),
        cost_estimate=cost(2 * rows * depth * width, 0, *weights),
        name="condition",
    )(h.astype(jnp.int32)[None], mine, residual, gain[None, :], *weights)


def sweep_kernel(
    sizes, steps, condition_ref, embed_ref, start_ref, noise_ref, in_ref, head_ref, out_ref
):
    times, rows = sizes
    start = start_ref[...]
    chan = start.shape[1]
    noise = [
        steps[times + i] * noise_ref[i * rows : (i + 1) * rows].astype(jnp.float32)
        for i in range(times - 1)
    ]

    def drift_of(first, preact):
        last = first + len(preact)
        inside = jnp.concatenate(
            [
                p + condition_ref[...] + embed_ref[i : i + 1]
                for i, p in zip(range(first, last), preact)
            ],
            axis=0,
        )
        action = (inside * jax.nn.sigmoid(inside)).astype(jnp.bfloat16)
        drift = jnp.dot(action, head_ref[...], preferred_element_type=jnp.float32)
        return [
            steps[i] * drift[(i - first) * rows : (i - first + 1) * rows] + noise[i]
            for i in range(first, last)
        ]

    opening = jnp.dot(start.astype(jnp.bfloat16), in_ref[...], preferred_element_type=jnp.float32)
    increments = drift_of(0, [opening] * (times - 1))
    for sweep in range(1, SWEEPS + 1):
        change = [jnp.zeros((rows, chan), jnp.float32)]
        for i in range(times - 1):
            change.append(change[-1] + increments[i])
        if sweep == SWEEPS or sweep >= times - 1:
            break
        states = jnp.concatenate(
            [start + change[i] for i in range(sweep, times - 1)], axis=0
        ).astype(jnp.bfloat16)
        product = jnp.dot(states, in_ref[...], preferred_element_type=jnp.float32)
        increments = increments[:sweep] + drift_of(
            sweep, [product[i * rows : (i + 1) * rows] for i in range(times - 1 - sweep)]
        )
    for i in range(times):
        out_ref[i * rows : (i + 1) * rows] = change[i].astype(jnp.bfloat16)


def sweep_all(condition, embedding, steps, start, noise, in_weight, head_out):
    rows, chan = start.shape
    times = noise.shape[0] // rows
    vmem = pl.BlockSpec(memory_space=pltpu.VMEM)
    return pl.pallas_call(
        functools.partial(sweep_kernel, (times, rows)),
        in_specs=[pl.BlockSpec(memory_space=pltpu.SMEM)] + [vmem] * 6,
        out_specs=vmem,
        out_shape=jax.ShapeDtypeStruct((times * rows, chan), jnp.bfloat16),
        cost_estimate=cost(
            12 * times * rows * chan * in_weight.shape[1], 0, in_weight, head_out
        ),
        name="sweeps",
    )(steps, condition, embedding, start, noise, in_weight, head_out)


def finish_kernel(sizes, info, start_ref, *refs):
    time_each, rows = sizes
    parts, out_ref = refs[:-1], refs[-1]
    for s, part in enumerate(parts):
        first = (info[0] ^ s) * rows
        start = start_ref[info[0] ^ s]
        for i in range(time_each):
            out_ref[pl.ds(first, rows), i, :] = start + part[i * rows : (i + 1) * rows].astype(
                jnp.float32
            )


def finish(start_state, parts, t, time_each):
    rows, chan = start_state.shape
    own_rows = rows // len(parts)
    vmem = pl.BlockSpec(memory_space=pltpu.VMEM)
    return pl.pallas_call(
        functools.partial(finish_kernel, (time_each, own_rows)),
        in_specs=[pl.BlockSpec(memory_space=pltpu.SMEM)] + [vmem] * (1 + len(parts)),
        out_specs=vmem,
        out_shape=jax.ShapeDtypeStruct((rows, time_each, chan), jnp.float32),
        name="finish",
    )(t.astype(jnp.int32)[None], start_state.reshape(len(parts), own_rows, chan), *parts)


def shards(
    queries,
    cache_keys,
    cache_values,
    residual,
    out_weight,
    norm_gain,
    cond_weight,
    in_weight,
    head_out,
    start_state,
    noise_draws,
    positions,
    cache_length,
    plan,
):
    rows, width = queries.shape
    n_heads = lax.axis_size("heads")
    n_tm = lax.axis_size("tm")
    h = lax.axis_index("heads")
    t = lax.axis_index("tm")
    local_heads = width // HD
    key_count = cache_keys.shape[0]
    model = out_weight.shape[1] * n_tm
    row_each, time_each, chan = noise_draws.shape
    own_rows = row_each // n_tm
    times = time_each * n_tm
    hidden_width = in_weight.shape[1]

    head_cuts = math.gcd(local_heads, n_tm)
    row_cuts = n_tm // head_cuts
    share = local_heads // head_cuts
    own_cut, own_row_cut = t // row_cuts, t % row_cuts

    def cut(values, index, axis):
        if row_cuts == 1:
            return values
        size = values.shape[axis] // row_cuts
        return lax.dynamic_slice_in_dim(values, index * size, size, axis)

    cosine, sine = rotation_tables(positions)
    valid_count = cache_length[0] - t * key_count
    order = list(range(head_cuts))[::-1]
    half = max(1, head_cuts // 2)
    outs, stats = [None] * n_tm, [None] * n_tm
    for groups in (order[:half], order[half:]):
        if not groups:
            continue
        blocks = attend(
            queries, cache_keys, cache_values, cosine, sine, own_cut, valid_count, groups, share
        )
        for a, (out, stat) in zip(groups, blocks):
            for b in range(row_cuts):
                s = a * row_cuts + b
                outs[s] = cut(out, own_row_cut ^ b, 0)
                stats[s] = cut(stat, own_row_cut ^ b, 1)
                if s:
                    outs[s], stats[s] = swap(outs[s], "tm", s), swap(stats[s], "tm", s)
    attended = merge(outs, stats, share)
    parts = [attended] + [swap(attended, "tm", s) for s in range(1, n_tm)]
    projected = None
    for a in range(head_cuts):
        part = parts[a * row_cuts : (a + 1) * row_cuts]
        if row_cuts > 1:
            part = jnp.take(jnp.stack(part), jnp.arange(row_cuts) ^ own_row_cut, axis=0)
            part = part.reshape(rows, share * HD)
        else:
            part = part[0]
        projected = project(part, out_weight, own_cut ^ a, projected)

    chips = n_heads // 2
    blocks = projected.reshape(chips, 2, row_each, -1).transpose(1, 0, 2, 3)
    core, chip = h % 2, h // 2
    pair = pick(blocks, core) + swap(
        pick(blocks, 1 - core).astype(jnp.bfloat16), "heads", 1
    ).astype(jnp.float32)
    mine = pick(pair, chip)
    for s in range(1, chips):
        mine = mine + swap(pick(pair, chip ^ s).astype(jnp.bfloat16), "heads", 2 * s).astype(
            jnp.float32
        )

    far = [cond_weight] + [swap(cond_weight, "heads", 2 * s) for s in range(1, chips)]
    near = [swap(w, "heads", 1) for w in far]
    cond_shards = [w for pair in zip(far, near) for w in pair]
    cond = condition_part(mine, residual, norm_gain, cond_shards, own_rows, h)
    cond_blocks = cond.reshape(n_tm, own_rows, -1)
    cond_sum = pick(cond_blocks, t) + sum(
        swap(pick(cond_blocks, t ^ s), "tm", s) for s in range(1, n_tm)
    )
    inverse = lax.rsqrt(cond_sum[:, hidden_width] / model + 1e-06)
    condition = cond_sum[:, :hidden_width]
    if cond_weight.shape[1] % LANES:
        condition = condition.reshape(own_rows, n_heads, -1)
        condition = jnp.take(condition, jnp.arange(n_heads) ^ h, axis=1)
        condition = condition.reshape(own_rows, hidden_width)
    condition = condition * inverse[:, None]

    noise_blocks = noise_draws.reshape(n_tm, own_rows, time_each, chan)
    noise = jnp.stack(
        [pick(noise_blocks, t)]
        + [swap(pick(noise_blocks, t ^ s), "tm", s) for s in range(1, n_tm)]
    )
    noise = jnp.take(noise, jnp.arange(n_tm) ^ t, axis=0)
    noise = noise.transpose(0, 2, 1, 3).reshape(times * own_rows, chan)
    levels = plan.astype(jnp.float32)
    half_width = hidden_width // 2
    frequencies = jnp.exp(
        -math.log(10000.0) * jnp.arange(half_width, dtype=jnp.float32) / half_width
    )
    angles = levels[:-1, None] * frequencies[None, :]
    embedding = jnp.concatenate([jnp.sin(angles), jnp.cos(angles)], axis=1)
    step_size = (levels[:-1] - levels[1:]) / 1000.0
    steps = jnp.concatenate([step_size, jnp.sqrt(step_size)])
    start = lax.dynamic_slice_in_dim(start_state, t * own_rows, own_rows, 0)
    change = sweep_all(condition, embedding, steps, start, noise, in_weight, head_out)
    change_blocks = change.reshape(n_tm, time_each * own_rows, chan)
    back = [pick(change_blocks, t)] + [
        swap(pick(change_blocks, t ^ s), "tm", s) for s in range(1, n_tm)
    ]
    return finish(start_state, back, t, time_each)


def solution(mesh):
    placed = (
        P("groups", "heads"),
        P(("groups", "tm"), "heads"),
        P(("groups", "tm"), "heads"),
        P("groups", "tm"),
        P("heads", "tm"),
        P("tm"),
        P("tm", "heads"),
        P(),
        P(),
        P(("groups", "heads"), None),
        P(("groups", "heads"), "tm", None),
        P("groups"),
        P("groups"),
        P(),
    )
    return jax.shard_map(
        shards,
        mesh=mesh,
        in_specs=placed,
        out_specs=P(("groups", "heads"), "tm", None),
        check_vma=False,
    )
```

time: 316 us -> 110 us (0.35)
  blocking collectives: 87.3 us -> 0 us
  waiting for transfers between devices: 101 us -> 15 us
  Pallas kernels: 0 us -> 47.4 us
  other arithmetic: 49 us -> 7.99 us
  matrix products: 28.9 us -> 0 us
  starting transfers between devices: 4.26 us -> 29.3 us
  local copies, waits for them, and re-layouts: 29.8 us -> 8.02 us
  between operations: 14.1 us -> 0.85 us
    all_gather x5 -> x0, blocking collectives: 75 us -> none  [the longest x3 46.4 us: prefix_sum(): gathered = lax.all_gather(totals[None], 'tm', axis=0, tiled=True)]
    psum x2 -> x0, waiting for transfers between devices: 54.3 us -> none  [the longest x1 33.3 us: shards(): lax.psum(jnp.dot(attended, out_weight, preferred_element_type=jnp.float32...]
    pallas_call x0 -> x10, Pallas kernels: none -> 47.4 us  [the longest x4 16.7 us: project(): pl.pallas_call(functools.partial(project_kernel, chained), grid_spec=pltp...]
    all_gather x1 -> x0, waiting for transfers between devices: 42.9 us -> none  [merged(): gathered = jax.tree.map(lambda a: lax.all_gather(a, axis), part)]
    ppermute x0 -> x23, starting transfers between devices: none -> 29.3 us  [swap(): return lax.ppermute(values, axis, [(i, i ^ distance) for i in range(size)])]
    dot_general x7 -> x0, matrix products: 28.9 us -> none  [the longest x3 12.9 us: shards(): jnp.dot(action.reshape(row_each * time_each, WIDTH), head_out, preferred_...]
    add x11 -> x3, other arithmetic: 20.8 us -> 2.65 us  [the longest x1 1.09 us: shards(): pick(blocks, core)]
    ppermute x0 -> x23, waiting for transfers between devices: none -> 15 us  [swap(): return lax.ppermute(values, axis, [(i, i ^ distance) for i in range(size)])]
  transfers between devices with their start and end apart: 4 -> 23, of which waited for: 4 -> 9; matrix products, arithmetic and copies ran while one was open for 5% -> 7% of each run, Pallas kernels for 0% -> 24%
where the time goes in v1:
time: 110 us; the launch traced here: 109 us
  Pallas kernels  47.4 us (43%)
  starting transfers between devices  29.3 us (27%)
  waiting for transfers between devices  15 us (14%)
  local copies, waits for them, and re-layouts  8.02 us (7%)
  other arithmetic  7.99 us (7%)
    ppermute x23, starting transfers between devices, swap(): return lax.ppermute(values, axis, [(i, i ^ distance) for i in range(size)])  29.3 us
    pallas_call x4, Pallas kernels, project(): pl.pallas_call(functools.partial(project_kernel, chained), grid_spec=pltp...  16.7 us
    ppermute x23, waiting for transfers between devices, swap(): return lax.ppermute(values, axis, [(i, i ^ distance) for i in range(size)])  15 us
    pallas_call x2, Pallas kernels, attend(): pl.pallas_call(functools.partial(attend_kernel, n, share, step_heads), gr...  14.4 us
    pallas_call x1, Pallas kernels, sweep_all(): pl.pallas_call(functools.partial(sweep_kernel, (times, rows)), in_specs=[...  7.57 us
    pallas_call x1, Pallas kernels, condition_part(): pl.pallas_call(functools.partial(condition_kernel, len(weights), own_rows...  4.72 us
    unnamed x32, local copies, waits for them, and re-layouts  2.65 us
    squeeze x2, local copies, waits for them, and re-layouts, pick(): return lax.dynamic_index_in_dim(values, index, 0, False)  2.31 us
  transfers between devices with their start and end apart: 23, of which 9 were waited for; matrix products, arithmetic and copies ran while one was open for 7% of the time, Pallas kernels for 24%

profile of v1, /device:TPU:0, one launch (start us, length us, event | category | flops | bytes accessed | tf_op | source)
XLA Modules:
  0.0 108.6 jit_solution(11166933186405701257)
XLA Ops:
  2.9 7.3 %attend.3 = (bf16[128,512]{1,0:T(8,128)(2,1)}, bf16[128,512]{1,0:T(8,128)(2,1)}, f32[8,128]{1,0:T(8,128)}, f32[8,128]{1,0:T(8,128)}) custom-call(s32[2]{0:T(128)} %pad_add_fusion.info, bf16[128,2048]{1,0:T(8,128)(2,1)} %q_ref.3, bf16[1024,2048]{1,0:T(8,128)(2,1)} %k_ref.3, bf16[1024,2048]{1,0:T(8,128)(2,1)} %v_ref.3, f32[128,128]{1,0:T(8,128)} %get-tuple-element.37.cos_ref, ...), custom_call_target="tpu_custom_call" | custom-call | flops 536870912 | bytes 4194304 | tf_op jit(solution)/shard_map/attend/pallas_call | solution.py:100
  10.2 4.0 %collective-permute-start.1 = (bf16[128,512]{1,0:T(8,128)(2,1)}, bf16[128,512]{1,0:T(8,128)(2,1)S(1)}, u32[]{:S(2)}, u32[]{:S(2)}) collective-permute-start(bf16[128,512]{1,0:T(8,128)(2,1)} %get-tuple-element.15), channel_id=1, source_target_pairs={{0,2},{1,3},{2,0},{3,1},{4,6},{5,7},{6,4},{7,5},{8,10},{9,11},{10,... | collective-permute-start | bytes 393224 | tf_op jit(solution)/shard_map/ppermute | solution.py:18
  15.6 1.7 %collective-permute-start.4 = (f32[8,128]{1,0:T(8,128)}, f32[8,128]{1,0:T(8,128)S(1)}, u32[]{:S(2)}, u32[]{:S(2)}) collective-permute-start(f32[8,128]{1,0:T(8,128)} %get-tuple-element.19), channel_id=1, source_target_pairs={{0,2},{1,3},{2,0},{3,1},{4,6},{5,7},{6,4},{7,5},{8,10},{9,11},{10,... | collective-permute-start | bytes 12296 | tf_op jit(solution)/shard_map/ppermute | solution.py:18
  18.2 1.5 %collective-permute-start.12 = (bf16[2048,384]{1,0:T(8,128)(2,1)S(1)}, bf16[2048,384]{1,0:T(8,128)(2,1)}, u32[]{:S(2)}, u32[]{:S(2)}) collective-permute-start(bf16[2048,384]{1,0:T(8,128)(2,1)S(1)} %copy-done), channel_id=1, source_target_pairs={{0,8},{4,12},{8,0},{12,4},{1,9},{5,13},{9,1},{13,5},{2,10},{6,14},... | collective-permute-start | bytes 4718600 | tf_op jit(solution)/shard_map/ppermute | solution.py:18
  20.0 1.4 %constant_dynamic-slice_fusion.start_ref = f32[8,1152]{1,0:T(8,128)} fusion(f32[32,1152]{1,0:T(8,128)} %param.23, s32[]{:T(128)S(6)} %select_n.116), kind=kLoop, calls=%fused_computation.29 | loop fusion | bytes 73732 | tf_op jit(solution)/shard_map/dynamic_slice | solution.py:429
  21.4 7.1 %attend.2 = (bf16[128,512]{1,0:T(8,128)(2,1)}, bf16[128,512]{1,0:T(8,128)(2,1)}, f32[8,128]{1,0:T(8,128)}, f32[8,128]{1,0:T(8,128)}) custom-call(s32[2]{0:T(128)} %pad_add_fusion.info, bf16[128,2048]{1,0:T(8,128)(2,1)} %q_ref.3, bf16[1024,2048]{1,0:T(8,128)(2,1)} %k_ref.3, bf16[1024,2048]{1,0:T(8,128)(2,1)} %v_ref.3, f32[128,128]{1,0:T(8,128)} %get-tuple-element.37.cos_ref, ...), custom_call_target="tpu_custom_call" | custom-call | flops 536870912 | bytes 4194304 | tf_op jit(solution)/shard_map/attend/pallas_call | solution.py:100
  30.7 3.1 %collective-permute-done.3.refs_5_ = f32[8,128]{1,0:T(8,128)S(1)} collective-permute-done((f32[8,128]{1,0:T(8,128)}, f32[8,128]{1,0:T(8,128)S(1)}, u32[]{:S(2)}, u32[]{:S(2)}) %collective-permute-start.3) | collective-permute-done | bytes 4128 | tf_op jit(solution)/shard_map/ppermute | solution.py:18
  34.5 2.3 %merge.1.a_ref = bf16[128,512]{1,0:T(8,128)(2,1)} custom-call(bf16[128,512]{1,0:T(8,128)(2,1)} %get-tuple-element.13.refs_0_, bf16[128,512]{1,0:T(8,128)(2,1)} %copy-done.7, bf16[128,512]{1,0:T(8,128)(2,1)} %copy-done.5, bf16[128,512]{1,0:T(8,128)(2,1)} %copy-done.6, f32[8,128]{1,0:T(8,128)} %get-tuple-element.17.refs_4_, f32[8,128]{1,0:T(8,128)} %copy-done.13, ...), custom_call_target="tpu_custom_call" | custom-call | flops 1048576 | bytes 540672 | tf_op jit(solution)/shard_map/merge/pallas_call | solution.py:149
  37.7 2.6 %collective-permute-start.7 = (bf16[128,512]{1,0:T(8,128)(2,1)}, bf16[128,512]{1,0:T(8,128)(2,1)S(1)}, u32[]{:S(2)}, u32[]{:S(2)}) collective-permute-start(bf16[128,512]{1,0:T(8,128)(2,1)} %merge.1.a_ref), channel_id=1, source_target_pairs={{0,2},{1,3},{2,0},{3,1},{4,6},{5,7},{6,4},{7,5},{8,10},{9,11},{10,... | collective-permute-start | bytes 393224 | tf_op jit(solution)/shard_map/ppermute | solution.py:18
  41.2 4.1 %project.4.refs_0_ = f32[128,2048]{1,0:T(8,128)} custom-call(s32[1]{0:T(128)} %bitcast.info, bf16[128,512]{1,0:T(8,128)(2,1)} %merge.1.a_ref, bf16[2048,2048]{1,0:T(8,128)(2,1)} %w_ref.7), custom_call_target="tpu_custom_call" | custom-call | flops 268435456 | bytes 2097152 | tf_op jit(solution)/shard_map/project/pallas_call | solution.py:170
  46.1 4.2 %project.5.refs_0_ = f32[128,2048]{1,0:T(8,128)} custom-call(s32[1]{0:T(128)} %bitcast.7.info, bf16[128,512]{1,0:T(8,128)(2,1)} %copy-done.4, bf16[2048,2048]{1,0:T(8,128)(2,1)} %w_ref.7, f32[128,2048]{1,0:T(8,128)} %project.4.refs_0_), custom_call_target="tpu_custom_call" | custom-call | flops 268435456 | bytes 2097152 | tf_op jit(solution)/shard_map/project/pallas_call | solution.py:170
  50.9 2.2 %collective-permute-start.18 = (bf16[8,2,1152]{2,0,1:T(8,128)(2,1)S(1)}, bf16[8,2,1152]{2,0,1:T(8,128)(2,1)S(1)}, u32[]{:S(2)}, u32[]{:S(2)}) collective-permute-start(bf16[8,2,1152]{2,0,1:T(8,128)(2,1)S(1)} %get-tuple-element.32), channel_id=1, source_target_pairs={{0,2},{1,3},{2,0},{3,1},{4,6},{5,7},{6,4},{7,5},{8,10},{9,11},{10,... | collective-permute-start | bytes 110600 | tf_op jit(solution)/shard_map/ppermute | solution.py:18
  53.0 4.2 %project.6.refs_0_ = f32[128,2048]{1,0:T(8,128)} custom-call(s32[1]{0:T(128)} %bitcast.6.info, bf16[128,512]{1,0:T(8,128)(2,1)} %copy-done.3, bf16[2048,2048]{1,0:T(8,128)(2,1)} %w_ref.7, f32[128,2048]{1,0:T(8,128)} %project.5.refs_0_), custom_call_target="tpu_custom_call" | custom-call | flops 268435456 | bytes 2097152 | tf_op jit(solution)/shard_map/project/pallas_call | solution.py:170
  58.0 4.2 %project.7 = f32[128,2048]{1,0:T(8,128)} custom-call(s32[1]{0:T(128)} %bitcast.3.info, bf16[128,512]{1,0:T(8,128)(2,1)} %copy-done.2, bf16[2048,2048]{1,0:T(8,128)(2,1)} %w_ref.7, f32[128,2048]{1,0:T(8,128)} %project.6.refs_0_), custom_call_target="tpu_custom_call" | custom-call | flops 268435456 | bytes 2097152 | tf_op jit(solution)/shard_map/project/pallas_call | solution.py:170
  67.9 2.9 %collective-permute-done.19 = bf16[8,2,1152]{2,0,1:T(8,128)(2,1)S(1)} collective-permute-done((bf16[8,2,1152]{2,0,1:T(8,128)(2,1)S(1)}, bf16[8,2,1152]{2,0,1:T(8,128)(2,1)S(1)}, u32[]{:S(2)}, u32[]{:S(2)}) %collective-permute-start.19) | collective-permute-done | bytes 36896 | tf_op jit(solution)/shard_map/ppermute | solution.py:18
  73.3 4.7 %condition.1 = f32[32,1664]{1,0:T(8,128)} custom-call(s32[1]{0:T(128)} %bitcast.2.info, f32[32,2048]{1,0:T(8,128)} %bitcast_add_fusion.1.mine_ref, bf16[128,2048]{1,0:T(8,128)(2,1)} %residual_ref.1, f32[1,2048]{1,0:T(1,128)} %bitcast.71, bf16[2048,384]{1,0:T(8,128)(2,1)} %refs_0_.1, bf16[2048,384]{1,0:T(8,128)(2,1)} %collective-permute-done.11.refs_1_, ...), custom_call_target="tpu_custom_call" | custom-call | flops 201326592 | bytes 6291456 | tf_op jit(solution)/shard_map/condition/pallas_call | solution.py:209
  79.1 3.0 %collective-permute-start.15 = (f32[8,1664]{1,0:T(8,128)S(1)}, f32[8,1664]{1,0:T(8,128)S(1)}, u32[]{:S(2)}, u32[]{:S(2)}) collective-permute-start(f32[8,1664]{1,0:T(8,128)S(1)} %get-tuple-element.23), channel_id=1, source_target_pairs={{0,2},{1,3},{2,0},{3,1},{4,6},{5,7},{6,4},{7,5},{8,10},{9,11},{10,... | collective-permute-start | bytes 159752 | tf_op jit(solution)/shard_map/ppermute | solution.py:18
  84.3 3.8 %collective-permute-done.16 = f32[8,1664]{1,0:T(8,128)S(1)} collective-permute-done((f32[8,1664]{1,0:T(8,128)S(1)}, f32[8,1664]{1,0:T(8,128)S(1)}, u32[]{:S(2)}, u32[]{:S(2)}) %collective-permute-start.16) | collective-permute-done | bytes 53280 | tf_op jit(solution)/shard_map/ppermute | solution.py:18
  89.8 7.6 %sweeps.1 = bf16[64,1152]{1,0:T(8,128)(2,1)} custom-call(f32[16]{0:T(128)} %pad_maximum_fusion.2.steps, f32[8,1536]{1,0:T(8,128)} %slice_multiply_fusion.condition_ref, f32[8,1536]{1,0:T(8,128)} %pad_maximum_fusion.1.embed_ref, f32[8,1152]{1,0:T(8,128)} %constant_dynamic-slice_fusion.start_ref, bf16[64,1152]{1,0:T(8,128)(2,1)} %bitcast.65, ...), custom_call_target="tpu_custom_call" | custom-call | flops 1358954496 | bytes 7077888 | tf_op jit(solution)/shard_map/sweeps/pallas_call | solution.py:278
  97.3 1.4 %dynamic-slice_bitcast_fusion.3 = (bf16[16,1152]{1,0:T(8,128)(2,1)S(1)}, bf16[16,1152]{1,0:T(8,128)(2,1)S(1)}, bf16[16,1152]{1,0:T(8,128)(2,1)S(1)}, bf16[16,1152]{1,0:T(8,128)(2,1)}) fusion(bf16[4,16,1152]{2,1,0:T(8,128)(2,1)} %bitcast.66, s32[]{:T(128)S(6)} %select_n.115, s32[]{:T(128)S(6)} %select_n.114, s32[]{:T(128)S(6)} %select_n.113, s32[]{:T(128)S(6)} %select_n.112), kind=kLoop, calls=%fused_computation.19 | loop fusion | bytes 294928 | tf_op jit(solution)/shard_map/jit(dynamic_index_in_dim)/squeeze | solution.py:22
  98.8 1.7 %collective-permute-start.21 = (bf16[16,1152]{1,0:T(8,128)(2,1)S(1)}, bf16[16,1152]{1,0:T(8,128)(2,1)S(1)}, u32[]{:S(2)}, u32[]{:S(2)}) collective-permute-start(bf16[16,1152]{1,0:T(8,128)(2,1)S(1)} %get-tuple-element.27), channel_id=1, source_target_pairs={{0,2},{1,3},{2,0},{3,1},{4,6},{5,7},{6,4},{7,5},{8,10},{9,11},{10,... | collective-permute-start | bytes 110600 | tf_op jit(solution)/shard_map/ppermute | solution.py:18
  100.5 2.7 %collective-permute-start.22 = (bf16[16,1152]{1,0:T(8,128)(2,1)S(1)}, bf16[16,1152]{1,0:T(8,128)(2,1)S(1)}, u32[]{:S(2)}, u32[]{:S(2)}) collective-permute-start(bf16[16,1152]{1,0:T(8,128)(2,1)S(1)} %get-tuple-element.26), channel_id=1, source_target_pairs={{0,3},{1,2},{2,1},{3,0},{4,7},{5,6},{6,5},{7,4},{8,11},{9,10},{10,... | collective-permute-start | bytes 110600 | tf_op jit(solution)/shard_map/ppermute | solution.py:18
  103.6 2.6 %collective-permute-done.22.refs_3_ = bf16[16,1152]{1,0:T(8,128)(2,1)S(1)} collective-permute-done((bf16[16,1152]{1,0:T(8,128)(2,1)S(1)}, bf16[16,1152]{1,0:T(8,128)(2,1)S(1)}, u32[]{:S(2)}, u32[]{:S(2)}) %collective-permute-start.22) | collective-permute-done | bytes 36896 | tf_op jit(solution)/shard_map/ppermute | solution.py:18
  106.9 1.8 %finish.1 = f32[32,2,1152]{2,1,0:T(2,128)} custom-call(s32[1]{0:T(128)} %bitcast.info, f32[4,8,1152]{2,1,0:T(8,128)} %bitcast.67, bf16[16,1152]{1,0:T(8,128)(2,1)} %get-tuple-element.29.refs_0_, bf16[16,1152]{1,0:T(8,128)(2,1)} %copy-done.8, bf16[16,1152]{1,0:T(8,128)(2,1)} %copy-done.9, bf16[16,1152]{1,0:T(8,128)(2,1)} %copy-done.10), custom_call_target="tpu_custom_call" | custom-call | tf_op jit(solution)/shard_map/finish/pallas_call | solution.py:306
  (90 shorter events, 25.7 us)
Async XLA Ops:
  2.9 16.8 %copy-start.14 = (s32[9]{0:T(128)S(1)}, s32[9]{0:T(128)}, u32[]{:S(2)}) copy-start(s32[9]{0:T(128)} %param.27) | copy-start | bytes 112
  10.2 23.6 %collective-permute-start.1 = (bf16[128,512]{1,0:T(8,128)(2,1)}, bf16[128,512]{1,0:T(8,128)(2,1)S(1)}, u32[]{:S(2)}, u32[]{:S(2)}) collective-permute-start(bf16[128,512]{1,0:T(8,128)(2,1)} %get-tuple-element.15), channel_id=1, source_target_pairs={{0,2},{1,3},{2,0},{3,1},{4,6},{5,7},{6,4},{7,5},{8,10},{9,11},{10,... | collective-permute-start | bytes 393224 | tf_op jit(solution)/shard_map/ppermute | solution.py:18
  14.2 19.6 %collective-permute-start.2 = (bf16[128,512]{1,0:T(8,128)(2,1)}, bf16[128,512]{1,0:T(8,128)(2,1)S(1)}, u32[]{:S(2)}, u32[]{:S(2)}) collective-permute-start(bf16[128,512]{1,0:T(8,128)(2,1)} %get-tuple-element.16), channel_id=1, source_target_pairs={{0,3},{1,2},{2,1},{3,0},{4,7},{5,6},{6,5},{7,4},{8,11},{9,10},{10,... | collective-permute-start | bytes 393224 | tf_op jit(solution)/shard_map/ppermute | solution.py:18
  15.6 12.9 %collective-permute-start.4 = (f32[8,128]{1,0:T(8,128)}, f32[8,128]{1,0:T(8,128)S(1)}, u32[]{:S(2)}, u32[]{:S(2)}) collective-permute-start(f32[8,128]{1,0:T(8,128)} %get-tuple-element.19), channel_id=1, source_target_pairs={{0,2},{1,3},{2,0},{3,1},{4,6},{5,7},{6,4},{7,5},{8,10},{9,11},{10,... | collective-permute-start | bytes 12296 | tf_op jit(solution)/shard_map/ppermute | solution.py:18
  17.3 12.2 %collective-permute-start.5 = (f32[8,128]{1,0:T(8,128)}, f32[8,128]{1,0:T(8,128)S(1)}, u32[]{:S(2)}, u32[]{:S(2)}) collective-permute-start(f32[8,128]{1,0:T(8,128)} %get-tuple-element.20), channel_id=1, source_target_pairs={{0,3},{1,2},{2,1},{3,0},{4,7},{5,6},{6,5},{7,4},{8,11},{9,10},{10,... | collective-permute-start | bytes 12296 | tf_op jit(solution)/shard_map/ppermute | solution.py:18
  18.2 45.8 %collective-permute-start.12 = (bf16[2048,384]{1,0:T(8,128)(2,1)S(1)}, bf16[2048,384]{1,0:T(8,128)(2,1)}, u32[]{:S(2)}, u32[]{:S(2)}) collective-permute-start(bf16[2048,384]{1,0:T(8,128)(2,1)S(1)} %copy-done), channel_id=1, source_target_pairs={{0,8},{4,12},{8,0},{12,4},{1,9},{5,13},{9,1},{13,5},{2,10},{6,14},... | collective-permute-start | bytes 4718600 | tf_op jit(solution)/shard_map/ppermute | solution.py:18
  28.5 5.3 %collective-permute-start = (bf16[128,512]{1,0:T(8,128)(2,1)}, bf16[128,512]{1,0:T(8,128)(2,1)S(1)}, u32[]{:S(2)}, u32[]{:S(2)}) collective-permute-start(bf16[128,512]{1,0:T(8,128)(2,1)} %get-tuple-element.14), channel_id=1, source_target_pairs={{0,1},{1,0},{2,3},{3,2},{4,5},{5,4},{6,7},{7,6},{8,9},{9,8},{10,11... | collective-permute-start | bytes 393224 | tf_op jit(solution)/shard_map/ppermute | solution.py:18
  29.5 4.3 %collective-permute-start.3 = (f32[8,128]{1,0:T(8,128)}, f32[8,128]{1,0:T(8,128)S(1)}, u32[]{:S(2)}, u32[]{:S(2)}) collective-permute-start(f32[8,128]{1,0:T(8,128)} %get-tuple-element.18), channel_id=1, source_target_pairs={{0,1},{1,0},{2,3},{3,2},{4,5},{5,4},{6,7},{7,6},{8,9},{9,8},{10,11... | collective-permute-start | bytes 12296 | tf_op jit(solution)/shard_map/ppermute | solution.py:18
  33.8 39.5 %collective-permute-start.11 = (bf16[2048,384]{1,0:T(8,128)(2,1)S(1)}, bf16[2048,384]{1,0:T(8,128)(2,1)}, u32[]{:S(2)}, u32[]{:S(2)}) collective-permute-start(bf16[2048,384]{1,0:T(8,128)(2,1)S(1)} %copy-done), channel_id=1, source_target_pairs={{0,4},{4,0},{8,12},{12,8},{1,5},{5,1},{9,13},{13,9},{2,6},{6,2},{1... | collective-permute-start | bytes 4718600 | tf_op jit(solution)/shard_map/ppermute | solution.py:18
  36.8 8.6 %collective-permute-start.8 = (bf16[128,512]{1,0:T(8,128)(2,1)}, bf16[128,512]{1,0:T(8,128)(2,1)S(1)}, u32[]{:S(2)}, u32[]{:S(2)}) collective-permute-start(bf16[128,512]{1,0:T(8,128)(2,1)} %merge.1.a_ref), channel_id=1, source_target_pairs={{0,1},{1,0},{2,3},{3,2},{4,5},{5,4},{6,7},{7,6},{8,9},{9,8},{10,11... | collective-permute-start | bytes 393224 | tf_op jit(solution)/shard_map/ppermute | solution.py:18
  37.7 13.2 %collective-permute-start.7 = (bf16[128,512]{1,0:T(8,128)(2,1)}, bf16[128,512]{1,0:T(8,128)(2,1)S(1)}, u32[]{:S(2)}, u32[]{:S(2)}) collective-permute-start(bf16[128,512]{1,0:T(8,128)(2,1)} %merge.1.a_ref), channel_id=1, source_target_pairs={{0,2},{1,3},{2,0},{3,1},{4,6},{5,7},{6,4},{7,5},{8,10},{9,11},{10,... | collective-permute-start | bytes 393224 | tf_op jit(solution)/shard_map/ppermute | solution.py:18
  40.3 17.0 %collective-permute-start.6 = (bf16[128,512]{1,0:T(8,128)(2,1)}, bf16[128,512]{1,0:T(8,128)(2,1)S(1)}, u32[]{:S(2)}, u32[]{:S(2)}) collective-permute-start(bf16[128,512]{1,0:T(8,128)(2,1)} %merge.1.a_ref), channel_id=1, source_target_pairs={{0,3},{1,2},{2,1},{3,0},{4,7},{5,6},{6,5},{7,4},{8,11},{9,10},{10,... | collective-permute-start | bytes 393224 | tf_op jit(solution)/shard_map/ppermute | solution.py:18
  45.4 21.9 %collective-permute-start.17 = (bf16[8,2,1152]{2,0,1:T(8,128)(2,1)S(1)}, bf16[8,2,1152]{2,0,1:T(8,128)(2,1)S(1)}, u32[]{:S(2)}, u32[]{:S(2)}) collective-permute-start(bf16[8,2,1152]{2,0,1:T(8,128)(2,1)S(1)} %get-tuple-element.33), channel_id=1, source_target_pairs={{0,1},{1,0},{2,3},{3,2},{4,5},{5,4},{6,7},{7,6},{8,9},{9,8},{10,11... | collective-permute-start | bytes 110600 | tf_op jit(solution)/shard_map/ppermute | solution.py:18
  50.9 17.1 %collective-permute-start.18 = (bf16[8,2,1152]{2,0,1:T(8,128)(2,1)S(1)}, bf16[8,2,1152]{2,0,1:T(8,128)(2,1)S(1)}, u32[]{:S(2)}, u32[]{:S(2)}) collective-permute-start(bf16[8,2,1152]{2,0,1:T(8,128)(2,1)S(1)} %get-tuple-element.32), channel_id=1, source_target_pairs={{0,2},{1,3},{2,0},{3,1},{4,6},{5,7},{6,4},{7,5},{8,10},{9,11},{10,... | collective-permute-start | bytes 110600 | tf_op jit(solution)/shard_map/ppermute | solution.py:18
  63.2 1.8 %collective-permute-start.9 = (bf16[2,32,2048]{2,1,0:T(8,128)(2,1)S(1)}, bf16[2,32,2048]{2,1,0:T(8,128)(2,1)S(1)}, u32[]{:S(2)}, u32[]{:S(2)}) collective-permute-start(bf16[2,32,2048]{2,1,0:T(8,128)(2,1)S(1)} %fusion), channel_id=1, source_target_pairs={{0,4},{4,0},{8,12},{12,8},{1,5},{5,1},{9,13},{13,9},{2,6},{6,2},{1... | collective-permute-start | bytes 786440 | tf_op jit(solution)/shard_map/ppermute | solution.py:18
  63.9 9.3 %collective-permute-start.13 = (bf16[2048,384]{1,0:T(8,128)(2,1)}, bf16[2048,384]{1,0:T(8,128)(2,1)}, u32[]{:S(2)}, u32[]{:S(2)}) collective-permute-start(bf16[2048,384]{1,0:T(8,128)(2,1)} %collective-permute-done.12.refs_2_), channel_id=1, source_target_pairs={{0,4},{4,0},{8,12},{12,8},{1,5},{5,1},{9,13},{13,9},{2,6},{6,2},{1... | collective-permute-start | bytes 4718600 | tf_op jit(solution)/shard_map/ppermute | solution.py:18
  65.1 5.8 %collective-permute-start.19 = (bf16[8,2,1152]{2,0,1:T(8,128)(2,1)S(1)}, bf16[8,2,1152]{2,0,1:T(8,128)(2,1)S(1)}, u32[]{:S(2)}, u32[]{:S(2)}) collective-permute-start(bf16[8,2,1152]{2,0,1:T(8,128)(2,1)S(1)} %get-tuple-element.31), channel_id=1, source_target_pairs={{0,3},{1,2},{2,1},{3,0},{4,7},{5,6},{6,5},{7,4},{8,11},{9,10},{10,... | collective-permute-start | bytes 110600 | tf_op jit(solution)/shard_map/ppermute | solution.py:18
  67.3 5.2 %collective-permute-start.10 = (bf16[32,2048]{1,0:T(8,128)(2,1)S(1)}, bf16[32,2048]{1,0:T(8,128)(2,1)S(1)}, u32[]{:S(2)}, u32[]{:S(2)}) collective-permute-start(bf16[32,2048]{1,0:T(8,128)(2,1)S(1)} %fusion.1), channel_id=1, source_target_pairs={{0,8},{4,12},{8,0},{12,4},{1,9},{5,13},{9,1},{13,5},{2,10},{6,14},... | collective-permute-start | bytes 393224 | tf_op jit(solution)/shard_map/ppermute | solution.py:18
  78.9 5.2 %collective-permute-start.14 = (f32[8,1664]{1,0:T(8,128)S(1)}, f32[8,1664]{1,0:T(8,128)S(1)}, u32[]{:S(2)}, u32[]{:S(2)}) collective-permute-start(f32[8,1664]{1,0:T(8,128)S(1)} %get-tuple-element.25), channel_id=1, source_target_pairs={{0,1},{1,0},{2,3},{3,2},{4,5},{5,4},{6,7},{7,6},{8,9},{9,8},{10,11... | collective-permute-start | bytes 159752 | tf_op jit(solution)/shard_map/ppermute | solution.py:18
  79.1 5.2 %collective-permute-start.15 = (f32[8,1664]{1,0:T(8,128)S(1)}, f32[8,1664]{1,0:T(8,128)S(1)}, u32[]{:S(2)}, u32[]{:S(2)}) collective-permute-start(f32[8,1664]{1,0:T(8,128)S(1)} %get-tuple-element.23), channel_id=1, source_target_pairs={{0,2},{1,3},{2,0},{3,1},{4,6},{5,7},{6,4},{7,5},{8,10},{9,11},{10,... | collective-permute-start | bytes 159752 | tf_op jit(solution)/shard_map/ppermute | solution.py:18
  82.2 5.9 %collective-permute-start.16 = (f32[8,1664]{1,0:T(8,128)S(1)}, f32[8,1664]{1,0:T(8,128)S(1)}, u32[]{:S(2)}, u32[]{:S(2)}) collective-permute-start(f32[8,1664]{1,0:T(8,128)S(1)} %get-tuple-element.24), channel_id=1, source_target_pairs={{0,3},{1,2},{2,1},{3,0},{4,7},{5,6},{6,5},{7,4},{8,11},{9,10},{10,... | collective-permute-start | bytes 159752 | tf_op jit(solution)/shard_map/ppermute | solution.py:18
  98.8 4.4 %collective-permute-start.20 = (bf16[16,1152]{1,0:T(8,128)(2,1)S(1)}, bf16[16,1152]{1,0:T(8,128)(2,1)S(1)}, u32[]{:S(2)}, u32[]{:S(2)}) collective-permute-start(bf16[16,1152]{1,0:T(8,128)(2,1)S(1)} %get-tuple-element.28), channel_id=1, source_target_pairs={{0,1},{1,0},{2,3},{3,2},{4,5},{5,4},{6,7},{7,6},{8,9},{9,8},{10,11... | collective-permute-start | bytes 110600 | tf_op jit(solution)/shard_map/ppermute | solution.py:18
  98.8 4.9 %collective-permute-start.21 = (bf16[16,1152]{1,0:T(8,128)(2,1)S(1)}, bf16[16,1152]{1,0:T(8,128)(2,1)S(1)}, u32[]{:S(2)}, u32[]{:S(2)}) collective-permute-start(bf16[16,1152]{1,0:T(8,128)(2,1)S(1)} %get-tuple-element.27), channel_id=1, source_target_pairs={{0,2},{1,3},{2,0},{3,1},{4,6},{5,7},{6,4},{7,5},{8,10},{9,11},{10,... | collective-permute-start | bytes 110600 | tf_op jit(solution)/shard_map/ppermute | solution.py:18
  100.5 5.8 %collective-permute-start.22 = (bf16[16,1152]{1,0:T(8,128)(2,1)S(1)}, bf16[16,1152]{1,0:T(8,128)(2,1)S(1)}, u32[]{:S(2)}, u32[]{:S(2)}) collective-permute-start(bf16[16,1152]{1,0:T(8,128)(2,1)S(1)} %get-tuple-element.26), channel_id=1, source_target_pairs={{0,3},{1,2},{2,1},{3,0},{4,7},{5,6},{6,5},{7,4},{8,11},{9,10},{10,... | collective-permute-start | bytes 110600 | tf_op jit(solution)/shard_map/ppermute | solution.py:18
  (14 other events, 54.2 us)

commit v2 on v1

v2 whole, which is shorter than its diff:
```python
import functools
import math

import jax
import jax.numpy as jnp
import numpy as np
from jax import lax
from jax.experimental import pallas as pl
from jax.experimental.pallas import tpu as pltpu
from jax.sharding import PartitionSpec as P

HD = 128
SWEEPS = 3
LANES = 128


def swap(values, axis, distance):
    size = lax.axis_size(axis)
    return lax.ppermute(values, axis, [(i, i ^ distance) for i in range(size)])


def pick(values, index):
    return lax.dynamic_index_in_dim(values, index, 0, False)


def cost(flops, transcendentals, *arrays):
    moved = sum(math.prod(a.shape) * jnp.dtype(a.dtype).itemsize for a in arrays)
    return pl.CostEstimate(flops=flops, bytes_accessed=moved, transcendentals=transcendentals)


def mib(count):
    return pltpu.CompilerParams(vmem_limit_bytes=count * 1024 * 1024)


VMEM = pl.BlockSpec(memory_space=pltpu.VMEM)
SMEM = pl.BlockSpec(memory_space=pltpu.SMEM)
HBM = pl.BlockSpec(memory_space=pltpu.HBM)
PIECES = 3


def pieces_of(value):
    high = value.astype(jnp.bfloat16)
    rest = value - high.astype(jnp.float32)
    middle = rest.astype(jnp.bfloat16)
    return high, middle, (rest - middle.astype(jnp.float32)).astype(jnp.bfloat16)


def sum_pieces(pieces):
    high, middle, low = (p.astype(jnp.float32) for p in pieces)
    return high + (middle + low)


def packed(rows, width, share):
    return PIECES * rows <= width and 2 * share <= 8 and rows % LANES == 0


def attend_kernel(
    groups, share, per_copy, row_cuts, length_ref, freq_ref, pos_ref, q_ref, k_hbm, v_hbm, *refs
):
    count = len(groups)
    outs, stats = refs[:count], refs[count:-6]
    k_buf, v_buf, k_sem, v_sem, cos_ref, sin_ref = refs[-6:]
    rows = q_ref.shape[0]
    keys = k_hbm.shape[0]
    t = lax.axis_index("tm")
    own = t // row_cuts
    width = per_copy * HD
    copies = []
    for g, a in enumerate(groups):
        for part in range(share // per_copy):
            slot = len(copies)
            column = pl.multiple_of(((own ^ a) * share + part * per_copy) * HD, HD)
            pair = [
                pltpu.make_async_copy(hbm.at[:, pl.ds(column, width)], buf.at[slot], sem.at[slot])
                for hbm, buf, sem in ((k_hbm, k_buf, k_sem), (v_hbm, v_buf, v_sem))
            ]
            for copy in pair:
                copy.start()
            copies.append((g, part, column, pair))

    even = lax.broadcasted_iota(jnp.int32, (rows, HD), 1) % 2 == 0
    place = jnp.broadcast_to(pos_ref[...].astype(jnp.float32), (HD, rows)).T
    angles = place * freq_ref[...]
    cos_ref[...] = jnp.cos(angles)
    sine = jnp.sin(angles)
    sin_ref[...] = jnp.where(even, -sine, sine)
    lane = lax.broadcasted_iota(jnp.int32, (rows, LANES), 1)
    valid = lax.broadcasted_iota(jnp.int32, (1, keys), 1) < length_ref[0] - t * keys
    scale = 1.0 / math.sqrt(HD)
    held = jnp.zeros((rows, LANES), jnp.float32)
    for slot, (g, part, column, pair) in enumerate(copies):
        for copy in pair:
            copy.wait()
        for i in range(per_copy):
            head = part * per_copy + i
            at = slice(i * HD, (i + 1) * HD)
            to = slice(head * HD, (head + 1) * HD)
            from_column = pl.multiple_of(column + i * HD, HD)
            wide = q_ref[:, pl.ds(from_column, HD)].astype(jnp.float32)
            partner = jnp.where(even, pltpu.roll(wide, HD - 1, 1), pltpu.roll(wide, 1, 1))
            rotated = (wide * cos_ref[...] + partner * sin_ref[...]).astype(jnp.bfloat16)
            scores = lax.dot_general(
                rotated,
                k_buf[slot, :, at],
                (((1,), (1,)), ((), ())),
                preferred_element_type=jnp.float32,
            )
            scores = jnp.where(valid, scores, jnp.float32(-1e30))
            block_max = jnp.maximum(jnp.max(scores, axis=1, keepdims=True), -1e29)
            weights = jnp.exp((scores - block_max) * scale)
            block_total = jnp.sum(weights, axis=1, keepdims=True)
            block_out = jnp.dot(
                weights.astype(jnp.bfloat16),
                v_buf[slot, :, at],
                preferred_element_type=jnp.float32,
            )
            outs[g][:rows, to] = block_out.astype(jnp.bfloat16)
            held = jnp.where(lane == head, block_max * scale, held)
            held = jnp.where(lane == share + head, block_total, held)
        if part == share // per_copy - 1:
            flat = held.T
            if stats:
                stats[g][...] = flat[: 2 * share]
            else:
                extra = outs[g].shape[0] - rows
                for p, piece in enumerate(pieces_of(flat[:extra])):
                    outs[g][rows:, p * rows : (p + 1) * rows] = piece


def attend(queries, keys, values, positions, cache_length, groups, share, row_cuts):
    rows = queries.shape[0]
    key_count = keys.shape[0]
    per_copy = 2 if share % 2 == 0 else 1
    n = len(groups)
    slots = n * share // per_copy
    wide = share * HD
    joined = row_cuts == 1 and packed(rows, wide, share)
    frequencies = np.exp(-math.log(10000.0) * 2.0 * (np.arange(HD) // 2) / HD)
    buffer = pltpu.VMEM((slots, key_count, per_copy * HD), jnp.bfloat16)
    out_shape = [jax.ShapeDtypeStruct((rows + 8 * joined, wide), jnp.bfloat16)] * n
    if not joined:
        out_shape = out_shape + [jax.ShapeDtypeStruct((2 * share, rows), jnp.float32)] * n
    result = pl.pallas_call(
        functools.partial(attend_kernel, groups, share, per_copy, row_cuts),
        in_specs=[SMEM, VMEM, VMEM, VMEM, HBM, HBM],
        out_specs=[VMEM] * len(out_shape),
        out_shape=out_shape,
        scratch_shapes=[
            buffer,
            buffer,
            pltpu.SemaphoreType.DMA((slots,)),
            pltpu.SemaphoreType.DMA((slots,)),
            pltpu.VMEM((rows, HD), jnp.float32),
            pltpu.VMEM((rows, HD), jnp.float32),
        ],
        cost_estimate=pl.CostEstimate(
            flops=4 * n * share * rows * key_count * HD,
            bytes_accessed=4 * n * share * key_count * HD,
            transcendentals=n * share * rows * key_count,
        ),
        compiler_params=mib(60),
        name="attend",
    )(cache_length, frequencies.astype(np.float32)[None], positions[None], queries, keys, values)
    return list(zip(result[:n], result[n:] if not joined else [None] * n))


def merge_kernel(count, share, *refs):
    out_ref = refs[-1]
    rows = out_ref.shape[0]
    outs, stats = refs[:count], refs[count:-1]
    if stats:
        tables = [s[...] for s in stats]
    else:
        tables = [
            sum_pieces([o[rows:, p * rows : (p + 1) * rows] for p in range(PIECES)]) for o in outs
        ]
    maxima = [s[:share] for s in tables]
    totals = [s[share : 2 * share] for s in tables]
    top = functools.reduce(jnp.maximum, maxima)
    factors = [jnp.exp(m - top) for m in maxima]
    total = sum(f * s for f, s in zip(factors, totals))
    scales = [f / total for f in factors]
    pad = -(count * share) % LANES
    table = jnp.concatenate(scales + [jnp.zeros((pad, rows), jnp.float32)], axis=0).T
    for head in range(share):
        at = slice(head * HD, (head + 1) * HD)
        value = sum(
            o[:rows, at].astype(jnp.float32) * table[:, i * share + head : i * share + head + 1]
            for i, o in enumerate(outs)
        )
        out_ref[:, at] = value.astype(jnp.bfloat16)


def merge(outs, stats, share, rows):
    width = outs[0].shape[1]
    stats = [s for s in stats if s is not None]
    return pl.pallas_call(
        functools.partial(merge_kernel, len(outs), share),
        in_specs=[VMEM] * (len(outs) + len(stats)),
        out_specs=VMEM,
        out_shape=jax.ShapeDtypeStruct((rows, width), jnp.bfloat16),
        cost_estimate=cost(4 * len(outs) * rows * width, 0, *outs, *stats),
        compiler_params=mib(4),
        name="merge",
    )(*outs, *stats)


def project_kernel(head_cuts, row_cuts, cuts, chained, last, *refs):
    parts, refs = refs[: len(cuts)], refs[len(cuts) :]
    w_ref, refs = refs[0], refs[1:]
    own = lax.axis_index("tm") // row_cuts
    depth = parts[0].shape[1]
    value = refs[0][...] if chained else None
    for a, part in zip(cuts, parts):
        first = pl.multiple_of((own ^ a) * depth, depth)
        product = jnp.dot(part[...], w_ref[pl.ds(first, depth), :], preferred_element_type=jnp.float32)
        value = product if value is None else value + product
    if not last:
        refs[-1][...] = value
        return
    keep_ref, send_ref, whole_ref = refs[chained:]
    chips, rows = keep_ref.shape[:2]
    core = lax.axis_index("heads") % 2
    for chip in range(chips):
        for c in range(2):
            first = (2 * chip + c) * rows
            whole_ref[c, chip] = value[first : first + rows]
    keep_ref[...] = whole_ref[core]
    send_ref[...] = whole_ref[1 - core].astype(jnp.bfloat16)


def project(parts, cuts, weight, total, row_cuts, chips):
    rows, depth = parts[0].shape
    columns = weight.shape[1]
    chained = total is not None
    last = chips > 0
    if last:
        block = (chips, rows // (2 * chips), columns)
        out_shape = [
            jax.ShapeDtypeStruct(block, jnp.float32),
            jax.ShapeDtypeStruct(block, jnp.bfloat16),
        ]
        scratch = [pltpu.VMEM((2, *block), jnp.float32)]
    else:
        out_shape, scratch = jax.ShapeDtypeStruct((rows, columns), jnp.float32), []
    return pl.pallas_call(
        functools.partial(project_kernel, None, row_cuts, cuts, chained, last),
        in_specs=[VMEM] * (len(parts) + 1 + chained),
        out_specs=[VMEM, VMEM] if last else VMEM,
        out_shape=out_shape,
        scratch_shapes=scratch,
        cost_estimate=pl.CostEstimate(
            flops=2 * len(parts) * rows * depth * columns,
            bytes_accessed=2 * len(parts) * depth * columns,
            transcendentals=0,
        ),
        compiler_params=mib(20),
        name="project",
    )(*parts, weight, *([total] if chained else []))


def pair_kernel(keep_ref, got_ref, mine_ref, *send_refs):
    chip = lax.axis_index("heads") // 2
    mine_ref[...] = keep_ref[chip] + got_ref[chip].astype(jnp.float32)
    for s, send_ref in enumerate(send_refs, 1):
        send_ref[...] = (keep_ref[chip ^ s] + got_ref[chip ^ s].astype(jnp.float32)).astype(
            jnp.bfloat16
        )


def pair_sum(keep, got):
    chips, rows, columns = keep.shape
    result = pl.pallas_call(
        pair_kernel,
        in_specs=[VMEM] * 2,
        out_specs=[VMEM] * chips,
        out_shape=[jax.ShapeDtypeStruct((rows, columns), jnp.float32)]
        + [jax.ShapeDtypeStruct((rows, columns), jnp.bfloat16)] * (chips - 1),
        cost_estimate=cost(chips * rows * columns, 0, keep, got),
        compiler_params=mib(8),
        name="pair",
    )(keep, got)
    return result[0], result[1:]


def condition_kernel(chips, shards, own_rows, mine_ref, residual_ref, gain_ref, *refs):
    got, refs = refs[: chips - 1], refs[chips - 1 :]
    weights, refs = refs[:shards], refs[shards:]
    rows = mine_ref.shape[0]
    h = lax.axis_index("heads")
    hidden = residual_ref[h].astype(jnp.float32) + mine_ref[...]
    for ref in got:
        hidden = hidden + ref[...].astype(jnp.float32)
    squares = jnp.sum(hidden * hidden, axis=1, keepdims=True)
    scaled = (hidden * gain_ref[...]).astype(jnp.bfloat16)
    width = weights[0].shape[1]
    products = [jnp.dot(scaled, w[...], preferred_element_type=jnp.float32) for w in weights]
    tail = jnp.zeros((rows, LANES), jnp.float32)
    lane = lax.broadcasted_iota(jnp.int32, (rows, LANES), 1)
    for p, piece in enumerate(pieces_of(squares)):
        tail = jnp.where(lane == p, piece.astype(jnp.float32), tail)
    if own_rows % 8 == 0 and width % LANES == 0:
        outs, held = refs[:-1], refs[-1]
        t = lax.axis_index("tm")
        for s, product in enumerate(products):
            held[:, pl.ds(pl.multiple_of((h ^ s) * width, LANES), width)] = product
        held[:, shards * width :] = tail
        for s, out_ref in enumerate(outs):
            first = pl.multiple_of((t ^ s) * own_rows, own_rows)
            out_ref[...] = held[pl.ds(first, own_rows), :].astype(jnp.bfloat16)
    else:
        for s, product in enumerate(products):
            refs[0][:, s * width : (s + 1) * width] = product.astype(jnp.bfloat16)
        refs[0][:, shards * width :] = tail.astype(jnp.bfloat16)


def condition_parts(mine, got, residual, gain, weights, n_tm, h, t):
    rows, depth = mine.shape
    shards = len(weights)
    width = weights[0].shape[1]
    full = shards * width + LANES
    own_rows = rows // n_tm
    aligned = own_rows % 8 == 0 and width % LANES == 0
    block = jax.ShapeDtypeStruct((own_rows, full), jnp.bfloat16)
    out_shape = [block] * n_tm if aligned else [jax.ShapeDtypeStruct((rows, full), jnp.bfloat16)]
    result = pl.pallas_call(
        functools.partial(condition_kernel, len(got) + 1, shards, own_rows),
        in_specs=[VMEM] * (3 + len(got) + shards),
        out_specs=[VMEM] * len(out_shape),
        out_shape=out_shape,
        scratch_shapes=[pltpu.VMEM((rows, full), jnp.float32)] * aligned,
        cost_estimate=cost(2 * rows * depth * full, 0, *weights),
        compiler_params=mib(12),
        name="condition",
    )(mine, residual.reshape(-1, rows, depth), gain[None, :], *got, *weights)
    if aligned:
        return result
    columns = result[0][:, :-LANES].reshape(rows, shards, width)
    columns = jnp.take(columns, jnp.arange(shards) ^ h, axis=1).reshape(rows, shards * width)
    result = jnp.concatenate([columns, result[0][:, -LANES:]], axis=1)
    result = result.reshape(n_tm, own_rows, full)
    return [pick(result, t ^ s) for s in range(n_tm)]


def sweep_kernel(sizes, steps, start_ref, embed_ref, in_ref, head_ref, *refs):
    n_tm, time_each, rows, model = sizes
    noise_refs, refs = refs[:n_tm], refs[n_tm:]
    parts, refs = refs[:n_tm], refs[n_tm:]
    outs, held = refs[:n_tm], refs[n_tm]
    t = lax.axis_index("tm")
    times = n_tm * time_each
    start = start_ref[t]
    chan = start.shape[1]
    for s, ref in enumerate(noise_refs):
        held[t ^ s] = ref[...].astype(jnp.float32)

    def block(i):
        at = (i % time_each) * rows
        return i // time_each, slice(at, at + rows)

    noise = [steps[times + i] * held[block(i)] for i in range(times - 1)]
    width = in_ref.shape[1]
    opening = jnp.dot(start.astype(jnp.bfloat16), in_ref[...], preferred_element_type=jnp.float32)
    total = sum(p[...].astype(jnp.float32) for p in parts)
    squares = total[:, width : width + 1]
    for p in range(1, PIECES):
        squares = squares + total[:, width + p : width + p + 1]
    condition = total[:, :width] * lax.rsqrt(squares / model + 1e-06)

    def increments_at(first, products):
        last = first + len(products)
        inside = jnp.concatenate(
            [p + (condition + embed_ref[i : i + 1]) for i, p in enumerate(products, first)], axis=0
        )
        action = (inside * jax.nn.sigmoid(inside)).astype(jnp.bfloat16)
        drift = jnp.dot(action, head_ref[...], preferred_element_type=jnp.float32)
        return [
            steps[i] * drift[(i - first) * rows : (i - first + 1) * rows] + noise[i]
            for i in range(first, last)
        ]

    increments = increments_at(0, [opening] * (times - 1))
    for sweep in range(1, SWEEPS + 1):
        change = [jnp.zeros((rows, chan), jnp.float32)]
        for i in range(times - 1):
            change.append(change[-1] + increments[i])
        if sweep == SWEEPS or sweep >= times - 1:
            break
        states = jnp.concatenate([start + change[i] for i in range(sweep, times - 1)], axis=0)
        product = jnp.dot(
            states.astype(jnp.bfloat16), in_ref[...], preferred_element_type=jnp.float32
        )
        increments = increments[:sweep] + increments_at(
            sweep, [product[i * rows : (i + 1) * rows] for i in range(times - 1 - sweep)]
        )
    for i in range(times):
        held[block(i)] = change[i]
    for s, out_ref in enumerate(outs):
        out_ref[...] = held[t ^ s].astype(jnp.bfloat16)


def sweep_all(parts, noise, embedding, steps, start, in_weight, head_out, time_each, model):
    n_tm, rows, chan = start.shape
    block = (time_each * rows, chan)
    return pl.pallas_call(
        functools.partial(sweep_kernel, (n_tm, time_each, rows, model)),
        in_specs=[SMEM] + [VMEM] * (4 + 2 * n_tm),
        out_specs=[VMEM] * n_tm,
        out_shape=[jax.ShapeDtypeStruct(block, jnp.bfloat16)] * n_tm,
        scratch_shapes=[pltpu.VMEM((n_tm, *block), jnp.float32)],
        cost_estimate=cost(
            10 * n_tm * time_each * rows * chan * in_weight.shape[1], 0, in_weight, head_out
        ),
        compiler_params=mib(16),
        name="sweeps",
    )(steps, start, embedding, in_weight, head_out, *noise, *parts)


def finish_kernel(sizes, start_ref, *refs):
    time_each, rows = sizes
    parts, out_ref = refs[:-1], refs[-1]
    t = lax.axis_index("tm")
    for s, part in enumerate(parts):
        start = start_ref[t ^ s]
        for i in range(time_each):
            out_ref[pl.ds((t ^ s) * rows, rows), i, :] = start + part[
                i * rows : (i + 1) * rows
            ].astype(jnp.float32)


def finish(start, parts, time_each):
    n_tm, rows, chan = start.shape
    return pl.pallas_call(
        functools.partial(finish_kernel, (time_each, rows)),
        in_specs=[VMEM] * (1 + len(parts)),
        out_specs=VMEM,
        out_shape=jax.ShapeDtypeStruct((n_tm * rows, time_each, chan), jnp.float32),
        cost_estimate=cost(n_tm * rows * time_each * chan, 0, start, *parts),
        compiler_params=mib(4),
        name="finish",
    )(start, *parts)


def shards(
    queries,
    cache_keys,
    cache_values,
    residual,
    out_weight,
    norm_gain,
    cond_weight,
    in_weight,
    head_out,
    start_state,
    noise_draws,
    positions,
    cache_length,
    plan,
):
    rows, width = queries.shape
    n_heads = lax.axis_size("heads")
    n_tm = lax.axis_size("tm")
    h = lax.axis_index("heads")
    t = lax.axis_index("tm")
    local_heads = width // HD
    model = out_weight.shape[1] * n_tm
    row_each, time_each, chan = noise_draws.shape
    own_rows = row_each // n_tm
    hidden_width = in_weight.shape[1]

    head_cuts = math.gcd(local_heads, n_tm)
    row_cuts = n_tm // head_cuts
    share = local_heads // head_cuts
    own_cut, own_row_cut = t // row_cuts, t % row_cuts

    def cut(values, index, axis):
        if row_cuts == 1:
            return values
        size = values.shape[axis] // row_cuts
        return lax.dynamic_slice_in_dim(values, index * size, size, axis)

    order = list(range(head_cuts))[::-1]
    half = max(1, head_cuts // 2)
    outs, stats = [None] * n_tm, [None] * n_tm
    for groups in (order[:half], order[half:]):
        if not groups:
            continue
        blocks = attend(
            queries, cache_keys, cache_values, positions, cache_length, groups, share, row_cuts
        )
        for a, (out, stat) in zip(groups, blocks):
            for b in range(row_cuts):
                s = a * row_cuts + b
                outs[s] = cut(out, own_row_cut ^ b, 0)
                stats[s] = None if stat is None else cut(stat, own_row_cut ^ b, 1)
                if s:
                    outs[s] = swap(outs[s], "tm", s)
                    stats[s] = None if stat is None else swap(stats[s], "tm", s)
    attended = merge(outs, stats, share, rows // row_cuts)
    chips = n_heads // 2

    far = [cond_weight] + [swap(cond_weight, "heads", 2 * s) for s in range(1, chips)]
    far, attended = lax.optimization_barrier((far, attended))
    near = [swap(w, "heads", 1) for w in far]
    cond_shards = [w for pair in zip(far, near) for w in pair]

    parts = [attended] + [swap(attended, "tm", s) for s in range(1, n_tm)]
    projected = None
    for a in range(head_cuts):
        part = parts[a * row_cuts : (a + 1) * row_cuts]
        if row_cuts > 1:
            part = jnp.take(jnp.stack(part), jnp.arange(row_cuts) ^ own_row_cut, axis=0)
            part = part.reshape(rows, share * HD)
        else:
            part = part[0]
        projected = project(
            [part], [a], out_weight, projected, row_cuts, chips if a == head_cuts - 1 else 0
        )

    keep, send = projected
    mine, far_rows = pair_sum(keep, swap(send, "heads", 1))
    got = [swap(r, "heads", 2 * s) for s, r in enumerate(far_rows, 1)]

    cond = condition_parts(mine, got, residual, norm_gain, cond_shards, n_tm, h, t)
    cond = [cond[0]] + [swap(cond[s], "tm", s) for s in range(1, n_tm)]

    noise_rows = noise_draws.transpose(1, 0, 2).reshape(time_each, n_tm, own_rows, chan)
    noise = [
        lax.dynamic_index_in_dim(noise_rows, t ^ s, 1, False).reshape(time_each * own_rows, chan)
        for s in range(n_tm)
    ]
    noise = [noise[0]] + [swap(noise[s], "tm", s) for s in range(1, n_tm)]
    levels = plan.astype(jnp.float32)
    half_width = hidden_width // 2
    frequencies = jnp.exp(
        -math.log(10000.0) * jnp.arange(half_width, dtype=jnp.float32) / half_width
    )
    angles = levels[:-1, None] * frequencies[None, :]
    embedding = jnp.concatenate([jnp.sin(angles), jnp.cos(angles)], axis=1)
    step_size = (levels[:-1] - levels[1:]) / 1000.0
    steps = jnp.concatenate([step_size, jnp.sqrt(step_size)])
    start = start_state.reshape(n_tm, own_rows, chan)
    change = sweep_all(
        cond, noise, embedding, steps, start, in_weight, head_out, time_each, model
    )
    back = [change[0]] + [swap(change[s], "tm", s) for s in range(1, n_tm)]
    return finish(start, back, time_each)


def solution(mesh):
    placed = (
        P("groups", "heads"),
        P(("groups", "tm"), "heads"),
        P(("groups", "tm"), "heads"),
        P("groups", "tm"),
        P("heads", "tm"),
        P("tm"),
        P("tm", "heads"),
        P(),
        P(),
        P(("groups", "heads"), None),
        P(("groups", "heads"), "tm", None),
        P("groups"),
        P("groups"),
        P(),
    )
    return jax.shard_map(
        shards,
        mesh=mesh,
        in_specs=placed,
        out_specs=P(("groups", "heads"), "tm", None),
        check_vma=False,
    )
```

time: 110 us -> 88.7 us (0.81); the launches traced: 109 us -> 88.4 us
  Pallas kernels: 47.4 us -> 24.1 us
  waiting for transfers between devices: 15 us -> 31.1 us
  other arithmetic: 7.99 us -> 0.34 us
  starting transfers between devices: 29.3 us -> 26.4 us
  local copies, waits for them, and re-layouts: 8.02 us -> 5.52 us
    pallas_call x10 -> x11, Pallas kernels: 47.4 us -> 24.1 us  [the longest x2 13.5 us: attend(): pl.pallas_call(functools.partial(attend_kernel, groups, share, per_copy,...]
    ppermute x23 -> x20, waiting for transfers between devices: 15 us -> 31.1 us  [swap(): return lax.ppermute(values, axis, [(i, i ^ distance) for i in range(size)])]
    ppermute x23 -> x20, starting transfers between devices: 29.3 us -> 26.4 us  [swap(): return lax.ppermute(values, axis, [(i, i ^ distance) for i in range(size)])]
    unnamed x32 -> x26, local copies, waits for them, and re-layouts: 2.65 us -> 5.41 us
    add x3 -> x0, other arithmetic: 2.65 us -> none  [the longest x1 1.09 us: shards(): pick(blocks, core)]
    squeeze x2 -> x0, local copies, waits for them, and re-layouts: 2.31 us -> none  [pick(): return lax.dynamic_index_in_dim(values, index, 0, False)]
    mul x2 -> x0, other arithmetic: 1.67 us -> none  [the longest x1 0.96 us: rotation_tables(): return (jnp.cos(angles), jnp.sin(angles) * sign[None, :])]
    dynamic_slice x1, local copies, waits for them, and re-layouts: 1.39 us -> 0.11 us  [shards(): lax.dynamic_index_in_dim(noise_rows, t ^ s, 1, False)]
  transfers between devices with their start and end apart: 23 -> 20, of which waited for: 9 -> 9; matrix products, arithmetic and copies ran while one was open for 7% -> 1% of each run, Pallas kernels for 24% -> 22%
where the time goes in v2:
time: 88.7 us; the launch traced here: 88.4 us
  waiting for transfers between devices  31.1 us (35%)
  starting transfers between devices  26.4 us (30%)
  Pallas kernels  24.1 us (27%)
  local copies, waits for them, and re-layouts  5.52 us (6%)
  between operations  0.92 us (1%)
    ppermute x20, waiting for transfers between devices, swap(): return lax.ppermute(values, axis, [(i, i ^ distance) for i in range(size)])  31.1 us
    ppermute x20, starting transfers between devices, swap(): return lax.ppermute(values, axis, [(i, i ^ distance) for i in range(size)])  26.4 us
    pallas_call x2, Pallas kernels, attend(): pl.pallas_call(functools.partial(attend_kernel, groups, share, per_copy,...  13.5 us
    unnamed x26, local copies, waits for them, and re-layouts  5.41 us
    pallas_call x1, Pallas kernels, sweep_all(): pl.pallas_call(functools.partial(sweep_kernel, (n_tm, time_each, rows, mo...  4.27 us
    pallas_call x1, Pallas kernels, condition_parts(): pl.pallas_call(functools.partial(condition_kernel, len(got) + 1, shards,...  3.07 us
    pallas_call x4, Pallas kernels, project(): pl.pallas_call(functools.partial(project_kernel, None, row_cuts, cuts, ch...  1.91 us
  transfers between devices with their start and end apart: 20, of which 9 were waited for; matrix products, arithmetic and copies ran while one was open for 1% of the time, Pallas kernels for 22%

profile of v2, /device:TPU:0, one launch (start us, length us, event | category | flops | bytes accessed | tf_op | source)
XLA Modules:
  0.0 88.4 jit_solution(15014180566674822316)
XLA Ops:
  0.0 3.0 %collective-permute-start.3 = (bf16[2048,384]{1,0:T(8,128)(2,1)}, bf16[2048,384]{1,0:T(8,128)(2,1)S(1)}, u32[]{:S(2)}, u32[]{:S(2)}) collective-permute-start(bf16[2048,384]{1,0:T(8,128)(2,1)} %refs_1_.8), channel_id=1, source_target_pairs={{0,8},{4,12},{8,0},{12,4},{1,9},{5,13},{9,1},{13,5},{2,10},{6,14},... | collective-permute-start | bytes 4718600 | tf_op jit(solution)/shard_map/ppermute | solution.py:19
  3.6 6.7 %attend.2 = (bf16[136,512]{1,0:T(8,128)(2,1)}, bf16[136,512]{1,0:T(8,128)(2,1)}) custom-call(s32[1]{0:T(128)S(6)} %copy.33.length_ref, f32[1,128]{1,0:T(1,128)} %constant.32.clone.freq_ref, s32[1,128]{1,0:T(1,128)} %bitcast.28, bf16[128,2048]{1,0:T(8,128)(2,1)} %q_ref.3, bf16[1024,2048]{1,0:T(8,128)(2,1)} %k_hbm.3, bf16[1024,2048]{1,0:T(8,128)(2,1)} %v_hbm.3), custom_call_target="tpu_custom_call" | custom-call | flops 536870912 | bytes 4194304 | tf_op jit(solution)/shard_map/attend/pallas_call | solution.py:143
  10.4 1.7 %collective-permute-start.4 = (bf16[136,512]{1,0:T(8,128)(2,1)}, bf16[136,512]{1,0:T(8,128)(2,1)S(1)}, u32[]{:S(2)}, u32[]{:S(2)}) collective-permute-start(bf16[136,512]{1,0:T(8,128)(2,1)} %get-tuple-element.25), channel_id=1, source_target_pairs={{0,1},{1,0},{2,3},{3,2},{4,5},{5,4},{6,7},{7,6},{8,9},{9,8},{10,11... | collective-permute-start | bytes 417800 | tf_op jit(solution)/shard_map/ppermute | solution.py:19
  12.1 6.8 %attend.3 = (bf16[136,512]{1,0:T(8,128)(2,1)}, bf16[136,512]{1,0:T(8,128)(2,1)}) custom-call(s32[1]{0:T(128)S(6)} %copy.33.length_ref, f32[1,128]{1,0:T(1,128)} %constant.32.clone.freq_ref, s32[1,128]{1,0:T(1,128)} %bitcast.29, bf16[128,2048]{1,0:T(8,128)(2,1)} %q_ref.3, bf16[1024,2048]{1,0:T(8,128)(2,1)} %k_hbm.3, bf16[1024,2048]{1,0:T(8,128)(2,1)} %v_hbm.3), custom_call_target="tpu_custom_call" | custom-call | flops 536870912 | bytes 4194304 | tf_op jit(solution)/shard_map/attend/pallas_call | solution.py:143
  18.8 2.6 %collective-permute-start.5 = (bf16[136,512]{1,0:T(8,128)(2,1)}, bf16[136,512]{1,0:T(8,128)(2,1)S(1)}, u32[]{:S(2)}, u32[]{:S(2)}) collective-permute-start(bf16[136,512]{1,0:T(8,128)(2,1)} %get-tuple-element.26), channel_id=1, source_target_pairs={{0,2},{1,3},{2,0},{3,1},{4,6},{5,7},{6,4},{7,5},{8,10},{9,11},{10,... | collective-permute-start | bytes 417800 | tf_op jit(solution)/shard_map/ppermute | solution.py:19
  21.7 9.2 %collective-permute-done.5.refs_2_ = bf16[136,512]{1,0:T(8,128)(2,1)S(1)} collective-permute-done((bf16[136,512]{1,0:T(8,128)(2,1)}, bf16[136,512]{1,0:T(8,128)(2,1)S(1)}, u32[]{:S(2)}, u32[]{:S(2)}) %collective-permute-start.5) | collective-permute-done | bytes 139296 | tf_op jit(solution)/shard_map/ppermute | solution.py:19
  31.5 6.1 %collective-permute-done.3.refs_3_ = bf16[2048,384]{1,0:T(8,128)(2,1)S(1)} collective-permute-done((bf16[2048,384]{1,0:T(8,128)(2,1)}, bf16[2048,384]{1,0:T(8,128)(2,1)S(1)}, u32[]{:S(2)}, u32[]{:S(2)}) %collective-permute-start.3) | collective-permute-done | bytes 1572896 | tf_op jit(solution)/shard_map/ppermute | solution.py:19
  38.2 1.9 %collective-permute-start.9 = (bf16[128,512]{1,0:T(8,128)(2,1)S(1)}, bf16[128,512]{1,0:T(8,128)(2,1)S(1)}, u32[]{:S(2)}, u32[]{:S(2)}) collective-permute-start(bf16[128,512]{1,0:T(8,128)(2,1)S(1)} %merge.1.refs_0_), channel_id=1, source_target_pairs={{0,1},{1,0},{2,3},{3,2},{4,5},{5,4},{6,7},{7,6},{8,9},{9,8},{10,11... | collective-permute-start | bytes 393224 | tf_op jit(solution)/shard_map/ppermute | solution.py:19
  40.1 2.6 %collective-permute-start.8 = (bf16[128,512]{1,0:T(8,128)(2,1)S(1)}, bf16[128,512]{1,0:T(8,128)(2,1)S(1)}, u32[]{:S(2)}, u32[]{:S(2)}) collective-permute-start(bf16[128,512]{1,0:T(8,128)(2,1)S(1)} %merge.1.refs_0_), channel_id=1, source_target_pairs={{0,2},{1,3},{2,0},{3,1},{4,6},{5,7},{6,4},{7,5},{8,10},{9,11},{10,... | collective-permute-start | bytes 393224 | tf_op jit(solution)/shard_map/ppermute | solution.py:19
  42.8 3.4 %copy-done = bf16[2048,2048]{1,0:T(8,128)(2,1)S(1)} copy-done((bf16[2048,2048]{1,0:T(8,128)(2,1)S(1)}, bf16[2048,2048]{1,0:T(8,128)(2,1)}, u32[]{:S(2)}) %copy-start) | copy-done | bytes 8388632
  47.6 2.0 %copy-done.1 = bf16[2048,2048]{1,0:T(8,128)(2,1)S(1)} copy-done((bf16[2048,2048]{1,0:T(8,128)(2,1)S(1)}, bf16[2048,2048]{1,0:T(8,128)(2,1)}, u32[]{:S(2)}) %copy-start.1) | copy-done | bytes 8388632
  50.0 3.0 %collective-permute-done.8.refs_0_ = bf16[128,512]{1,0:T(8,128)(2,1)S(1)} collective-permute-done((bf16[128,512]{1,0:T(8,128)(2,1)S(1)}, bf16[128,512]{1,0:T(8,128)(2,1)S(1)}, u32[]{:S(2)}, u32[]{:S(2)}) %collective-permute-start.8) | collective-permute-done | bytes 131104 | tf_op jit(solution)/shard_map/ppermute | solution.py:19
  54.3 1.3 %collective-permute-done.10.got_ref = bf16[2,32,2048]{2,1,0:T(8,128)(2,1)S(1)} collective-permute-done((bf16[2,32,2048]{2,1,0:T(8,128)(2,1)S(1)}, bf16[2,32,2048]{2,1,0:T(8,128)(2,1)S(1)}, u32[]{:S(2)}, u32[]{:S(2)}) %collective-permute-start.10) | collective-permute-done | bytes 262176 | tf_op jit(solution)/shard_map/ppermute | solution.py:19
  55.7 1.6 %collective-permute-start.11 = (bf16[32,2048]{1,0:T(8,128)(2,1)S(1)}, bf16[32,2048]{1,0:T(8,128)(2,1)S(1)}, u32[]{:S(2)}, u32[]{:S(2)}) collective-permute-start(bf16[32,2048]{1,0:T(8,128)(2,1)S(1)} %get-tuple-element.32), channel_id=1, source_target_pairs={{0,8},{4,12},{8,0},{12,4},{1,9},{5,13},{9,1},{13,5},{2,10},{6,14},... | collective-permute-start | bytes 393224 | tf_op jit(solution)/shard_map/ppermute | solution.py:19
  57.3 4.0 %collective-permute-done.11.refs_0_ = bf16[32,2048]{1,0:T(8,128)(2,1)S(1)} collective-permute-done((bf16[32,2048]{1,0:T(8,128)(2,1)S(1)}, bf16[32,2048]{1,0:T(8,128)(2,1)S(1)}, u32[]{:S(2)}, u32[]{:S(2)}) %collective-permute-start.11) | collective-permute-done | bytes 131104 | tf_op jit(solution)/shard_map/ppermute | solution.py:19
  61.3 2.4 %collective-permute-start.2 = (bf16[16,1152]{1,0:T(8,128)(2,1)S(1)}, bf16[16,1152]{1,0:T(8,128)(2,1)S(1)}, u32[]{:S(2)}, u32[]{:S(2)}) collective-permute-start(bf16[16,1152]{1,0:T(8,128)(2,1)S(1)} %bitcast.27), channel_id=1, source_target_pairs={{0,3},{1,2},{2,1},{3,0},{4,7},{5,6},{6,5},{7,4},{8,11},{9,10},{10,... | collective-permute-start | bytes 110600 | tf_op jit(solution)/shard_map/ppermute | solution.py:19
  63.8 3.1 %condition.1 = (bf16[8,1664]{1,0:T(8,128)(2,1)S(1)}, bf16[8,1664]{1,0:T(8,128)(2,1)S(1)}, bf16[8,1664]{1,0:T(8,128)(2,1)S(1)}, bf16[8,1664]{1,0:T(8,128)(2,1)S(1)}) custom-call(f32[32,2048]{1,0:T(8,128)S(1)} %get-tuple-element.31.mine_ref, bf16[4,32,2048]{2,1,0:T(8,128)(2,1)S(1)} %bitcast.21, f32[1,2048]{1,0:T(1,128)S(1)} %bitcast.23, ...), custom_call_target="tpu_custom_call" | custom-call | flops 218103808 | bytes 6291456 | tf_op jit(solution)/shard_map/condition/pallas_call | solution.py:326
  66.8 1.8 %collective-permute-start.14 = (bf16[8,1664]{1,0:T(8,128)(2,1)S(1)}, bf16[8,1664]{1,0:T(8,128)(2,1)S(1)}, u32[]{:S(2)}, u32[]{:S(2)}) collective-permute-start(bf16[8,1664]{1,0:T(8,128)(2,1)S(1)} %get-tuple-element.36), channel_id=1, source_target_pairs={{0,1},{1,0},{2,3},{3,2},{4,5},{5,4},{6,7},{7,6},{8,9},{9,8},{10,11... | collective-permute-start | bytes 79880 | tf_op jit(solution)/shard_map/ppermute | solution.py:19
  69.0 2.3 %collective-permute-start.16 = (bf16[8,1664]{1,0:T(8,128)(2,1)S(1)}, bf16[8,1664]{1,0:T(8,128)(2,1)S(1)}, u32[]{:S(2)}, u32[]{:S(2)}) collective-permute-start(bf16[8,1664]{1,0:T(8,128)(2,1)S(1)} %get-tuple-element.38), channel_id=1, source_target_pairs={{0,3},{1,2},{2,1},{3,0},{4,7},{5,6},{6,5},{7,4},{8,11},{9,10},{10,... | collective-permute-start | bytes 79880 | tf_op jit(solution)/shard_map/ppermute | solution.py:19
  71.4 2.0 %collective-permute-done.15.refs_6_ = bf16[8,1664]{1,0:T(8,128)(2,1)S(1)} collective-permute-done((bf16[8,1664]{1,0:T(8,128)(2,1)S(1)}, bf16[8,1664]{1,0:T(8,128)(2,1)S(1)}, u32[]{:S(2)}, u32[]{:S(2)}) %collective-permute-start.15) | collective-permute-done | bytes 26656 | tf_op jit(solution)/shard_map/ppermute | solution.py:19
  74.7 4.3 %sweeps.1 = (bf16[16,1152]{1,0:T(8,128)(2,1)S(1)}, bf16[16,1152]{1,0:T(8,128)(2,1)S(1)}, bf16[16,1152]{1,0:T(8,128)(2,1)S(1)}, bf16[16,1152]{1,0:T(8,128)(2,1)S(1)}) custom-call(f32[16]{0:T(128)S(1)} %pad_maximum_fusion.1.steps, f32[4,8,1152]{2,1,0:T(8,128)S(1)} %bitcast.19, f32[8,1536]{1,0:T(8,128)S(1)} %pad_maximum_fusion.embed_ref, ...), custom_call_target="tpu_custom_call" | custom-call | flops 1132462080 | bytes 7077888 | tf_op jit(solution)/shard_map/sweeps/pallas_call | solution.py:405
  79.2 2.7 %collective-permute-start.18 = (bf16[16,1152]{1,0:T(8,128)(2,1)S(1)}, bf16[16,1152]{1,0:T(8,128)(2,1)S(1)}, u32[]{:S(2)}, u32[]{:S(2)}) collective-permute-start(bf16[16,1152]{1,0:T(8,128)(2,1)S(1)} %get-tuple-element.41), channel_id=1, source_target_pairs={{0,2},{1,3},{2,0},{3,1},{4,6},{5,7},{6,4},{7,5},{8,10},{9,11},{10,... | collective-permute-start | bytes 110600 | tf_op jit(solution)/shard_map/ppermute | solution.py:19
  81.9 1.5 %collective-permute-start.19 = (bf16[16,1152]{1,0:T(8,128)(2,1)S(1)}, bf16[16,1152]{1,0:T(8,128)(2,1)S(1)}, u32[]{:S(2)}, u32[]{:S(2)}) collective-permute-start(bf16[16,1152]{1,0:T(8,128)(2,1)S(1)} %get-tuple-element.42), channel_id=1, source_target_pairs={{0,3},{1,2},{2,1},{3,0},{4,7},{5,6},{6,5},{7,4},{8,11},{9,10},{10,... | collective-permute-start | bytes 110600 | tf_op jit(solution)/shard_map/ppermute | solution.py:19
  84.1 3.6 %collective-permute-done.19.refs_3_ = bf16[16,1152]{1,0:T(8,128)(2,1)S(1)} collective-permute-done((bf16[16,1152]{1,0:T(8,128)(2,1)S(1)}, bf16[16,1152]{1,0:T(8,128)(2,1)S(1)}, u32[]{:S(2)}, u32[]{:S(2)}) %collective-permute-start.19) | collective-permute-done | bytes 36896 | tf_op jit(solution)/shard_map/ppermute | solution.py:19
  (60 shorter events, 8.2 us)
Async XLA Ops:
  0.0 37.6 %collective-permute-start.3 = (bf16[2048,384]{1,0:T(8,128)(2,1)}, bf16[2048,384]{1,0:T(8,128)(2,1)S(1)}, u32[]{:S(2)}, u32[]{:S(2)}) collective-permute-start(bf16[2048,384]{1,0:T(8,128)(2,1)} %refs_1_.8), channel_id=1, source_target_pairs={{0,8},{4,12},{8,0},{12,4},{1,9},{5,13},{9,1},{13,5},{2,10},{6,14},... | collective-permute-start | bytes 4718600 | tf_op jit(solution)/shard_map/ppermute | solution.py:19
  10.4 20.6 %copy-start.7 = (bf16[136,512]{1,0:T(8,128)(2,1)S(1)}, bf16[136,512]{1,0:T(8,128)(2,1)}, u32[]{:S(2)}) copy-start(bf16[136,512]{1,0:T(8,128)(2,1)} %get-tuple-element.24.refs_0_) | copy-start | bytes 417796
  10.4 27.2 %copy-start.4 = (bf16[2048,384]{1,0:T(8,128)(2,1)S(1)}, bf16[2048,384]{1,0:T(8,128)(2,1)}, u32[]{:S(2)}) copy-start(bf16[2048,384]{1,0:T(8,128)(2,1)} %refs_1_.8) | copy-start | bytes 4718596
  10.4 27.7 %copy-start.10 = (s32[9]{0:T(128)S(1)}, s32[9]{0:T(128)}, u32[]{:S(2)}) copy-start(s32[9]{0:T(128)} %param.29) | copy-start | bytes 112
  10.4 27.7 %copy-start.9 = (bf16[32,2,1152]{2,1,0:T(2,128)(2,1)S(1)}, bf16[32,2,1152]{2,1,0:T(2,128)(2,1)}, u32[]{:S(2)}) copy-start(bf16[32,2,1152]{2,1,0:T(2,128)(2,1)} %param.26) | copy-start | bytes 442372
  10.4 11.3 %collective-permute-start.4 = (bf16[136,512]{1,0:T(8,128)(2,1)}, bf16[136,512]{1,0:T(8,128)(2,1)S(1)}, u32[]{:S(2)}, u32[]{:S(2)}) collective-permute-start(bf16[136,512]{1,0:T(8,128)(2,1)} %get-tuple-element.25), channel_id=1, source_target_pairs={{0,1},{1,0},{2,3},{3,2},{4,5},{5,4},{6,7},{7,6},{8,9},{9,8},{10,11... | collective-permute-start | bytes 417800 | tf_op jit(solution)/shard_map/ppermute | solution.py:19
  18.8 12.1 %collective-permute-start.5 = (bf16[136,512]{1,0:T(8,128)(2,1)}, bf16[136,512]{1,0:T(8,128)(2,1)S(1)}, u32[]{:S(2)}, u32[]{:S(2)}) collective-permute-start(bf16[136,512]{1,0:T(8,128)(2,1)} %get-tuple-element.26), channel_id=1, source_target_pairs={{0,2},{1,3},{2,0},{3,1},{4,6},{5,7},{6,4},{7,5},{8,10},{9,11},{10,... | collective-permute-start | bytes 417800 | tf_op jit(solution)/shard_map/ppermute | solution.py:19
  21.5 9.5 %collective-permute-start.6 = (bf16[136,512]{1,0:T(8,128)(2,1)}, bf16[136,512]{1,0:T(8,128)(2,1)S(1)}, u32[]{:S(2)}, u32[]{:S(2)}) collective-permute-start(bf16[136,512]{1,0:T(8,128)(2,1)} %get-tuple-element.27), channel_id=1, source_target_pairs={{0,3},{1,2},{2,1},{3,0},{4,7},{5,6},{6,5},{7,4},{8,11},{9,10},{10,... | collective-permute-start | bytes 417800 | tf_op jit(solution)/shard_map/ppermute | solution.py:19
  37.6 26.1 %collective-permute-start.12 = (bf16[2048,384]{1,0:T(8,128)(2,1)S(1)}, bf16[2048,384]{1,0:T(8,128)(2,1)}, u32[]{:S(2)}, u32[]{:S(2)}) collective-permute-start(bf16[2048,384]{1,0:T(8,128)(2,1)S(1)} %copy-done.4), channel_id=1, source_target_pairs={{0,4},{4,0},{8,12},{12,8},{1,5},{5,1},{9,13},{13,9},{2,6},{6,2},{1... | collective-permute-start | bytes 4718600 | tf_op jit(solution)/shard_map/ppermute | solution.py:19
  37.6 26.1 %collective-permute-start.13 = (bf16[2048,384]{1,0:T(8,128)(2,1)S(1)}, bf16[2048,384]{1,0:T(8,128)(2,1)}, u32[]{:S(2)}, u32[]{:S(2)}) collective-permute-start(bf16[2048,384]{1,0:T(8,128)(2,1)S(1)} %collective-permute-done.3.refs_3_), channel_id=1, source_target_pairs={{0,4},{4,0},{8,12},{12,8},{1,5},{5,1},{9,13},{13,9},{2,6},{6,2},{1... | collective-permute-start | bytes 4718600 | tf_op jit(solution)/shard_map/ppermute | solution.py:19
  38.2 8.4 %collective-permute-start.9 = (bf16[128,512]{1,0:T(8,128)(2,1)S(1)}, bf16[128,512]{1,0:T(8,128)(2,1)S(1)}, u32[]{:S(2)}, u32[]{:S(2)}) collective-permute-start(bf16[128,512]{1,0:T(8,128)(2,1)S(1)} %merge.1.refs_0_), channel_id=1, source_target_pairs={{0,1},{1,0},{2,3},{3,2},{4,5},{5,4},{6,7},{7,6},{8,9},{9,8},{10,11... | collective-permute-start | bytes 393224 | tf_op jit(solution)/shard_map/ppermute | solution.py:19
  40.1 12.9 %collective-permute-start.8 = (bf16[128,512]{1,0:T(8,128)(2,1)S(1)}, bf16[128,512]{1,0:T(8,128)(2,1)S(1)}, u32[]{:S(2)}, u32[]{:S(2)}) collective-permute-start(bf16[128,512]{1,0:T(8,128)(2,1)S(1)} %merge.1.refs_0_), channel_id=1, source_target_pairs={{0,2},{1,3},{2,0},{3,1},{4,6},{5,7},{6,4},{7,5},{8,10},{9,11},{10,... | collective-permute-start | bytes 393224 | tf_op jit(solution)/shard_map/ppermute | solution.py:19
  42.7 10.8 %collective-permute-start.7 = (bf16[128,512]{1,0:T(8,128)(2,1)S(1)}, bf16[128,512]{1,0:T(8,128)(2,1)S(1)}, u32[]{:S(2)}, u32[]{:S(2)}) collective-permute-start(bf16[128,512]{1,0:T(8,128)(2,1)S(1)} %merge.1.refs_0_), channel_id=1, source_target_pairs={{0,3},{1,2},{2,1},{3,0},{4,7},{5,6},{6,5},{7,4},{8,11},{9,10},{10,... | collective-permute-start | bytes 393224 | tf_op jit(solution)/shard_map/ppermute | solution.py:19
  46.7 22.4 %collective-permute-start = (bf16[16,1152]{1,0:T(8,128)(2,1)S(1)}, bf16[16,1152]{1,0:T(8,128)(2,1)S(1)}, u32[]{:S(2)}, u32[]{:S(2)}) collective-permute-start(bf16[16,1152]{1,0:T(8,128)(2,1)S(1)} %bitcast.26), channel_id=1, source_target_pairs={{0,1},{1,0},{2,3},{3,2},{4,5},{5,4},{6,7},{7,6},{8,9},{9,8},{10,11... | collective-permute-start | bytes 110600 | tf_op jit(solution)/shard_map/ppermute | solution.py:19
  53.0 18.4 %collective-permute-start.1 = (bf16[16,1152]{1,0:T(8,128)(2,1)S(1)}, bf16[16,1152]{1,0:T(8,128)(2,1)S(1)}, u32[]{:S(2)}, u32[]{:S(2)}) collective-permute-start(bf16[16,1152]{1,0:T(8,128)(2,1)S(1)} %bitcast.25), channel_id=1, source_target_pairs={{0,2},{1,3},{2,0},{3,1},{4,6},{5,7},{6,4},{7,5},{8,10},{9,11},{10,... | collective-permute-start | bytes 110600 | tf_op jit(solution)/shard_map/ppermute | solution.py:19
  54.1 1.6 %collective-permute-start.10 = (bf16[2,32,2048]{2,1,0:T(8,128)(2,1)S(1)}, bf16[2,32,2048]{2,1,0:T(8,128)(2,1)S(1)}, u32[]{:S(2)}, u32[]{:S(2)}) collective-permute-start(bf16[2,32,2048]{2,1,0:T(8,128)(2,1)S(1)} %get-tuple-element.30), channel_id=1, source_target_pairs={{0,4},{4,0},{8,12},{12,8},{1,5},{5,1},{9,13},{13,9},{2,6},{6,2},{1... | collective-permute-start | bytes 786440 | tf_op jit(solution)/shard_map/ppermute | solution.py:19
  55.7 5.6 %collective-permute-start.11 = (bf16[32,2048]{1,0:T(8,128)(2,1)S(1)}, bf16[32,2048]{1,0:T(8,128)(2,1)S(1)}, u32[]{:S(2)}, u32[]{:S(2)}) collective-permute-start(bf16[32,2048]{1,0:T(8,128)(2,1)S(1)} %get-tuple-element.32), channel_id=1, source_target_pairs={{0,8},{4,12},{8,0},{12,4},{1,9},{5,13},{9,1},{13,5},{2,10},{6,14},... | collective-permute-start | bytes 393224 | tf_op jit(solution)/shard_map/ppermute | solution.py:19
  61.3 10.1 %collective-permute-start.2 = (bf16[16,1152]{1,0:T(8,128)(2,1)S(1)}, bf16[16,1152]{1,0:T(8,128)(2,1)S(1)}, u32[]{:S(2)}, u32[]{:S(2)}) collective-permute-start(bf16[16,1152]{1,0:T(8,128)(2,1)S(1)} %bitcast.27), channel_id=1, source_target_pairs={{0,3},{1,2},{2,1},{3,0},{4,7},{5,6},{6,5},{7,4},{8,11},{9,10},{10,... | collective-permute-start | bytes 110600 | tf_op jit(solution)/shard_map/ppermute | solution.py:19
  66.8 4.6 %collective-permute-start.14 = (bf16[8,1664]{1,0:T(8,128)(2,1)S(1)}, bf16[8,1664]{1,0:T(8,128)(2,1)S(1)}, u32[]{:S(2)}, u32[]{:S(2)}) collective-permute-start(bf16[8,1664]{1,0:T(8,128)(2,1)S(1)} %get-tuple-element.36), channel_id=1, source_target_pairs={{0,1},{1,0},{2,3},{3,2},{4,5},{5,4},{6,7},{7,6},{8,9},{9,8},{10,11... | collective-permute-start | bytes 79880 | tf_op jit(solution)/shard_map/ppermute | solution.py:19
  68.6 4.8 %collective-permute-start.15 = (bf16[8,1664]{1,0:T(8,128)(2,1)S(1)}, bf16[8,1664]{1,0:T(8,128)(2,1)S(1)}, u32[]{:S(2)}, u32[]{:S(2)}) collective-permute-start(bf16[8,1664]{1,0:T(8,128)(2,1)S(1)} %get-tuple-element.37), channel_id=1, source_target_pairs={{0,2},{1,3},{2,0},{3,1},{4,6},{5,7},{6,4},{7,5},{8,10},{9,11},{10,... | collective-permute-start | bytes 79880 | tf_op jit(solution)/shard_map/ppermute | solution.py:19
  69.0 5.6 %collective-permute-start.16 = (bf16[8,1664]{1,0:T(8,128)(2,1)S(1)}, bf16[8,1664]{1,0:T(8,128)(2,1)S(1)}, u32[]{:S(2)}, u32[]{:S(2)}) collective-permute-start(bf16[8,1664]{1,0:T(8,128)(2,1)S(1)} %get-tuple-element.38), channel_id=1, source_target_pairs={{0,3},{1,2},{2,1},{3,0},{4,7},{5,6},{6,5},{7,4},{8,11},{9,10},{10,... | collective-permute-start | bytes 79880 | tf_op jit(solution)/shard_map/ppermute | solution.py:19
  78.9 4.5 %collective-permute-start.17 = (bf16[16,1152]{1,0:T(8,128)(2,1)S(1)}, bf16[16,1152]{1,0:T(8,128)(2,1)S(1)}, u32[]{:S(2)}, u32[]{:S(2)}) collective-permute-start(bf16[16,1152]{1,0:T(8,128)(2,1)S(1)} %get-tuple-element.40), channel_id=1, source_target_pairs={{0,1},{1,0},{2,3},{3,2},{4,5},{5,4},{6,7},{7,6},{8,9},{9,8},{10,11... | collective-permute-start | bytes 110600 | tf_op jit(solution)/shard_map/ppermute | solution.py:19
  79.2 4.9 %collective-permute-start.18 = (bf16[16,1152]{1,0:T(8,128)(2,1)S(1)}, bf16[16,1152]{1,0:T(8,128)(2,1)S(1)}, u32[]{:S(2)}, u32[]{:S(2)}) collective-permute-start(bf16[16,1152]{1,0:T(8,128)(2,1)S(1)} %get-tuple-element.41), channel_id=1, source_target_pairs={{0,2},{1,3},{2,0},{3,1},{4,6},{5,7},{6,4},{7,5},{8,10},{9,11},{10,... | collective-permute-start | bytes 110600 | tf_op jit(solution)/shard_map/ppermute | solution.py:19
  81.9 5.8 %collective-permute-start.19 = (bf16[16,1152]{1,0:T(8,128)(2,1)S(1)}, bf16[16,1152]{1,0:T(8,128)(2,1)S(1)}, u32[]{:S(2)}, u32[]{:S(2)}) collective-permute-start(bf16[16,1152]{1,0:T(8,128)(2,1)S(1)} %get-tuple-element.42), channel_id=1, source_target_pairs={{0,3},{1,2},{2,1},{3,0},{4,7},{5,6},{6,5},{7,4},{8,11},{9,10},{10,... | collective-permute-start | bytes 110600 | tf_op jit(solution)/shard_map/ppermute | solution.py:19
  (7 other events, 60.0 us)

commit v3 on v2

--- a/solution.py
+++ b/solution.py
@@ -9,6 +9,7 @@
 from jax.experimental.pallas import tpu as pltpu
 from jax.sharding import PartitionSpec as P
 
+
 HD = 128
 SWEEPS = 3
 LANES = 128
@@ -17,6 +18,13 @@
 def swap(values, axis, distance):
     size = lax.axis_size(axis)
     return lax.ppermute(values, axis, [(i, i ^ distance) for i in range(size)])
+
+
+def exchange(blocks):
+    got = [blocks[0]]
+    for s, block in enumerate(blocks[1:], 1):
+        got.append(swap(block, "tm", s))
+    return got
 
 
 def pick(values, index):
@@ -54,19 +62,36 @@
     return PIECES * rows <= width and 2 * share <= 8 and rows % LANES == 0
 
 
+def calls_of(order):
+    return [groups for groups in (order[:1], order[1:-1], order[-1:] if order[1:] else []) if groups]
+
+
 def attend_kernel(
-    groups, share, per_copy, row_cuts, length_ref, freq_ref, pos_ref, q_ref, k_hbm, v_hbm, *refs
+    groups, share, per_copy, row_cuts, length_ref, freq_hbm, pos_hbm, q_hbm, k_hbm, v_hbm, *refs
 ):
     count = len(groups)
-    outs, stats = refs[:count], refs[count:-6]
-    k_buf, v_buf, k_sem, v_sem, cos_ref, sin_ref = refs[-6:]
-    rows = q_ref.shape[0]
+    outs, stats = refs[:count], refs[count:-10]
+    k_buf, v_buf, q_buf, freq_ref, pos_ref, k_sem, v_sem, q_sem, cos_ref, sin_ref = refs[-10:]
+    rows = q_hbm.shape[0]
     keys = k_hbm.shape[0]
     t = lax.axis_index("tm")
     own = t // row_cuts
     width = per_copy * HD
-    copies = []
+    small = [
+        pltpu.make_async_copy(freq_hbm, freq_ref, q_sem.at[count]),
+        pltpu.make_async_copy(pos_hbm, pos_ref, q_sem.at[count + 1]),
+    ]
+    for copy in small:
+        copy.start()
+    copies, wanted = [], []
     for g, a in enumerate(groups):
+        first = pl.multiple_of((own ^ a) * share * HD, HD)
+        wanted.append(
+            pltpu.make_async_copy(
+                q_hbm.at[:, pl.ds(first, share * HD)], q_buf.at[g], q_sem.at[g]
+            )
+        )
+        wanted[g].start()
         for part in range(share // per_copy):
             slot = len(copies)
             column = pl.multiple_of(((own ^ a) * share + part * per_copy) * HD, HD)
@@ -76,7 +101,9 @@
             ]
             for copy in pair:
                 copy.start()
-            copies.append((g, part, column, pair))
+            copies.append((g, part, pair))
+    for copy in small:
+        copy.wait()
 
     even = lax.broadcasted_iota(jnp.int32, (rows, HD), 1) % 2 == 0
     place = jnp.broadcast_to(pos_ref[...].astype(jnp.float32), (HD, rows)).T
@@ -88,15 +115,14 @@
     valid = lax.broadcasted_iota(jnp.int32, (1, keys), 1) < length_ref[0] - t * keys
     scale = 1.0 / math.sqrt(HD)
     held = jnp.zeros((rows, LANES), jnp.float32)
-    for slot, (g, part, column, pair) in enumerate(copies):
-        for copy in pair:
+    for slot, (g, part, pair) in enumerate(copies):
+        for copy in ([wanted[g]] if part == 0 else []) + pair:
             copy.wait()
         for i in range(per_copy):
             head = part * per_copy + i
             at = slice(i * HD, (i + 1) * HD)
             to = slice(head * HD, (head + 1) * HD)
-            from_column = pl.multiple_of(column + i * HD, HD)
-            wide = q_ref[:, pl.ds(from_column, HD)].astype(jnp.float32)
+            wide = q_buf[g, :, to].astype(jnp.float32)
             partner = jnp.where(even, pltpu.roll(wide, HD - 1, 1), pltpu.roll(wide, 1, 1))
             rotated = (wide * cos_ref[...] + partner * sin_ref[...]).astype(jnp.bfloat16)
             scores = lax.dot_general(
@@ -142,14 +168,18 @@
         out_shape = out_shape + [jax.ShapeDtypeStruct((2 * share, rows), jnp.float32)] * n
     result = pl.pallas_call(
         functools.partial(attend_kernel, groups, share, per_copy, row_cuts),
-        in_specs=[SMEM, VMEM, VMEM, VMEM, HBM, HBM],
+        in_specs=[SMEM, HBM, HBM, HBM, HBM, HBM],
         out_specs=[VMEM] * len(out_shape),
         out_shape=out_shape,
         scratch_shapes=[
             buffer,
             buffer,
+            pltpu.VMEM((n, rows, wide), jnp.bfloat16),
+            pltpu.VMEM((1, HD), jnp.float32),
+            pltpu.VMEM((1, rows), jnp.int32),
             pltpu.SemaphoreType.DMA((slots,)),
             pltpu.SemaphoreType.DMA((slots,)),
+            pltpu.SemaphoreType.DMA((n + 2,)),
             pltpu.VMEM((rows, HD), jnp.float32),
             pltpu.VMEM((rows, HD), jnp.float32),
         ],
@@ -158,7 +188,7 @@
             bytes_accessed=4 * n * share * key_count * HD,
             transcendentals=n * share * rows * key_count,
         ),
-        compiler_params=mib(60),
+        compiler_params=mib(57 if groups[-1] == 0 else 60),
         name="attend",
     )(cache_length, frequencies.astype(np.float32)[None], positions[None], queries, keys, values)
     return list(zip(result[:n], result[n:] if not joined else [None] * n))
@@ -205,20 +235,51 @@
     )(*outs, *stats)
 
 
-def project_kernel(head_cuts, row_cuts, cuts, chained, last, *refs):
+def project_kernel(cuts, later, row_cuts, *refs):
     parts, refs = refs[: len(cuts)], refs[len(cuts) :]
-    w_ref, refs = refs[0], refs[1:]
+    w_hbm, total_ref, kept_ref, w_buf, sem = refs
     own = lax.axis_index("tm") // row_cuts
-    depth = parts[0].shape[1]
-    value = refs[0][...] if chained else None
-    for a, part in zip(cuts, parts):
+    depth = w_buf.shape[1]
+    copies = []
+    for i, a in enumerate((*cuts, *later)):
         first = pl.multiple_of((own ^ a) * depth, depth)
-        product = jnp.dot(part[...], w_ref[pl.ds(first, depth), :], preferred_element_type=jnp.float32)
-        value = product if value is None else value + product
-    if not last:
-        refs[-1][...] = value
-        return
-    keep_ref, send_ref, whole_ref = refs[chained:]
+        to = w_buf.at[i] if i < len(cuts) else kept_ref.at[i - len(cuts)]
+        copies.append(pltpu.make_async_copy(w_hbm.at[pl.ds(first, depth)], to, sem.at[i]))
+        copies[i].start()
+    for i, part in enumerate(parts):
+        copies[i].wait()
+        product = jnp.dot(part[...], w_buf[i], preferred_element_type=jnp.float32)
+        total_ref[...] = product + total_ref[...] if i else product
+    for copy in copies[len(cuts) :]:
+        copy.wait()
+
+
+def project(parts, cuts, later, weight, row_cuts):
+    rows, depth = parts[0].shape
+    columns = weight.shape[1]
+    return pl.pallas_call(
+        functools.partial(project_kernel, cuts, later, row_cuts),
+        in_specs=[VMEM] * len(parts) + [HBM],
+        out_specs=[VMEM, VMEM],
+        out_shape=[
+            jax.ShapeDtypeStruct((rows, columns), jnp.float32),
+            jax.ShapeDtypeStruct((len(later), depth, columns), weight.dtype),
+        ],
+        scratch_shapes=[
+            pltpu.VMEM((len(cuts), depth, columns), weight.dtype),
+            pltpu.SemaphoreType.DMA((len(cuts) + len(later),)),
+        ],
+        cost_estimate=cost(2 * len(parts) * rows * depth * columns, 0, weight),
+        compiler_params=mib(16),
+        name="project",
+    )(*parts, weight)
+
+
+def project_rest_kernel(count, total_ref, kept_ref, *refs):
+    parts, (keep_ref, send_ref, whole_ref) = refs[:count], refs[count:]
+    value = total_ref[...]
+    for i, part in enumerate(parts):
+        value = value + jnp.dot(part[...], kept_ref[i], preferred_element_type=jnp.float32)
     chips, rows = keep_ref.shape[:2]
     core = lax.axis_index("heads") % 2
     for chip in range(chips):
@@ -229,34 +290,22 @@
     send_ref[...] = whole_ref[1 - core].astype(jnp.bfloat16)
 
 
-def project(parts, cuts, weight, total, row_cuts, chips):
-    rows, depth = parts[0].shape
-    columns = weight.shape[1]
-    chained = total is not None
-    last = chips > 0
-    if last:
-        block = (chips, rows // (2 * chips), columns)
-        out_shape = [
+def project_rest(total, kept, parts, chips):
+    rows, columns = total.shape
+    block = (chips, rows // (2 * chips), columns)
+    return pl.pallas_call(
+        functools.partial(project_rest_kernel, len(parts)),
+        in_specs=[VMEM] * (2 + len(parts)),
+        out_specs=[VMEM, VMEM],
+        out_shape=[
             jax.ShapeDtypeStruct(block, jnp.float32),
             jax.ShapeDtypeStruct(block, jnp.bfloat16),
-        ]
-        scratch = [pltpu.VMEM((2, *block), jnp.float32)]
-    else:
-        out_shape, scratch = jax.ShapeDtypeStruct((rows, columns), jnp.float32), []
-    return pl.pallas_call(
-        functools.partial(project_kernel, None, row_cuts, cuts, chained, last),
-        in_specs=[VMEM] * (len(parts) + 1 + chained),
-        out_specs=[VMEM, VMEM] if last else VMEM,
-        out_shape=out_shape,
-        scratch_shapes=scratch,
-        cost_estimate=pl.CostEstimate(
-            flops=2 * len(parts) * rows * depth * columns,
-            bytes_accessed=2 * len(parts) * depth * columns,
-            transcendentals=0,
-        ),
-        compiler_params=mib(20),
-        name="project",
-    )(*parts, weight, *([total] if chained else []))
+        ],
+        scratch_shapes=[pltpu.VMEM((2, *block), jnp.float32)],
+        cost_estimate=cost(2 * rows * columns * kept.shape[0] * kept.shape[1], 0, kept),
+        compiler_params=mib(16),
+        name="project_rest",
+    )(total, kept, *parts)
 
 
 def pair_kernel(keep_ref, got_ref, mine_ref, *send_refs):
@@ -416,6 +465,30 @@
     )(steps, start, embedding, in_weight, head_out, *noise, *parts)
 
 
+def noise_kernel(time_each, noise_ref, *outs):
+    t = lax.axis_index("tm")
+    rows = noise_ref.shape[1]
+    for s, out_ref in enumerate(outs):
+        block = noise_ref[t ^ s].astype(jnp.float32)
+        for i in range(time_each):
+            out_ref[i * rows : (i + 1) * rows] = block[:, i, :].astype(jnp.bfloat16)
+
+
+def noise_blocks(noise_draws, n_tm):
+    rows, time_each, chan = noise_draws.shape
+    own_rows = rows // n_tm
+    block = jax.ShapeDtypeStruct((time_each * own_rows, chan), noise_draws.dtype)
+    return pl.pallas_call(
+        functools.partial(noise_kernel, time_each),
+        in_specs=[VMEM],
+        out_specs=[VMEM] * n_tm,
+        out_shape=[block] * n_tm,
+        cost_estimate=cost(0, 0, noise_draws, noise_draws),
+        compiler_params=mib(4),
+        name="noise",
+    )(noise_draws.reshape(n_tm, own_rows, time_each, chan))
+
+
 def finish_kernel(sizes, start_ref, *refs):
     time_each, rows = sizes
     parts, out_ref = refs[:-1], refs[-1]
@@ -471,7 +544,7 @@
     head_cuts = math.gcd(local_heads, n_tm)
     row_cuts = n_tm // head_cuts
     share = local_heads // head_cuts
-    own_cut, own_row_cut = t // row_cuts, t % row_cuts
+    own_row_cut = t % row_cuts
 
     def cut(values, index, axis):
         if row_cuts == 1:
@@ -479,12 +552,15 @@
         size = values.shape[axis] // row_cuts
         return lax.dynamic_slice_in_dim(values, index * size, size, axis)
 
+    chips = n_heads // 2
+    far = []
+    for s in range(1, chips):
+        far.append(swap(cond_weight, "heads", 2 * s))
+    near = swap(cond_weight, "heads", 1)
+
     order = list(range(head_cuts))[::-1]
-    half = max(1, head_cuts // 2)
     outs, stats = [None] * n_tm, [None] * n_tm
-    for groups in (order[:half], order[half:]):
-        if not groups:
-            continue
+    for groups in calls_of(order):
         blocks = attend(
             queries, cache_keys, cache_values, positions, cache_length, groups, share, row_cuts
         )
@@ -497,15 +573,8 @@
                     outs[s] = swap(outs[s], "tm", s)
                     stats[s] = None if stat is None else swap(stats[s], "tm", s)
     attended = merge(outs, stats, share, rows // row_cuts)
-    chips = n_heads // 2
-
-    far = [cond_weight] + [swap(cond_weight, "heads", 2 * s) for s in range(1, chips)]
-    far, attended = lax.optimization_barrier((far, attended))
-    near = [swap(w, "heads", 1) for w in far]
-    cond_shards = [w for pair in zip(far, near) for w in pair]
-
-    parts = [attended] + [swap(attended, "tm", s) for s in range(1, n_tm)]
-    projected = None
+    parts = exchange([attended] * n_tm)
+    by_cut = []
     for a in range(head_cuts):
         part = parts[a * row_cuts : (a + 1) * row_cuts]
         if row_cuts > 1:
@@ -513,23 +582,28 @@
             part = part.reshape(rows, share * HD)
         else:
             part = part[0]
-        projected = project(
-            [part], [a], out_weight, projected, row_cuts, chips if a == head_cuts - 1 else 0
-        )
-
-    keep, send = projected
-    mine, far_rows = pair_sum(keep, swap(send, "heads", 1))
-    got = [swap(r, "heads", 2 * s) for s, r in enumerate(far_rows, 1)]
+        by_cut.append(part)
+    half = max(1, head_cuts // 2)
+    cuts = list(range(head_cuts))
+    total, kept = project(by_cut[:half], cuts[:half], cuts[half:], out_weight, row_cuts)
+    keep, send = project_rest(total, kept, by_cut[half:], chips)
+
+    far, send = lax.optimization_barrier((far, send))
+    other = swap(send, "heads", 1)
+    mine, far_rows = pair_sum(keep, other)
+    got = []
+    for s, r in enumerate(far_rows, 1):
+        got.append(swap(r, "heads", 2 * s))
+
+    cond_shards = [cond_weight, near]
+    for s, w in enumerate(far, 1):
+        cond_shards += [w, swap(w, "heads", 1)]
 
     cond = condition_parts(mine, got, residual, norm_gain, cond_shards, n_tm, h, t)
-    cond = [cond[0]] + [swap(cond[s], "tm", s) for s in range(1, n_tm)]
-
-    noise_rows = noise_draws.transpose(1, 0, 2).reshape(time_each, n_tm, own_rows, chan)
-    noise = [
-        lax.dynamic_index_in_dim(noise_rows, t ^ s, 1, False).reshape(time_each * own_rows, chan)
-        for s in range(n_tm)
-    ]
-    noise = [noise[0]] + [swap(noise[s], "tm", s) for s in range(1, n_tm)]
+    cond = exchange(cond)
+
+    noise = noise_blocks(noise_draws, n_tm)
+    noise = exchange(noise)
     levels = plan.astype(jnp.float32)
     half_width = hidden_width // 2
     frequencies = jnp.exp(
@@ -543,7 +617,7 @@
     change = sweep_all(
         cond, noise, embedding, steps, start, in_weight, head_out, time_each, model
     )
-    back = [change[0]] + [swap(change[s], "tm", s) for s in range(1, n_tm)]
+    back = exchange(change)
     return finish(start, back, time_each)
 
 
@@ -564,6 +638,7 @@
         P("groups"),
         P(),
     )
+
     return jax.shard_map(
         shards,
         mesh=mesh,

time: 88.7 us -> 75 us (0.85)
  waiting for transfers between devices: 31.1 us -> 19.6 us
  local copies, waits for them, and re-layouts: 5.52 us -> 4.34 us
  Pallas kernels: 24.1 us -> 23.2 us
    ppermute x20, waiting for transfers between devices: 31.1 us -> 19.6 us  [swap(): return lax.ppermute(values, axis, [(i, i ^ distance) for i in range(size)])]
    pallas_call x1, Pallas kernels: 3.07 us -> 1.06 us  [condition_parts(): pl.pallas_call(functools.partial(condition_kernel, len(got) + 1, shards,...]
    unnamed x26 -> x20, local copies, waits for them, and re-layouts: 5.41 us -> 4.34 us
    pallas_call x4 -> x3, Pallas kernels: 1.91 us -> 2.66 us  [the longest x1 1.45 us: project(): pl.pallas_call(functools.partial(project_kernel, cuts, later, row_cuts),...]
    pallas_call x2 -> x3, Pallas kernels: 13.5 us -> 13.9 us  [attend(): pl.pallas_call(functools.partial(attend_kernel, groups, share, per_copy,...]
  transfers between devices with their start and end apart: 20 -> 20, of which waited for: 9 -> 9; matrix products, arithmetic and copies ran while one was open for 1% -> 0% of each run, Pallas kernels for 22% -> 24%
where the time goes in v3:
time: 75 us; the launch traced here: 74.8 us
  starting transfers between devices  26.3 us (35%)
  Pallas kernels  23.2 us (31%)
  waiting for transfers between devices  19.6 us (26%)
  local copies, waits for them, and re-layouts  4.34 us (6%)
  between operations  0.87 us (1%)
    ppermute x20, starting transfers between devices, swap(): return lax.ppermute(values, axis, [(i, i ^ distance) for i in range(size)])  26.3 us
    ppermute x20, waiting for transfers between devices, swap(): return lax.ppermute(values, axis, [(i, i ^ distance) for i in range(size)])  19.6 us
    pallas_call x3, Pallas kernels, attend(): pl.pallas_call(functools.partial(attend_kernel, groups, share, per_copy,...  13.9 us
    unnamed x20, local copies, waits for them, and re-layouts  4.34 us
    pallas_call x1, Pallas kernels, sweep_all(): pl.pallas_call(functools.partial(sweep_kernel, (n_tm, time_each, rows, mo...  4.25 us
  transfers between devices with their start and end apart: 20, of which 9 were waited for; matrix products, arithmetic and copies ran while one was open for 0% of the time, Pallas kernels for 24%

profile of v3, /device:TPU:0, one launch (start us, length us, event | category | flops | bytes accessed | tf_op | source)
XLA Modules:
  0.0 74.8 jit_solution(3608266115211323920)
XLA Ops:
  0.0 3.0 %collective-permute-start.9 = (bf16[2048,384]{1,0:T(8,128)(2,1)}, bf16[2048,384]{1,0:T(8,128)(2,1)S(1)}, u32[]{:S(2)}, u32[]{:S(2)}) collective-permute-start(bf16[2048,384]{1,0:T(8,128)(2,1)} %refs_1_.1), channel_id=1, source_target_pairs={{0,8},{4,12},{8,0},{12,4},{1,9},{5,13},{9,1},{13,5},{2,10},{6,14},... | collective-permute-start | bytes 4718600 | tf_op jit(solution)/shard_map/ppermute | solution.py:20
  3.6 6.1 %attend.4 = (bf16[136,512]{1,0:T(8,128)(2,1)}, bf16[136,512]{1,0:T(8,128)(2,1)}) custom-call(s32[1]{0:T(128)S(6)} %copy.18.length_ref, f32[1,128]{1,0:T(1,128)} %constant.10.clone.freq_hbm, s32[1,128]{1,0:T(1,128)} %bitcast.10, bf16[128,2048]{1,0:T(8,128)(2,1)} %q_hbm.5, bf16[1024,2048]{1,0:T(8,128)(2,1)} %k_hbm.5, bf16[1024,2048]{1,0:T(8,128)(2,1)} %v_hbm.5), custom_call_target="tpu_custom_call" | custom-call | flops 536870912 | bytes 4194304 | tf_op jit(solution)/shard_map/attend/pallas_call | solution.py:169
  9.7 1.6 %collective-permute-start.3 = (bf16[136,512]{1,0:T(8,128)(2,1)}, bf16[136,512]{1,0:T(8,128)(2,1)S(1)}, u32[]{:S(2)}, u32[]{:S(2)}) collective-permute-start(bf16[136,512]{1,0:T(8,128)(2,1)} %get-tuple-element.31), channel_id=1, source_target_pairs={{0,1},{1,0},{2,3},{3,2},{4,5},{5,4},{6,7},{7,6},{8,9},{9,8},{10,11... | collective-permute-start | bytes 417800 | tf_op jit(solution)/shard_map/ppermute | solution.py:20
  11.4 2.6 %collective-permute-start.4 = (bf16[136,512]{1,0:T(8,128)(2,1)}, bf16[136,512]{1,0:T(8,128)(2,1)S(1)}, u32[]{:S(2)}, u32[]{:S(2)}) collective-permute-start(bf16[136,512]{1,0:T(8,128)(2,1)} %get-tuple-element.32), channel_id=1, source_target_pairs={{0,2},{1,3},{2,0},{3,1},{4,6},{5,7},{6,4},{7,5},{8,10},{9,11},{10,... | collective-permute-start | bytes 417800 | tf_op jit(solution)/shard_map/ppermute | solution.py:20
  14.0 3.8 %attend.5 = bf16[136,512]{1,0:T(8,128)(2,1)} custom-call(s32[1]{0:T(128)S(6)} %copy.18.length_ref, f32[1,128]{1,0:T(1,128)} %constant.10.clone.freq_hbm, s32[1,128]{1,0:T(1,128)} %bitcast.11, bf16[128,2048]{1,0:T(8,128)(2,1)} %q_hbm.5, bf16[1024,2048]{1,0:T(8,128)(2,1)} %k_hbm.5, bf16[1024,2048]{1,0:T(8,128)(2,1)} %v_hbm.5), custom_call_target="tpu_custom_call" | custom-call | flops 268435456 | bytes 2097152 | tf_op jit(solution)/shard_map/attend/pallas_call | solution.py:169
  18.1 4.0 %attend.3.refs_0_ = bf16[136,512]{1,0:T(8,128)(2,1)} custom-call(s32[1]{0:T(128)S(6)} %copy.18.length_ref, f32[1,128]{1,0:T(1,128)} %constant.10.clone.freq_hbm, s32[1,128]{1,0:T(1,128)} %bitcast.12, bf16[128,2048]{1,0:T(8,128)(2,1)} %q_hbm.5, bf16[1024,2048]{1,0:T(8,128)(2,1)} %k_hbm.5, bf16[1024,2048]{1,0:T(8,128)(2,1)} %v_hbm.5), custom_call_target="tpu_custom_call" | custom-call | flops 268435456 | bytes 2097152 | tf_op jit(solution)/shard_map/attend/pallas_call | solution.py:169
  22.1 2.8 %collective-permute-done.5.refs_3_ = bf16[136,512]{1,0:T(8,128)(2,1)S(1)} collective-permute-done((bf16[136,512]{1,0:T(8,128)(2,1)}, bf16[136,512]{1,0:T(8,128)(2,1)S(1)}, u32[]{:S(2)}, u32[]{:S(2)}) %collective-permute-start.5) | collective-permute-done | bytes 139296 | tf_op jit(solution)/shard_map/ppermute | solution.py:20
  26.4 2.0 %collective-permute-start.6 = (bf16[128,512]{1,0:T(8,128)(2,1)S(1)}, bf16[128,512]{1,0:T(8,128)(2,1)S(1)}, u32[]{:S(2)}, u32[]{:S(2)}) collective-permute-start(bf16[128,512]{1,0:T(8,128)(2,1)S(1)} %merge.1.refs_0_), channel_id=1, source_target_pairs={{0,1},{1,0},{2,3},{3,2},{4,5},{5,4},{6,7},{7,6},{8,9},{9,8},{10,11... | collective-permute-start | bytes 393224 | tf_op jit(solution)/shard_map/ppermute | solution.py:20
  29.4 1.4 %collective-permute-start.8 = (bf16[128,512]{1,0:T(8,128)(2,1)S(1)}, bf16[128,512]{1,0:T(8,128)(2,1)S(1)}, u32[]{:S(2)}, u32[]{:S(2)}) collective-permute-start(bf16[128,512]{1,0:T(8,128)(2,1)S(1)} %merge.1.refs_0_), channel_id=1, source_target_pairs={{0,3},{1,2},{2,1},{3,0},{4,7},{5,6},{6,5},{7,4},{8,11},{9,10},{10,... | collective-permute-start | bytes 393224 | tf_op jit(solution)/shard_map/ppermute | solution.py:20
  30.8 1.8 %collective-permute-done.6.refs_1_ = bf16[128,512]{1,0:T(8,128)(2,1)S(1)} collective-permute-done((bf16[128,512]{1,0:T(8,128)(2,1)S(1)}, bf16[128,512]{1,0:T(8,128)(2,1)S(1)}, u32[]{:S(2)}, u32[]{:S(2)}) %collective-permute-start.6) | collective-permute-done | bytes 131104 | tf_op jit(solution)/shard_map/ppermute | solution.py:20
  32.7 3.4 %copy-done = bf16[2048,2048]{1,0:T(8,128)(2,1)S(1)} copy-done((bf16[2048,2048]{1,0:T(8,128)(2,1)S(1)}, bf16[2048,2048]{1,0:T(8,128)(2,1)}, u32[]{:S(2)}) %copy-start) | copy-done | bytes 8388632
  36.1 1.4 %project.1 = (f32[128,2048]{1,0:T(8,128)S(1)}, bf16[2,512,2048]{2,1,0:T(8,128)(2,1)S(1)}) custom-call(bf16[128,512]{1,0:T(8,128)(2,1)S(1)} %merge.1.refs_0_, bf16[128,512]{1,0:T(8,128)(2,1)S(1)} %collective-permute-done.6.refs_1_, bf16[2048,2048]{1,0:T(8,128)(2,1)S(1)} %copy-done), custom_call_target="tpu_custom_call" | custom-call | flops 536870912 | bytes 8388608 | tf_op jit(solution)/shard_map/project/pallas_call | solution.py:260
  37.6 2.8 %collective-permute-done.7.refs_0_ = bf16[128,512]{1,0:T(8,128)(2,1)S(1)} collective-permute-done((bf16[128,512]{1,0:T(8,128)(2,1)S(1)}, bf16[128,512]{1,0:T(8,128)(2,1)S(1)}, u32[]{:S(2)}, u32[]{:S(2)}) %collective-permute-start.7) | collective-permute-done | bytes 131104 | tf_op jit(solution)/shard_map/ppermute | solution.py:20
  41.7 2.1 %collective-permute-start = (bf16[16,1152]{1,0:T(8,128)(2,1)S(1)}, bf16[16,1152]{1,0:T(8,128)(2,1)S(1)}, u32[]{:S(2)}, u32[]{:S(2)}) collective-permute-start(bf16[16,1152]{1,0:T(8,128)(2,1)S(1)} %get-tuple-element.28), channel_id=1, source_target_pairs={{0,1},{1,0},{2,3},{3,2},{4,5},{5,4},{6,7},{7,6},{8,9},{9,8},{10,11... | collective-permute-start | bytes 110600 | tf_op jit(solution)/shard_map/ppermute | solution.py:20
  45.2 1.2 %collective-permute-done.10.got_ref = bf16[2,32,2048]{2,1,0:T(8,128)(2,1)S(1)} collective-permute-done((bf16[2,32,2048]{2,1,0:T(8,128)(2,1)S(1)}, bf16[2,32,2048]{2,1,0:T(8,128)(2,1)S(1)}, u32[]{:S(2)}, u32[]{:S(2)}) %collective-permute-start.10) | collective-permute-done | bytes 262176 | tf_op jit(solution)/shard_map/ppermute | solution.py:20
  47.0 1.6 %collective-permute-start.2 = (bf16[16,1152]{1,0:T(8,128)(2,1)S(1)}, bf16[16,1152]{1,0:T(8,128)(2,1)S(1)}, u32[]{:S(2)}, u32[]{:S(2)}) collective-permute-start(bf16[16,1152]{1,0:T(8,128)(2,1)S(1)} %get-tuple-element.30), channel_id=1, source_target_pairs={{0,3},{1,2},{2,1},{3,0},{4,7},{5,6},{6,5},{7,4},{8,11},{9,10},{10,... | collective-permute-start | bytes 110600 | tf_op jit(solution)/shard_map/ppermute | solution.py:20
  48.6 3.5 %collective-permute-done.11.refs_0_ = bf16[32,2048]{1,0:T(8,128)(2,1)S(1)} collective-permute-done((bf16[32,2048]{1,0:T(8,128)(2,1)S(1)}, bf16[32,2048]{1,0:T(8,128)(2,1)S(1)}, u32[]{:S(2)}, u32[]{:S(2)}) %collective-permute-start.11) | collective-permute-done | bytes 131104 | tf_op jit(solution)/shard_map/ppermute | solution.py:20
  53.2 2.0 %collective-permute-start.14 = (bf16[8,1664]{1,0:T(8,128)(2,1)S(1)}, bf16[8,1664]{1,0:T(8,128)(2,1)S(1)}, u32[]{:S(2)}, u32[]{:S(2)}) collective-permute-start(bf16[8,1664]{1,0:T(8,128)(2,1)S(1)} %get-tuple-element.42), channel_id=1, source_target_pairs={{0,1},{1,0},{2,3},{3,2},{4,5},{5,4},{6,7},{7,6},{8,9},{9,8},{10,11... | collective-permute-start | bytes 79880 | tf_op jit(solution)/shard_map/ppermute | solution.py:20
  55.3 2.4 %collective-permute-start.16 = (bf16[8,1664]{1,0:T(8,128)(2,1)S(1)}, bf16[8,1664]{1,0:T(8,128)(2,1)S(1)}, u32[]{:S(2)}, u32[]{:S(2)}) collective-permute-start(bf16[8,1664]{1,0:T(8,128)(2,1)S(1)} %get-tuple-element.44), channel_id=1, source_target_pairs={{0,3},{1,2},{2,1},{3,0},{4,7},{5,6},{6,5},{7,4},{8,11},{9,10},{10,... | collective-permute-start | bytes 79880 | tf_op jit(solution)/shard_map/ppermute | solution.py:20
  57.7 2.2 %collective-permute-done.15.refs_6_ = bf16[8,1664]{1,0:T(8,128)(2,1)S(1)} collective-permute-done((bf16[8,1664]{1,0:T(8,128)(2,1)S(1)}, bf16[8,1664]{1,0:T(8,128)(2,1)S(1)}, u32[]{:S(2)}, u32[]{:S(2)}) %collective-permute-start.15) | collective-permute-done | bytes 26656 | tf_op jit(solution)/shard_map/ppermute | solution.py:20
  60.9 4.2 %sweeps.1 = (bf16[16,1152]{1,0:T(8,128)(2,1)S(1)}, bf16[16,1152]{1,0:T(8,128)(2,1)S(1)}, bf16[16,1152]{1,0:T(8,128)(2,1)S(1)}, bf16[16,1152]{1,0:T(8,128)(2,1)S(1)}) custom-call(f32[16]{0:T(128)S(1)} %pad_maximum_fusion.1.steps, f32[4,8,1152]{2,1,0:T(8,128)S(1)} %bitcast.5, f32[8,1536]{1,0:T(8,128)S(1)} %pad_maximum_fusion.embed_ref, ...), custom_call_target="tpu_custom_call" | custom-call | flops 1132462080 | bytes 7077888 | tf_op jit(solution)/shard_map/sweeps/pallas_call | solution.py:454
  65.3 2.8 %collective-permute-start.18 = (bf16[16,1152]{1,0:T(8,128)(2,1)S(1)}, bf16[16,1152]{1,0:T(8,128)(2,1)S(1)}, u32[]{:S(2)}, u32[]{:S(2)}) collective-permute-start(bf16[16,1152]{1,0:T(8,128)(2,1)S(1)} %get-tuple-element.47), channel_id=1, source_target_pairs={{0,2},{1,3},{2,0},{3,1},{4,6},{5,7},{6,4},{7,5},{8,10},{9,11},{10,... | collective-permute-start | bytes 110600 | tf_op jit(solution)/shard_map/ppermute | solution.py:20
  68.2 1.5 %collective-permute-start.19 = (bf16[16,1152]{1,0:T(8,128)(2,1)S(1)}, bf16[16,1152]{1,0:T(8,128)(2,1)S(1)}, u32[]{:S(2)}, u32[]{:S(2)}) collective-permute-start(bf16[16,1152]{1,0:T(8,128)(2,1)S(1)} %get-tuple-element.48), channel_id=1, source_target_pairs={{0,3},{1,2},{2,1},{3,0},{4,7},{5,6},{6,5},{7,4},{8,11},{9,10},{10,... | collective-permute-start | bytes 110600 | tf_op jit(solution)/shard_map/ppermute | solution.py:20
  70.6 3.3 %collective-permute-done.19.refs_3_ = bf16[16,1152]{1,0:T(8,128)(2,1)S(1)} collective-permute-done((bf16[16,1152]{1,0:T(8,128)(2,1)S(1)}, bf16[16,1152]{1,0:T(8,128)(2,1)S(1)}, u32[]{:S(2)}, u32[]{:S(2)}) %collective-permute-start.19) | collective-permute-done | bytes 36896 | tf_op jit(solution)/shard_map/ppermute | solution.py:20
  (53 shorter events, 10.4 us)
Async XLA Ops:
  0.0 41.2 %collective-permute-start.9 = (bf16[2048,384]{1,0:T(8,128)(2,1)}, bf16[2048,384]{1,0:T(8,128)(2,1)S(1)}, u32[]{:S(2)}, u32[]{:S(2)}) collective-permute-start(bf16[2048,384]{1,0:T(8,128)(2,1)} %refs_1_.1), channel_id=1, source_target_pairs={{0,8},{4,12},{8,0},{12,4},{1,9},{5,13},{9,1},{13,5},{2,10},{6,14},... | collective-permute-start | bytes 4718600 | tf_op jit(solution)/shard_map/ppermute | solution.py:20
  9.7 12.4 %collective-permute-start.3 = (bf16[136,512]{1,0:T(8,128)(2,1)}, bf16[136,512]{1,0:T(8,128)(2,1)S(1)}, u32[]{:S(2)}, u32[]{:S(2)}) collective-permute-start(bf16[136,512]{1,0:T(8,128)(2,1)} %get-tuple-element.31), channel_id=1, source_target_pairs={{0,1},{1,0},{2,3},{3,2},{4,5},{5,4},{6,7},{7,6},{8,9},{9,8},{10,11... | collective-permute-start | bytes 417800 | tf_op jit(solution)/shard_map/ppermute | solution.py:20
  11.4 10.7 %collective-permute-start.4 = (bf16[136,512]{1,0:T(8,128)(2,1)}, bf16[136,512]{1,0:T(8,128)(2,1)S(1)}, u32[]{:S(2)}, u32[]{:S(2)}) collective-permute-start(bf16[136,512]{1,0:T(8,128)(2,1)} %get-tuple-element.32), channel_id=1, source_target_pairs={{0,2},{1,3},{2,0},{3,1},{4,6},{5,7},{6,4},{7,5},{8,10},{9,11},{10,... | collective-permute-start | bytes 417800 | tf_op jit(solution)/shard_map/ppermute | solution.py:20
  17.8 13.0 %copy-start.3 = (bf16[2048,384]{1,0:T(8,128)(2,1)S(1)}, bf16[2048,384]{1,0:T(8,128)(2,1)}, u32[]{:S(2)}) copy-start(bf16[2048,384]{1,0:T(8,128)(2,1)} %refs_1_.1) | copy-start | bytes 4718596
  17.8 7.1 %collective-permute-start.5 = (bf16[136,512]{1,0:T(8,128)(2,1)}, bf16[136,512]{1,0:T(8,128)(2,1)S(1)}, u32[]{:S(2)}, u32[]{:S(2)}) collective-permute-start(bf16[136,512]{1,0:T(8,128)(2,1)} %attend.5), channel_id=1, source_target_pairs={{0,3},{1,2},{2,1},{3,0},{4,7},{5,6},{6,5},{7,4},{8,11},{9,10},{10,... | collective-permute-start | bytes 417800 | tf_op jit(solution)/shard_map/ppermute | solution.py:20
  26.4 6.3 %collective-permute-start.6 = (bf16[128,512]{1,0:T(8,128)(2,1)S(1)}, bf16[128,512]{1,0:T(8,128)(2,1)S(1)}, u32[]{:S(2)}, u32[]{:S(2)}) collective-permute-start(bf16[128,512]{1,0:T(8,128)(2,1)S(1)} %merge.1.refs_0_), channel_id=1, source_target_pairs={{0,1},{1,0},{2,3},{3,2},{4,5},{5,4},{6,7},{7,6},{8,9},{9,8},{10,11... | collective-permute-start | bytes 393224 | tf_op jit(solution)/shard_map/ppermute | solution.py:20
  28.4 12.0 %collective-permute-start.7 = (bf16[128,512]{1,0:T(8,128)(2,1)S(1)}, bf16[128,512]{1,0:T(8,128)(2,1)S(1)}, u32[]{:S(2)}, u32[]{:S(2)}) collective-permute-start(bf16[128,512]{1,0:T(8,128)(2,1)S(1)} %merge.1.refs_0_), channel_id=1, source_target_pairs={{0,2},{1,3},{2,0},{3,1},{4,6},{5,7},{6,4},{7,5},{8,10},{9,11},{10,... | collective-permute-start | bytes 393224 | tf_op jit(solution)/shard_map/ppermute | solution.py:20
  29.4 10.9 %collective-permute-start.8 = (bf16[128,512]{1,0:T(8,128)(2,1)S(1)}, bf16[128,512]{1,0:T(8,128)(2,1)S(1)}, u32[]{:S(2)}, u32[]{:S(2)}) collective-permute-start(bf16[128,512]{1,0:T(8,128)(2,1)S(1)} %merge.1.refs_0_), channel_id=1, source_target_pairs={{0,3},{1,2},{2,1},{3,0},{4,7},{5,6},{6,5},{7,4},{8,11},{9,10},{10,... | collective-permute-start | bytes 393224 | tf_op jit(solution)/shard_map/ppermute | solution.py:20
  30.8 16.2 %collective-permute-start.12 = (bf16[2048,384]{1,0:T(8,128)(2,1)S(1)}, bf16[2048,384]{1,0:T(8,128)(2,1)S(1)}, u32[]{:S(2)}, u32[]{:S(2)}) collective-permute-start(bf16[2048,384]{1,0:T(8,128)(2,1)S(1)} %copy-done.3), channel_id=1, source_target_pairs={{0,4},{4,0},{8,12},{12,8},{1,5},{5,1},{9,13},{13,9},{2,6},{6,2},{1... | collective-permute-start | bytes 4718600 | tf_op jit(solution)/shard_map/ppermute | solution.py:20
  37.5 14.5 %copy-start.6 = (bf16[128,2048]{1,0:T(8,128)(2,1)S(1)}, bf16[128,2048]{1,0:T(8,128)(2,1)}, u32[]{:S(2)}) copy-start(bf16[128,2048]{1,0:T(8,128)(2,1)} %param.20) | copy-start | bytes 1572868
  37.5 14.5 %copy-start.8 = (f32[2048]{0:T(1024)S(1)}, f32[2048]{0:T(1024)}, u32[]{:S(2)}) copy-start(f32[2048]{0:T(1024)} %param.22) | copy-start | bytes 24580
  41.2 10.9 %collective-permute-start.13 = (bf16[2048,384]{1,0:T(8,128)(2,1)S(1)}, bf16[2048,384]{1,0:T(8,128)(2,1)S(1)}, u32[]{:S(2)}, u32[]{:S(2)}) collective-permute-start(bf16[2048,384]{1,0:T(8,128)(2,1)S(1)} %collective-permute-done.9.refs_3_), channel_id=1, source_target_pairs={{0,4},{4,0},{8,12},{12,8},{1,5},{5,1},{9,13},{13,9},{2,6},{6,2},{1... | collective-permute-start | bytes 4718600 | tf_op jit(solution)/shard_map/ppermute | solution.py:20
  41.7 13.6 %collective-permute-start = (bf16[16,1152]{1,0:T(8,128)(2,1)S(1)}, bf16[16,1152]{1,0:T(8,128)(2,1)S(1)}, u32[]{:S(2)}, u32[]{:S(2)}) collective-permute-start(bf16[16,1152]{1,0:T(8,128)(2,1)S(1)} %get-tuple-element.28), channel_id=1, source_target_pairs={{0,1},{1,0},{2,3},{3,2},{4,5},{5,4},{6,7},{7,6},{8,9},{9,8},{10,11... | collective-permute-start | bytes 110600 | tf_op jit(solution)/shard_map/ppermute | solution.py:20
  43.8 14.0 %collective-permute-start.1 = (bf16[16,1152]{1,0:T(8,128)(2,1)S(1)}, bf16[16,1152]{1,0:T(8,128)(2,1)S(1)}, u32[]{:S(2)}, u32[]{:S(2)}) collective-permute-start(bf16[16,1152]{1,0:T(8,128)(2,1)S(1)} %get-tuple-element.29), channel_id=1, source_target_pairs={{0,2},{1,3},{2,0},{3,1},{4,6},{5,7},{6,4},{7,5},{8,10},{9,11},{10,... | collective-permute-start | bytes 110600 | tf_op jit(solution)/shard_map/ppermute | solution.py:20
  44.8 1.5 %collective-permute-start.10 = (bf16[2,32,2048]{2,1,0:T(8,128)(2,1)S(1)}, bf16[2,32,2048]{2,1,0:T(8,128)(2,1)S(1)}, u32[]{:S(2)}, u32[]{:S(2)}) collective-permute-start(bf16[2,32,2048]{2,1,0:T(8,128)(2,1)S(1)} %get-tuple-element.37), channel_id=1, source_target_pairs={{0,4},{4,0},{8,12},{12,8},{1,5},{5,1},{9,13},{13,9},{2,6},{6,2},{1... | collective-permute-start | bytes 786440 | tf_op jit(solution)/shard_map/ppermute | solution.py:20
  46.4 5.7 %collective-permute-start.11 = (bf16[32,2048]{1,0:T(8,128)(2,1)S(1)}, bf16[32,2048]{1,0:T(8,128)(2,1)S(1)}, u32[]{:S(2)}, u32[]{:S(2)}) collective-permute-start(bf16[32,2048]{1,0:T(8,128)(2,1)S(1)} %get-tuple-element.39), channel_id=1, source_target_pairs={{0,8},{4,12},{8,0},{12,4},{1,9},{5,13},{9,1},{13,5},{2,10},{6,14},... | collective-permute-start | bytes 393224 | tf_op jit(solution)/shard_map/ppermute | solution.py:20
  47.0 10.7 %collective-permute-start.2 = (bf16[16,1152]{1,0:T(8,128)(2,1)S(1)}, bf16[16,1152]{1,0:T(8,128)(2,1)S(1)}, u32[]{:S(2)}, u32[]{:S(2)}) collective-permute-start(bf16[16,1152]{1,0:T(8,128)(2,1)S(1)} %get-tuple-element.30), channel_id=1, source_target_pairs={{0,3},{1,2},{2,1},{3,0},{4,7},{5,6},{6,5},{7,4},{8,11},{9,10},{10,... | collective-permute-start | bytes 110600 | tf_op jit(solution)/shard_map/ppermute | solution.py:20
  52.1 8.9 %copy-start.1 = (bf16[1152,1536]{1,0:T(8,128)(2,1)S(1)}, bf16[1152,1536]{1,0:T(8,128)(2,1)}, u32[]{:S(2)}) copy-start(bf16[1152,1536]{1,0:T(8,128)(2,1)} %in_ref.1) | copy-start | bytes 10616836
  53.2 4.5 %collective-permute-start.14 = (bf16[8,1664]{1,0:T(8,128)(2,1)S(1)}, bf16[8,1664]{1,0:T(8,128)(2,1)S(1)}, u32[]{:S(2)}, u32[]{:S(2)}) collective-permute-start(bf16[8,1664]{1,0:T(8,128)(2,1)S(1)} %get-tuple-element.42), channel_id=1, source_target_pairs={{0,1},{1,0},{2,3},{3,2},{4,5},{5,4},{6,7},{7,6},{8,9},{9,8},{10,11... | collective-permute-start | bytes 79880 | tf_op jit(solution)/shard_map/ppermute | solution.py:20
  55.1 4.7 %collective-permute-start.15 = (bf16[8,1664]{1,0:T(8,128)(2,1)S(1)}, bf16[8,1664]{1,0:T(8,128)(2,1)S(1)}, u32[]{:S(2)}, u32[]{:S(2)}) collective-permute-start(bf16[8,1664]{1,0:T(8,128)(2,1)S(1)} %get-tuple-element.43), channel_id=1, source_target_pairs={{0,2},{1,3},{2,0},{3,1},{4,6},{5,7},{6,4},{7,5},{8,10},{9,11},{10,... | collective-permute-start | bytes 79880 | tf_op jit(solution)/shard_map/ppermute | solution.py:20
  55.3 5.6 %collective-permute-start.16 = (bf16[8,1664]{1,0:T(8,128)(2,1)S(1)}, bf16[8,1664]{1,0:T(8,128)(2,1)S(1)}, u32[]{:S(2)}, u32[]{:S(2)}) collective-permute-start(bf16[8,1664]{1,0:T(8,128)(2,1)S(1)} %get-tuple-element.44), channel_id=1, source_target_pairs={{0,3},{1,2},{2,1},{3,0},{4,7},{5,6},{6,5},{7,4},{8,11},{9,10},{10,... | collective-permute-start | bytes 79880 | tf_op jit(solution)/shard_map/ppermute | solution.py:20
  65.2 4.5 %collective-permute-start.17 = (bf16[16,1152]{1,0:T(8,128)(2,1)S(1)}, bf16[16,1152]{1,0:T(8,128)(2,1)S(1)}, u32[]{:S(2)}, u32[]{:S(2)}) collective-permute-start(bf16[16,1152]{1,0:T(8,128)(2,1)S(1)} %get-tuple-element.46), channel_id=1, source_target_pairs={{0,1},{1,0},{2,3},{3,2},{4,5},{5,4},{6,7},{7,6},{8,9},{9,8},{10,11... | collective-permute-start | bytes 110600 | tf_op jit(solution)/shard_map/ppermute | solution.py:20
  65.3 5.3 %collective-permute-start.18 = (bf16[16,1152]{1,0:T(8,128)(2,1)S(1)}, bf16[16,1152]{1,0:T(8,128)(2,1)S(1)}, u32[]{:S(2)}, u32[]{:S(2)}) collective-permute-start(bf16[16,1152]{1,0:T(8,128)(2,1)S(1)} %get-tuple-element.47), channel_id=1, source_target_pairs={{0,2},{1,3},{2,0},{3,1},{4,6},{5,7},{6,4},{7,5},{8,10},{9,11},{10,... | collective-permute-start | bytes 110600 | tf_op jit(solution)/shard_map/ppermute | solution.py:20
  68.2 5.8 %collective-permute-start.19 = (bf16[16,1152]{1,0:T(8,128)(2,1)S(1)}, bf16[16,1152]{1,0:T(8,128)(2,1)S(1)}, u32[]{:S(2)}, u32[]{:S(2)}) collective-permute-start(bf16[16,1152]{1,0:T(8,128)(2,1)S(1)} %get-tuple-element.48), channel_id=1, source_target_pairs={{0,3},{1,2},{2,1},{3,0},{4,7},{5,6},{6,5},{7,4},{8,11},{9,10},{10,... | collective-permute-start | bytes 110600 | tf_op jit(solution)/shard_map/ppermute | solution.py:20
  (6 other events, 32.9 us)

commit v4 on v3

--- a/solution.py
+++ b/solution.py
@@ -3,7 +3,6 @@
 
 import jax
 import jax.numpy as jnp
-import numpy as np
 from jax import lax
 from jax.experimental import pallas as pl
 from jax.experimental.pallas import tpu as pltpu
@@ -44,6 +43,7 @@
 SMEM = pl.BlockSpec(memory_space=pltpu.SMEM)
 HBM = pl.BlockSpec(memory_space=pltpu.HBM)
 PIECES = 3
+ATTEND_MIB = 44
 
 
 def pieces_of(value):
@@ -66,68 +66,25 @@
     return [groups for groups in (order[:1], order[1:-1], order[-1:] if order[1:] else []) if groups]
 
 
-def attend_kernel(
-    groups, share, per_copy, row_cuts, length_ref, freq_hbm, pos_hbm, q_hbm, k_hbm, v_hbm, *refs
-):
-    count = len(groups)
-    outs, stats = refs[:count], refs[count:-10]
-    k_buf, v_buf, q_buf, freq_ref, pos_ref, k_sem, v_sem, q_sem, cos_ref, sin_ref = refs[-10:]
-    rows = q_hbm.shape[0]
-    keys = k_hbm.shape[0]
-    t = lax.axis_index("tm")
-    own = t // row_cuts
-    width = per_copy * HD
-    small = [
-        pltpu.make_async_copy(freq_hbm, freq_ref, q_sem.at[count]),
-        pltpu.make_async_copy(pos_hbm, pos_ref, q_sem.at[count + 1]),
-    ]
-    for copy in small:
-        copy.start()
-    copies, wanted = [], []
-    for g, a in enumerate(groups):
-        first = pl.multiple_of((own ^ a) * share * HD, HD)
-        wanted.append(
-            pltpu.make_async_copy(
-                q_hbm.at[:, pl.ds(first, share * HD)], q_buf.at[g], q_sem.at[g]
-            )
-        )
-        wanted[g].start()
-        for part in range(share // per_copy):
-            slot = len(copies)
-            column = pl.multiple_of(((own ^ a) * share + part * per_copy) * HD, HD)
-            pair = [
-                pltpu.make_async_copy(hbm.at[:, pl.ds(column, width)], buf.at[slot], sem.at[slot])
-                for hbm, buf, sem in ((k_hbm, k_buf, k_sem), (v_hbm, v_buf, v_sem))
-            ]
-            for copy in pair:
-                copy.start()
-            copies.append((g, part, pair))
-    for copy in small:
-        copy.wait()
-
+def attend_heads(groups, share, per_copy, valid, q_of, k_of, v_of, cos_ref, sin_ref, outs, stats):
+    rows = cos_ref.shape[0]
     even = lax.broadcasted_iota(jnp.int32, (rows, HD), 1) % 2 == 0
-    place = jnp.broadcast_to(pos_ref[...].astype(jnp.float32), (HD, rows)).T
-    angles = place * freq_ref[...]
-    cos_ref[...] = jnp.cos(angles)
-    sine = jnp.sin(angles)
-    sin_ref[...] = jnp.where(even, -sine, sine)
     lane = lax.broadcasted_iota(jnp.int32, (rows, LANES), 1)
-    valid = lax.broadcasted_iota(jnp.int32, (1, keys), 1) < length_ref[0] - t * keys
     scale = 1.0 / math.sqrt(HD)
     held = jnp.zeros((rows, LANES), jnp.float32)
-    for slot, (g, part, pair) in enumerate(copies):
-        for copy in ([wanted[g]] if part == 0 else []) + pair:
-            copy.wait()
+    parts = share // per_copy
+    for slot in range(len(groups) * parts):
+        g, part = divmod(slot, parts)
         for i in range(per_copy):
             head = part * per_copy + i
             at = slice(i * HD, (i + 1) * HD)
             to = slice(head * HD, (head + 1) * HD)
-            wide = q_buf[g, :, to].astype(jnp.float32)
+            wide = q_of(g, to).astype(jnp.float32)
             partner = jnp.where(even, pltpu.roll(wide, HD - 1, 1), pltpu.roll(wide, 1, 1))
             rotated = (wide * cos_ref[...] + partner * sin_ref[...]).astype(jnp.bfloat16)
             scores = lax.dot_general(
                 rotated,
-                k_buf[slot, :, at],
+                k_of(slot, at),
                 (((1,), (1,)), ((), ())),
                 preferred_element_type=jnp.float32,
             )
@@ -136,14 +93,12 @@
             weights = jnp.exp((scores - block_max) * scale)
             block_total = jnp.sum(weights, axis=1, keepdims=True)
             block_out = jnp.dot(
-                weights.astype(jnp.bfloat16),
-                v_buf[slot, :, at],
-                preferred_element_type=jnp.float32,
+                weights.astype(jnp.bfloat16), v_of(slot, at), preferred_element_type=jnp.float32
             )
             outs[g][:rows, to] = block_out.astype(jnp.bfloat16)
             held = jnp.where(lane == head, block_max * scale, held)
             held = jnp.where(lane == share + head, block_total, held)
-        if part == share // per_copy - 1:
+        if part == parts - 1:
             flat = held.T
             if stats:
                 stats[g][...] = flat[: 2 * share]
@@ -153,45 +108,177 @@
                     outs[g][rows:, p * rows : (p + 1) * rows] = piece
 
 
-def attend(queries, keys, values, positions, cache_length, groups, share, row_cuts):
+def valid_keys(length_ref, keys):
+    return (
+        lax.broadcasted_iota(jnp.int32, (1, keys), 1)
+        < length_ref[0] - lax.axis_index("tm") * keys
+    )
+
+
+def attend_kernel(calls, share, per_copy, row_cuts, joined, *refs):
+    length_ref, pos_ref, q_hbm, k_hbm, v_hbm = refs[:5]
+    groups = calls[0]
+    n = len(groups)
+    outs, refs = refs[5 : 5 + n], refs[5 + n :]
+    stats, refs = ([], refs) if joined else (refs[:n], refs[n:])
+    cos_ref, sin_ref, refs = refs[0], refs[1], refs[2:]
+    kept, refs = refs[: 3 * len(calls) - 3], refs[3 * len(calls) - 3 :]
+    q_buf, k_buf, v_buf, sem = refs
+    rows = q_hbm.shape[0]
+    keys = k_hbm.shape[0]
+    own = lax.axis_index("tm") // row_cuts
+    width = per_copy * HD
+    parts = share // per_copy
+    copies = []
+
+    def start(from_ref, to_ref):
+        copies.append(pltpu.make_async_copy(from_ref, to_ref, sem.at[len(copies)]))
+        copies[-1].start()
+        return copies[-1]
+
+    first_copies = []
+    for c, call in enumerate(calls):
+        to = (q_buf, k_buf, v_buf) if c == 0 else kept[3 * c - 3 : 3 * c]
+        for g, a in enumerate(call):
+            first = pl.multiple_of((own ^ a) * share * HD, HD)
+            wanted = [start(q_hbm.at[:, pl.ds(first, share * HD)], to[0].at[g])]
+            for part in range(parts):
+                slot = g * parts + part
+                column = pl.multiple_of(first + part * width, HD)
+                wanted += [
+                    start(hbm.at[:, pl.ds(column, width)], buf.at[slot])
+                    for hbm, buf in ((k_hbm, to[1]), (v_hbm, to[2]))
+                ]
+                if c == 0:
+                    first_copies.append(wanted)
+                    wanted = []
+    lane = lax.broadcasted_iota(jnp.int32, (8, HD), 1)
+    sublane = lax.broadcasted_iota(jnp.int32, (8, HD), 0)
+    pair = (lane - lane % 2).astype(jnp.float32)
+    frequencies = jnp.exp(pair * (-math.log(10000.0) / HD))
+    for r in range(0, rows, 8):
+        place = jnp.full((8, HD), pos_ref[r], jnp.int32)
+        for i in range(1, 8):
+            place = jnp.where(sublane == i, pos_ref[r + i], place)
+        angles = place.astype(jnp.float32) * frequencies
+        cos_ref[r : r + 8] = jnp.cos(angles)
+        sine = jnp.sin(angles)
+        sin_ref[r : r + 8] = jnp.where(lane % 2 == 0, -sine, sine)
+    done = set()
+
+    def near(buf):
+        def read(slot, at):
+            if slot not in done:
+                done.add(slot)
+                for copy in first_copies[slot]:
+                    copy.wait()
+            return buf[slot, :, at]
+
+        return read
+
+    def query(g, at):
+        if g * parts not in done:
+            done.add(g * parts)
+            for copy in first_copies[g * parts]:
+                copy.wait()
+        return q_buf[g, :, at]
+
+    attend_heads(
+        groups,
+        share,
+        per_copy,
+        valid_keys(length_ref, keys),
+        query,
+        near(k_buf),
+        near(v_buf),
+        cos_ref,
+        sin_ref,
+        outs,
+        stats,
+    )
+    for copy in copies[sum(len(wanted) for wanted in first_copies) :]:
+        copy.wait()
+
+
+def attend_near_kernel(groups, share, per_copy, joined, *refs):
+    length_ref, cos_ref, sin_ref, q_ref, k_ref, v_ref = refs[:6]
+    n = len(groups)
+    outs, stats = refs[6 : 6 + n], [] if joined else refs[6 + n :]
+    attend_heads(
+        groups,
+        share,
+        per_copy,
+        valid_keys(length_ref, k_ref.shape[1]),
+        lambda g, at: q_ref[g, :, at],
+        lambda slot, at: k_ref[slot, :, at],
+        lambda slot, at: v_ref[slot, :, at],
+        cos_ref,
+        sin_ref,
+        outs,
+        stats,
+    )
+
+
+def attend(queries, keys, values, positions, cache_length, calls, share, row_cuts):
     rows = queries.shape[0]
     key_count = keys.shape[0]
     per_copy = 2 if share % 2 == 0 else 1
-    n = len(groups)
-    slots = n * share // per_copy
     wide = share * HD
     joined = row_cuts == 1 and packed(rows, wide, share)
-    frequencies = np.exp(-math.log(10000.0) * 2.0 * (np.arange(HD) // 2) / HD)
-    buffer = pltpu.VMEM((slots, key_count, per_copy * HD), jnp.bfloat16)
-    out_shape = [jax.ShapeDtypeStruct((rows + 8 * joined, wide), jnp.bfloat16)] * n
-    if not joined:
-        out_shape = out_shape + [jax.ShapeDtypeStruct((2 * share, rows), jnp.float32)] * n
-    result = pl.pallas_call(
-        functools.partial(attend_kernel, groups, share, per_copy, row_cuts),
-        in_specs=[SMEM, HBM, HBM, HBM, HBM, HBM],
-        out_specs=[VMEM] * len(out_shape),
-        out_shape=out_shape,
-        scratch_shapes=[
-            buffer,
-            buffer,
-            pltpu.VMEM((n, rows, wide), jnp.bfloat16),
-            pltpu.VMEM((1, HD), jnp.float32),
-            pltpu.VMEM((1, rows), jnp.int32),
-            pltpu.SemaphoreType.DMA((slots,)),
-            pltpu.SemaphoreType.DMA((slots,)),
-            pltpu.SemaphoreType.DMA((n + 2,)),
-            pltpu.VMEM((rows, HD), jnp.float32),
-            pltpu.VMEM((rows, HD), jnp.float32),
-        ],
-        cost_estimate=pl.CostEstimate(
+    table = jax.ShapeDtypeStruct((rows, HD), jnp.float32)
+
+    def blocks(n):
+        shapes = [jax.ShapeDtypeStruct((rows + 8 * joined, wide), jnp.bfloat16)] * n
+        if not joined:
+            shapes = shapes + [jax.ShapeDtypeStruct((2 * share, rows), jnp.float32)] * n
+        return shapes
+
+    def near(n):
+        cache = (n * share // per_copy, key_count, per_copy * HD)
+        return [((n, rows, wide), jnp.bfloat16), (cache, jnp.bfloat16), (cache, jnp.bfloat16)]
+
+    def price(n):
+        return pl.CostEstimate(
             flops=4 * n * share * rows * key_count * HD,
             bytes_accessed=4 * n * share * key_count * HD,
             transcendentals=n * share * rows * key_count,
-        ),
-        compiler_params=mib(57 if groups[-1] == 0 else 60),
+        )
+
+    def found(result, n):
+        return list(zip(result[:n], [None] * n if joined else result[n : 2 * n]))
+
+    n = len(calls[0])
+    out_shape = blocks(n) + [table] * 2
+    for call in calls[1:]:
+        out_shape = out_shape + [jax.ShapeDtypeStruct(*entry) for entry in near(len(call))]
+    count = sum(len(call) for call in calls) * (1 + 2 * share // per_copy)
+    result = pl.pallas_call(
+        functools.partial(attend_kernel, calls, share, per_copy, row_cuts, joined),
+        in_specs=[SMEM] * 2 + [HBM] * 3,
+        out_specs=[VMEM] * len(out_shape),
+        out_shape=out_shape,
+        scratch_shapes=[pltpu.VMEM(*entry) for entry in near(n)]
+        + [pltpu.SemaphoreType.DMA((count,))],
+        cost_estimate=price(n),
+        compiler_params=mib(ATTEND_MIB),
         name="attend",
-    )(cache_length, frequencies.astype(np.float32)[None], positions[None], queries, keys, values)
-    return list(zip(result[:n], result[n:] if not joined else [None] * n))
+    )(cache_length, positions, queries, keys, values)
+    skip = len(blocks(n))
+    tables, kept = result[skip : skip + 2], result[skip + 2 :]
+    blocks_of = [found(result, n)]
+    for c, call in enumerate(calls[1:]):
+        n = len(call)
+        result = pl.pallas_call(
+            functools.partial(attend_near_kernel, call, share, per_copy, joined),
+            in_specs=[SMEM] + [VMEM] * 5,
+            out_specs=[VMEM] * len(blocks(n)),
+            out_shape=blocks(n),
+            cost_estimate=price(n),
+            compiler_params=mib(16),
+            name="attend_near",
+        )(cache_length, *tables, *kept[3 * c : 3 * c + 3])
+        blocks_of.append(found(result, n))
+    return blocks_of
 
 
 def merge_kernel(count, share, *refs):
@@ -560,10 +647,11 @@
 
     order = list(range(head_cuts))[::-1]
     outs, stats = [None] * n_tm, [None] * n_tm
-    for groups in calls_of(order):
-        blocks = attend(
-            queries, cache_keys, cache_values, positions, cache_length, groups, share, row_cuts
-        )
+    calls = calls_of(order)
+    found = attend(
+        queries, cache_keys, cache_values, positions, cache_length, calls, share, row_cuts
+    )
+    for groups, blocks in zip(calls, found):
         for a, (out, stat) in zip(groups, blocks):
             for b in range(row_cuts):
                 s = a * row_cuts + b

time: 75 us -> 77.3 us (1.031)
  waiting for transfers between devices: 19.6 us -> 28.6 us
  Pallas kernels: 23.2 us -> 18.9 us
  local copies, waits for them, and re-layouts: 4.34 us -> 1.91 us
    ppermute x20, waiting for transfers between devices: 19.6 us -> 28.6 us  [swap(): return lax.ppermute(values, axis, [(i, i ^ distance) for i in range(size)])]
    pallas_call x3, Pallas kernels: 13.9 us -> 9.33 us  [the longest x2 4.81 us: attend(): pl.pallas_call(functools.partial(attend_near_kernel, call, share, per_cop...]
    unnamed x20 -> x24, local copies, waits for them, and re-layouts: 4.34 us -> 1.91 us
  transfers between devices with their start and end apart: 20 -> 20, of which waited for: 9 -> 10; matrix products, arithmetic and copies ran while one was open for 0% -> 0% of each run, Pallas kernels for 24% -> 18%
where the time goes in v4:
time: 77.3 us; the launch traced here: 77.2 us
  waiting for transfers between devices  28.6 us (37%)
  starting transfers between devices  26.4 us (34%)
  Pallas kernels  18.9 us (24%)
  local copies, waits for them, and re-layouts  1.91 us (2%)
  between operations  1.01 us (1%)
    ppermute x20, waiting for transfers between devices, swap(): return lax.ppermute(values, axis, [(i, i ^ distance) for i in range(size)])  28.6 us
    ppermute x20, starting transfers between devices, swap(): return lax.ppermute(values, axis, [(i, i ^ distance) for i in range(size)])  26.4 us
    pallas_call x2, Pallas kernels, attend(): pl.pallas_call(functools.partial(attend_near_kernel, call, share, per_cop...  4.81 us
    pallas_call x1, Pallas kernels, attend(): pl.pallas_call(functools.partial(attend_kernel, calls, share, per_copy, r...  4.52 us
    pallas_call x1, Pallas kernels, sweep_all(): pl.pallas_call(functools.partial(sweep_kernel, (n_tm, time_each, rows, mo...  4.26 us
    unnamed x24, local copies, waits for them, and re-layouts  1.91 us
    pallas_call x1, Pallas kernels, project(): pl.pallas_call(functools.partial(project_kernel, cuts, later, row_cuts),...  1.6 us
  transfers between devices with their start and end apart: 20, of which 10 were waited for; matrix products, arithmetic and copies ran while one was open for 0% of the time, Pallas kernels for 18%

profile of v4, /device:TPU:0, one launch (start us, length us, event | category | flops | bytes accessed | tf_op | source)
XLA Modules:
  0.0 77.2 jit_solution(9735536821643826742)
XLA Ops:
  0.0 3.0 %collective-permute-start.9 = (bf16[2048,384]{1,0:T(8,128)(2,1)}, bf16[2048,384]{1,0:T(8,128)(2,1)S(1)}, u32[]{:S(2)}, u32[]{:S(2)}) collective-permute-start(bf16[2048,384]{1,0:T(8,128)(2,1)} %refs_1_.3), channel_id=1, source_target_pairs={{0,8},{4,12},{8,0},{12,4},{1,9},{5,13},{9,1},{13,5},{2,10},{6,14},... | collective-permute-start | bytes 4718600 | tf_op jit(solution)/shard_map/ppermute | solution.py:19
  3.8 1.2 %copy-done.4 = bf16[128,2048]{1,0:T(8,128)(2,1)S(1)} copy-done((bf16[128,2048]{1,0:T(8,128)(2,1)S(1)}, bf16[128,2048]{1,0:T(8,128)(2,1)}, u32[]{:S(2)}) %copy-start.4) | copy-done | bytes 524312
  5.6 4.5 %attend.1 = (bf16[136,512]{1,0:T(8,128)(2,1)S(1)}, f32[128,128]{1,0:T(8,128)S(1)}, f32[128,128]{1,0:T(8,128)S(1)}, bf16[2,128,512]{2,1,0:T(8,128)(2,1)S(1)}, bf1...) custom-call(s32[1]{0:T(128)S(6)} %copy.15.refs_0_, ...), custom_call_target="tpu_custom_call" | custom-call | flops 268435456 | bytes 2097152 | tf_op jit(solution)/shard_map/attend/pallas_call | solution.py:255
  10.2 3.2 %attend_near.3 = (bf16[136,512]{1,0:T(8,128)(2,1)S(1)}, bf16[136,512]{1,0:T(8,128)(2,1)S(1)}) custom-call(s32[1]{0:T(128)S(6)} %copy.15.refs_0_, f32[128,128]{1,0:T(8,128)S(1)} %get-tuple-element.40.refs_1_, f32[128,128]{1,0:T(8,128)S(1)} %get-tuple-element.41.refs_2_, bf16[2,128,512]{2,1,0:T(8,128)(2,1)S(1)} %get-tuple-element.45.refs_3_, ...), custom_call_target="tpu_custom_call" | custom-call | flops 536870912 | bytes 4194304 | tf_op jit(solution)/shard_map/attend_near/pallas_call | solution.py:271
  13.3 1.6 %collective-permute-start.3 = (bf16[136,512]{1,0:T(8,128)(2,1)S(1)}, bf16[136,512]{1,0:T(8,128)(2,1)S(1)}, u32[]{:S(2)}, u32[]{:S(2)}) collective-permute-start(bf16[136,512]{1,0:T(8,128)(2,1)S(1)} %get-tuple-element.48), channel_id=1, source_target_pairs={{0,1},{1,0},{2,3},{3,2},{4,5},{5,4},{6,7},{7,6},{8,9},{9,8},{10,11... | collective-permute-start | bytes 417800 | tf_op jit(solution)/shard_map/ppermute | solution.py:19
  15.0 2.6 %collective-permute-start.4 = (bf16[136,512]{1,0:T(8,128)(2,1)S(1)}, bf16[136,512]{1,0:T(8,128)(2,1)S(1)}, u32[]{:S(2)}, u32[]{:S(2)}) collective-permute-start(bf16[136,512]{1,0:T(8,128)(2,1)S(1)} %get-tuple-element.49), channel_id=1, source_target_pairs={{0,2},{1,3},{2,0},{3,1},{4,6},{5,7},{6,4},{7,5},{8,10},{9,11},{10,... | collective-permute-start | bytes 417800 | tf_op jit(solution)/shard_map/ppermute | solution.py:19
  17.8 1.6 %attend_near.2.refs_0_ = bf16[136,512]{1,0:T(8,128)(2,1)S(1)} custom-call(s32[1]{0:T(128)S(6)} %copy.15.refs_0_, f32[128,128]{1,0:T(8,128)S(1)} %get-tuple-element.40.refs_1_, f32[128,128]{1,0:T(8,128)S(1)} %get-tuple-element.41.refs_2_, bf16[1,128,512]{2,1,0:T(8,128)(2,1)S(1)} %get-tuple-element.42.refs_3_, ...), custom_call_target="tpu_custom_call" | custom-call | flops 268435456 | bytes 2097152 | tf_op jit(solution)/shard_map/attend_near/pallas_call | solution.py:271
  20.2 8.0 %collective-permute-done.4.refs_2_ = bf16[136,512]{1,0:T(8,128)(2,1)S(1)} collective-permute-done((bf16[136,512]{1,0:T(8,128)(2,1)S(1)}, bf16[136,512]{1,0:T(8,128)(2,1)S(1)}, u32[]{:S(2)}, u32[]{:S(2)}) %collective-permute-start.4) | collective-permute-done | bytes 139296 | tf_op jit(solution)/shard_map/ppermute | solution.py:19
  28.7 2.1 %collective-permute-start.6 = (bf16[128,512]{1,0:T(8,128)(2,1)S(1)}, bf16[128,512]{1,0:T(8,128)(2,1)S(1)}, u32[]{:S(2)}, u32[]{:S(2)}) collective-permute-start(bf16[128,512]{1,0:T(8,128)(2,1)S(1)} %merge.1.refs_0_), channel_id=1, source_target_pairs={{0,1},{1,0},{2,3},{3,2},{4,5},{5,4},{6,7},{7,6},{8,9},{9,8},{10,11... | collective-permute-start | bytes 393224 | tf_op jit(solution)/shard_map/ppermute | solution.py:19
  31.9 1.4 %collective-permute-start.8 = (bf16[128,512]{1,0:T(8,128)(2,1)S(1)}, bf16[128,512]{1,0:T(8,128)(2,1)S(1)}, u32[]{:S(2)}, u32[]{:S(2)}) collective-permute-start(bf16[128,512]{1,0:T(8,128)(2,1)S(1)} %merge.1.refs_0_), channel_id=1, source_target_pairs={{0,3},{1,2},{2,1},{3,0},{4,7},{5,6},{6,5},{7,4},{8,11},{9,10},{10,... | collective-permute-start | bytes 393224 | tf_op jit(solution)/shard_map/ppermute | solution.py:19
  33.3 1.9 %collective-permute-done.6.refs_1_ = bf16[128,512]{1,0:T(8,128)(2,1)S(1)} collective-permute-done((bf16[128,512]{1,0:T(8,128)(2,1)S(1)}, bf16[128,512]{1,0:T(8,128)(2,1)S(1)}, u32[]{:S(2)}, u32[]{:S(2)}) %collective-permute-start.6) | collective-permute-done | bytes 131104 | tf_op jit(solution)/shard_map/ppermute | solution.py:19
  35.2 1.6 %project.1 = (f32[128,2048]{1,0:T(8,128)S(1)}, bf16[2,512,2048]{2,1,0:T(8,128)(2,1)S(1)}) custom-call(bf16[128,512]{1,0:T(8,128)(2,1)S(1)} %merge.1.refs_0_, bf16[128,512]{1,0:T(8,128)(2,1)S(1)} %collective-permute-done.6.refs_1_, bf16[2048,2048]{1,0:T(8,128)(2,1)S(1)} %bitcast.5), custom_call_target="tpu_custom_call" | custom-call | flops 536870912 | bytes 8388608 | tf_op jit(solution)/shard_map/project/pallas_call | solution.py:347
  36.9 5.7 %collective-permute-done.7.refs_0_ = bf16[128,512]{1,0:T(8,128)(2,1)S(1)} collective-permute-done((bf16[128,512]{1,0:T(8,128)(2,1)S(1)}, bf16[128,512]{1,0:T(8,128)(2,1)S(1)}, u32[]{:S(2)}, u32[]{:S(2)}) %collective-permute-start.7) | collective-permute-done | bytes 131104 | tf_op jit(solution)/shard_map/ppermute | solution.py:19
  43.9 2.0 %collective-permute-start = (bf16[16,1152]{1,0:T(8,128)(2,1)S(1)}, bf16[16,1152]{1,0:T(8,128)(2,1)S(1)}, u32[]{:S(2)}, u32[]{:S(2)}) collective-permute-start(bf16[16,1152]{1,0:T(8,128)(2,1)S(1)} %get-tuple-element.37), channel_id=1, source_target_pairs={{0,1},{1,0},{2,3},{3,2},{4,5},{5,4},{6,7},{7,6},{8,9},{9,8},{10,11... | collective-permute-start | bytes 110600 | tf_op jit(solution)/shard_map/ppermute | solution.py:19
  45.9 1.2 %collective-permute-start.1 = (bf16[16,1152]{1,0:T(8,128)(2,1)S(1)}, bf16[16,1152]{1,0:T(8,128)(2,1)S(1)}, u32[]{:S(2)}, u32[]{:S(2)}) collective-permute-start(bf16[16,1152]{1,0:T(8,128)(2,1)S(1)} %get-tuple-element.38), channel_id=1, source_target_pairs={{0,2},{1,3},{2,0},{3,1},{4,6},{5,7},{6,4},{7,5},{8,10},{9,11},{10,... | collective-permute-start | bytes 110600 | tf_op jit(solution)/shard_map/ppermute | solution.py:19
  49.4 1.4 %collective-permute-start.2 = (bf16[16,1152]{1,0:T(8,128)(2,1)S(1)}, bf16[16,1152]{1,0:T(8,128)(2,1)S(1)}, u32[]{:S(2)}, u32[]{:S(2)}) collective-permute-start(bf16[16,1152]{1,0:T(8,128)(2,1)S(1)} %get-tuple-element.39), channel_id=1, source_target_pairs={{0,3},{1,2},{2,1},{3,0},{4,7},{5,6},{6,5},{7,4},{8,11},{9,10},{10,... | collective-permute-start | bytes 110600 | tf_op jit(solution)/shard_map/ppermute | solution.py:19
  50.8 3.6 %collective-permute-done.11.refs_0_ = bf16[32,2048]{1,0:T(8,128)(2,1)S(1)} collective-permute-done((bf16[32,2048]{1,0:T(8,128)(2,1)S(1)}, bf16[32,2048]{1,0:T(8,128)(2,1)S(1)}, u32[]{:S(2)}, u32[]{:S(2)}) %collective-permute-start.11) | collective-permute-done | bytes 131104 | tf_op jit(solution)/shard_map/ppermute | solution.py:19
  55.6 2.0 %collective-permute-start.14 = (bf16[8,1664]{1,0:T(8,128)(2,1)S(1)}, bf16[8,1664]{1,0:T(8,128)(2,1)S(1)}, u32[]{:S(2)}, u32[]{:S(2)}) collective-permute-start(bf16[8,1664]{1,0:T(8,128)(2,1)S(1)} %get-tuple-element.60), channel_id=1, source_target_pairs={{0,1},{1,0},{2,3},{3,2},{4,5},{5,4},{6,7},{7,6},{8,9},{9,8},{10,11... | collective-permute-start | bytes 79880 | tf_op jit(solution)/shard_map/ppermute | solution.py:19
  57.6 2.4 %collective-permute-start.16 = (bf16[8,1664]{1,0:T(8,128)(2,1)S(1)}, bf16[8,1664]{1,0:T(8,128)(2,1)S(1)}, u32[]{:S(2)}, u32[]{:S(2)}) collective-permute-start(bf16[8,1664]{1,0:T(8,128)(2,1)S(1)} %get-tuple-element.62), channel_id=1, source_target_pairs={{0,3},{1,2},{2,1},{3,0},{4,7},{5,6},{6,5},{7,4},{8,11},{9,10},{10,... | collective-permute-start | bytes 79880 | tf_op jit(solution)/shard_map/ppermute | solution.py:19
  60.1 2.2 %collective-permute-done.15.refs_6_ = bf16[8,1664]{1,0:T(8,128)(2,1)S(1)} collective-permute-done((bf16[8,1664]{1,0:T(8,128)(2,1)S(1)}, bf16[8,1664]{1,0:T(8,128)(2,1)S(1)}, u32[]{:S(2)}, u32[]{:S(2)}) %collective-permute-start.15) | collective-permute-done | bytes 26656 | tf_op jit(solution)/shard_map/ppermute | solution.py:19
  63.3 4.3 %sweeps.1 = (bf16[16,1152]{1,0:T(8,128)(2,1)S(1)}, bf16[16,1152]{1,0:T(8,128)(2,1)S(1)}, bf16[16,1152]{1,0:T(8,128)(2,1)S(1)}, bf16[16,1152]{1,0:T(8,128)(2,1)S(1)}) custom-call(f32[16]{0:T(128)S(1)} %pad_maximum_fusion.1.steps, f32[4,8,1152]{2,1,0:T(8,128)S(1)} %bitcast.6, f32[8,1536]{1,0:T(8,128)S(1)} %pad_maximum_fusion.embed_ref, ...), custom_call_target="tpu_custom_call" | custom-call | flops 1132462080 | bytes 7077888 | tf_op jit(solution)/shard_map/sweeps/pallas_call | solution.py:541
  67.6 3.0 %collective-permute-start.18 = (bf16[16,1152]{1,0:T(8,128)(2,1)S(1)}, bf16[16,1152]{1,0:T(8,128)(2,1)S(1)}, u32[]{:S(2)}, u32[]{:S(2)}) collective-permute-start(bf16[16,1152]{1,0:T(8,128)(2,1)S(1)} %get-tuple-element.65), channel_id=1, source_target_pairs={{0,2},{1,3},{2,0},{3,1},{4,6},{5,7},{6,4},{7,5},{8,10},{9,11},{10,... | collective-permute-start | bytes 110600 | tf_op jit(solution)/shard_map/ppermute | solution.py:19
  70.6 1.4 %collective-permute-start.19 = (bf16[16,1152]{1,0:T(8,128)(2,1)S(1)}, bf16[16,1152]{1,0:T(8,128)(2,1)S(1)}, u32[]{:S(2)}, u32[]{:S(2)}) collective-permute-start(bf16[16,1152]{1,0:T(8,128)(2,1)S(1)} %get-tuple-element.66), channel_id=1, source_target_pairs={{0,3},{1,2},{2,1},{3,0},{4,7},{5,6},{6,5},{7,4},{8,11},{9,10},{10,... | collective-permute-start | bytes 110600 | tf_op jit(solution)/shard_map/ppermute | solution.py:19
  72.9 3.4 %collective-permute-done.19.refs_3_ = bf16[16,1152]{1,0:T(8,128)(2,1)S(1)} collective-permute-done((bf16[16,1152]{1,0:T(8,128)(2,1)S(1)}, bf16[16,1152]{1,0:T(8,128)(2,1)S(1)}, u32[]{:S(2)}, u32[]{:S(2)}) %collective-permute-start.19) | collective-permute-done | bytes 36896 | tf_op jit(solution)/shard_map/ppermute | solution.py:19
  (58 shorter events, 10.9 us)
Async XLA Ops:
  0.0 43.4 %collective-permute-start.9 = (bf16[2048,384]{1,0:T(8,128)(2,1)}, bf16[2048,384]{1,0:T(8,128)(2,1)S(1)}, u32[]{:S(2)}, u32[]{:S(2)}) collective-permute-start(bf16[2048,384]{1,0:T(8,128)(2,1)} %refs_1_.3), channel_id=1, source_target_pairs={{0,8},{4,12},{8,0},{12,4},{1,9},{5,13},{9,1},{13,5},{2,10},{6,14},... | collective-permute-start | bytes 4718600 | tf_op jit(solution)/shard_map/ppermute | solution.py:19
  3.0 32.2 %slice-start = ((s8[8388608]{0:T(1024)(128)(4,1)}), s8[4194304]{0:T(1024)(128)(4,1)S(1)}, s32[]{:S(2)}) async-start(s8[8388608]{0:T(1024)(128)(4,1)} %bitcast.4), calls=%async_computation | async-start | bytes 8388608
  5.6 29.6 %slice-start.1 = ((s8[8388608]{0:T(1024)(128)(4,1)}), s8[4194304]{0:T(1024)(128)(4,1)S(1)}, s32[]{:S(2)}) async-start(s8[8388608]{0:T(1024)(128)(4,1)} %bitcast.4), calls=%async_computation.1 | async-start | bytes 8388608
  10.2 23.2 %copy-start.2 = (bf16[2048,384]{1,0:T(8,128)(2,1)S(1)}, bf16[2048,384]{1,0:T(8,128)(2,1)}, u32[]{:S(2)}) copy-start(bf16[2048,384]{1,0:T(8,128)(2,1)} %refs_1_.3) | copy-start | bytes 4718596
  13.3 6.8 %collective-permute-start.3 = (bf16[136,512]{1,0:T(8,128)(2,1)S(1)}, bf16[136,512]{1,0:T(8,128)(2,1)S(1)}, u32[]{:S(2)}, u32[]{:S(2)}) collective-permute-start(bf16[136,512]{1,0:T(8,128)(2,1)S(1)} %get-tuple-element.48), channel_id=1, source_target_pairs={{0,1},{1,0},{2,3},{3,2},{4,5},{5,4},{6,7},{7,6},{8,9},{9,8},{10,11... | collective-permute-start | bytes 417800 | tf_op jit(solution)/shard_map/ppermute | solution.py:19
  15.0 13.2 %collective-permute-start.4 = (bf16[136,512]{1,0:T(8,128)(2,1)S(1)}, bf16[136,512]{1,0:T(8,128)(2,1)S(1)}, u32[]{:S(2)}, u32[]{:S(2)}) collective-permute-start(bf16[136,512]{1,0:T(8,128)(2,1)S(1)} %get-tuple-element.49), channel_id=1, source_target_pairs={{0,2},{1,3},{2,0},{3,1},{4,6},{5,7},{6,4},{7,5},{8,10},{9,11},{10,... | collective-permute-start | bytes 417800 | tf_op jit(solution)/shard_map/ppermute | solution.py:19
  17.5 10.7 %collective-permute-start.5 = (bf16[136,512]{1,0:T(8,128)(2,1)S(1)}, bf16[136,512]{1,0:T(8,128)(2,1)S(1)}, u32[]{:S(2)}, u32[]{:S(2)}) collective-permute-start(bf16[136,512]{1,0:T(8,128)(2,1)S(1)} %get-tuple-element.50), channel_id=1, source_target_pairs={{0,3},{1,2},{2,1},{3,0},{4,7},{5,6},{6,5},{7,4},{8,11},{9,10},{10,... | collective-permute-start | bytes 417800 | tf_op jit(solution)/shard_map/ppermute | solution.py:19
  28.7 6.5 %collective-permute-start.6 = (bf16[128,512]{1,0:T(8,128)(2,1)S(1)}, bf16[128,512]{1,0:T(8,128)(2,1)S(1)}, u32[]{:S(2)}, u32[]{:S(2)}) collective-permute-start(bf16[128,512]{1,0:T(8,128)(2,1)S(1)} %merge.1.refs_0_), channel_id=1, source_target_pairs={{0,1},{1,0},{2,3},{3,2},{4,5},{5,4},{6,7},{7,6},{8,9},{9,8},{10,11... | collective-permute-start | bytes 393224 | tf_op jit(solution)/shard_map/ppermute | solution.py:19
  30.8 11.7 %collective-permute-start.7 = (bf16[128,512]{1,0:T(8,128)(2,1)S(1)}, bf16[128,512]{1,0:T(8,128)(2,1)S(1)}, u32[]{:S(2)}, u32[]{:S(2)}) collective-permute-start(bf16[128,512]{1,0:T(8,128)(2,1)S(1)} %merge.1.refs_0_), channel_id=1, source_target_pairs={{0,2},{1,3},{2,0},{3,1},{4,6},{5,7},{6,4},{7,5},{8,10},{9,11},{10,... | collective-permute-start | bytes 393224 | tf_op jit(solution)/shard_map/ppermute | solution.py:19
  31.9 10.6 %collective-permute-start.8 = (bf16[128,512]{1,0:T(8,128)(2,1)S(1)}, bf16[128,512]{1,0:T(8,128)(2,1)S(1)}, u32[]{:S(2)}, u32[]{:S(2)}) collective-permute-start(bf16[128,512]{1,0:T(8,128)(2,1)S(1)} %merge.1.refs_0_), channel_id=1, source_target_pairs={{0,3},{1,2},{2,1},{3,0},{4,7},{5,6},{6,5},{7,4},{8,11},{9,10},{10,... | collective-permute-start | bytes 393224 | tf_op jit(solution)/shard_map/ppermute | solution.py:19
  33.3 16.1 %collective-permute-start.12 = (bf16[2048,384]{1,0:T(8,128)(2,1)S(1)}, bf16[2048,384]{1,0:T(8,128)(2,1)S(1)}, u32[]{:S(2)}, u32[]{:S(2)}) collective-permute-start(bf16[2048,384]{1,0:T(8,128)(2,1)S(1)} %copy-done.2), channel_id=1, source_target_pairs={{0,4},{4,0},{8,12},{12,8},{1,5},{5,1},{9,13},{13,9},{2,6},{6,2},{1... | collective-permute-start | bytes 4718600 | tf_op jit(solution)/shard_map/ppermute | solution.py:19
  36.8 17.6 %copy-start.5 = (bf16[128,2048]{1,0:T(8,128)(2,1)S(1)}, bf16[128,2048]{1,0:T(8,128)(2,1)}, u32[]{:S(2)}) copy-start(bf16[128,2048]{1,0:T(8,128)(2,1)} %param.17) | copy-start | bytes 1572868
  43.4 11.0 %collective-permute-start.13 = (bf16[2048,384]{1,0:T(8,128)(2,1)S(1)}, bf16[2048,384]{1,0:T(8,128)(2,1)S(1)}, u32[]{:S(2)}, u32[]{:S(2)}) collective-permute-start(bf16[2048,384]{1,0:T(8,128)(2,1)S(1)} %collective-permute-done.9.refs_3_), channel_id=1, source_target_pairs={{0,4},{4,0},{8,12},{12,8},{1,5},{5,1},{9,13},{13,9},{2,6},{6,2},{1... | collective-permute-start | bytes 4718600 | tf_op jit(solution)/shard_map/ppermute | solution.py:19
  43.9 13.7 %collective-permute-start = (bf16[16,1152]{1,0:T(8,128)(2,1)S(1)}, bf16[16,1152]{1,0:T(8,128)(2,1)S(1)}, u32[]{:S(2)}, u32[]{:S(2)}) collective-permute-start(bf16[16,1152]{1,0:T(8,128)(2,1)S(1)} %get-tuple-element.37), channel_id=1, source_target_pairs={{0,1},{1,0},{2,3},{3,2},{4,5},{5,4},{6,7},{7,6},{8,9},{9,8},{10,11... | collective-permute-start | bytes 110600 | tf_op jit(solution)/shard_map/ppermute | solution.py:19
  45.9 14.2 %collective-permute-start.1 = (bf16[16,1152]{1,0:T(8,128)(2,1)S(1)}, bf16[16,1152]{1,0:T(8,128)(2,1)S(1)}, u32[]{:S(2)}, u32[]{:S(2)}) collective-permute-start(bf16[16,1152]{1,0:T(8,128)(2,1)S(1)} %get-tuple-element.38), channel_id=1, source_target_pairs={{0,2},{1,3},{2,0},{3,1},{4,6},{5,7},{6,4},{7,5},{8,10},{9,11},{10,... | collective-permute-start | bytes 110600 | tf_op jit(solution)/shard_map/ppermute | solution.py:19
  47.2 1.5 %collective-permute-start.10 = (bf16[2,32,2048]{2,1,0:T(8,128)(2,1)S(1)}, bf16[2,32,2048]{2,1,0:T(8,128)(2,1)S(1)}, u32[]{:S(2)}, u32[]{:S(2)}) collective-permute-start(bf16[2,32,2048]{2,1,0:T(8,128)(2,1)S(1)} %get-tuple-element.55), channel_id=1, source_target_pairs={{0,4},{4,0},{8,12},{12,8},{1,5},{5,1},{9,13},{13,9},{2,6},{6,2},{1... | collective-permute-start | bytes 786440 | tf_op jit(solution)/shard_map/ppermute | solution.py:19
  48.8 5.7 %collective-permute-start.11 = (bf16[32,2048]{1,0:T(8,128)(2,1)S(1)}, bf16[32,2048]{1,0:T(8,128)(2,1)S(1)}, u32[]{:S(2)}, u32[]{:S(2)}) collective-permute-start(bf16[32,2048]{1,0:T(8,128)(2,1)S(1)} %get-tuple-element.57), channel_id=1, source_target_pairs={{0,8},{4,12},{8,0},{12,4},{1,9},{5,13},{9,1},{13,5},{2,10},{6,14},... | collective-permute-start | bytes 393224 | tf_op jit(solution)/shard_map/ppermute | solution.py:19
  49.4 10.7 %collective-permute-start.2 = (bf16[16,1152]{1,0:T(8,128)(2,1)S(1)}, bf16[16,1152]{1,0:T(8,128)(2,1)S(1)}, u32[]{:S(2)}, u32[]{:S(2)}) collective-permute-start(bf16[16,1152]{1,0:T(8,128)(2,1)S(1)} %get-tuple-element.39), channel_id=1, source_target_pairs={{0,3},{1,2},{2,1},{3,0},{4,7},{5,6},{6,5},{7,4},{8,11},{9,10},{10,... | collective-permute-start | bytes 110600 | tf_op jit(solution)/shard_map/ppermute | solution.py:19
  55.6 4.5 %collective-permute-start.14 = (bf16[8,1664]{1,0:T(8,128)(2,1)S(1)}, bf16[8,1664]{1,0:T(8,128)(2,1)S(1)}, u32[]{:S(2)}, u32[]{:S(2)}) collective-permute-start(bf16[8,1664]{1,0:T(8,128)(2,1)S(1)} %get-tuple-element.60), channel_id=1, source_target_pairs={{0,1},{1,0},{2,3},{3,2},{4,5},{5,4},{6,7},{7,6},{8,9},{9,8},{10,11... | collective-permute-start | bytes 79880 | tf_op jit(solution)/shard_map/ppermute | solution.py:19
  57.5 4.7 %collective-permute-start.15 = (bf16[8,1664]{1,0:T(8,128)(2,1)S(1)}, bf16[8,1664]{1,0:T(8,128)(2,1)S(1)}, u32[]{:S(2)}, u32[]{:S(2)}) collective-permute-start(bf16[8,1664]{1,0:T(8,128)(2,1)S(1)} %get-tuple-element.61), channel_id=1, source_target_pairs={{0,2},{1,3},{2,0},{3,1},{4,6},{5,7},{6,4},{7,5},{8,10},{9,11},{10,... | collective-permute-start | bytes 79880 | tf_op jit(solution)/shard_map/ppermute | solution.py:19
  57.6 5.6 %collective-permute-start.16 = (bf16[8,1664]{1,0:T(8,128)(2,1)S(1)}, bf16[8,1664]{1,0:T(8,128)(2,1)S(1)}, u32[]{:S(2)}, u32[]{:S(2)}) collective-permute-start(bf16[8,1664]{1,0:T(8,128)(2,1)S(1)} %get-tuple-element.62), channel_id=1, source_target_pairs={{0,3},{1,2},{2,1},{3,0},{4,7},{5,6},{6,5},{7,4},{8,11},{9,10},{10,... | collective-permute-start | bytes 79880 | tf_op jit(solution)/shard_map/ppermute | solution.py:19
  67.5 4.5 %collective-permute-start.17 = (bf16[16,1152]{1,0:T(8,128)(2,1)S(1)}, bf16[16,1152]{1,0:T(8,128)(2,1)S(1)}, u32[]{:S(2)}, u32[]{:S(2)}) collective-permute-start(bf16[16,1152]{1,0:T(8,128)(2,1)S(1)} %get-tuple-element.64), channel_id=1, source_target_pairs={{0,1},{1,0},{2,3},{3,2},{4,5},{5,4},{6,7},{7,6},{8,9},{9,8},{10,11... | collective-permute-start | bytes 110600 | tf_op jit(solution)/shard_map/ppermute | solution.py:19
  67.6 5.3 %collective-permute-start.18 = (bf16[16,1152]{1,0:T(8,128)(2,1)S(1)}, bf16[16,1152]{1,0:T(8,128)(2,1)S(1)}, u32[]{:S(2)}, u32[]{:S(2)}) collective-permute-start(bf16[16,1152]{1,0:T(8,128)(2,1)S(1)} %get-tuple-element.65), channel_id=1, source_target_pairs={{0,2},{1,3},{2,0},{3,1},{4,6},{5,7},{6,4},{7,5},{8,10},{9,11},{10,... | collective-permute-start | bytes 110600 | tf_op jit(solution)/shard_map/ppermute | solution.py:19
  70.6 5.8 %collective-permute-start.19 = (bf16[16,1152]{1,0:T(8,128)(2,1)S(1)}, bf16[16,1152]{1,0:T(8,128)(2,1)S(1)}, u32[]{:S(2)}, u32[]{:S(2)}) collective-permute-start(bf16[16,1152]{1,0:T(8,128)(2,1)S(1)} %get-tuple-element.66), channel_id=1, source_target_pairs={{0,3},{1,2},{2,1},{3,0},{4,7},{5,6},{6,5},{7,4},{8,11},{9,10},{10,... | collective-permute-start | bytes 110600 | tf_op jit(solution)/shard_map/ppermute | solution.py:19
  (8 other events, 62.8 us)

commit v5 on v4

--- a/solution.py
+++ b/solution.py
@@ -152,18 +152,13 @@
                 if c == 0:
                     first_copies.append(wanted)
                     wanted = []
-    lane = lax.broadcasted_iota(jnp.int32, (8, HD), 1)
-    sublane = lax.broadcasted_iota(jnp.int32, (8, HD), 0)
-    pair = (lane - lane % 2).astype(jnp.float32)
-    frequencies = jnp.exp(pair * (-math.log(10000.0) / HD))
-    for r in range(0, rows, 8):
-        place = jnp.full((8, HD), pos_ref[r], jnp.int32)
-        for i in range(1, 8):
-            place = jnp.where(sublane == i, pos_ref[r + i], place)
-        angles = place.astype(jnp.float32) * frequencies
-        cos_ref[r : r + 8] = jnp.cos(angles)
-        sine = jnp.sin(angles)
-        sin_ref[r : r + 8] = jnp.where(lane % 2 == 0, -sine, sine)
+    lane = lax.broadcasted_iota(jnp.int32, (1, HD), 1)
+    frequencies = jnp.exp((lane - lane % 2).astype(jnp.float32) * (-math.log(10000.0) / HD))
+    place = jnp.broadcast_to(pos_ref[...].astype(jnp.float32), (HD, rows)).T
+    angles = place * frequencies
+    cos_ref[...] = jnp.cos(angles)
+    sine = jnp.sin(angles)
+    sin_ref[...] = jnp.where(lane % 2 == 0, -sine, sine)
     done = set()
 
     def near(buf):
@@ -254,7 +249,7 @@
     count = sum(len(call) for call in calls) * (1 + 2 * share // per_copy)
     result = pl.pallas_call(
         functools.partial(attend_kernel, calls, share, per_copy, row_cuts, joined),
-        in_specs=[SMEM] * 2 + [HBM] * 3,
+        in_specs=[SMEM, VMEM] + [HBM] * 3,
         out_specs=[VMEM] * len(out_shape),
         out_shape=out_shape,
         scratch_shapes=[pltpu.VMEM(*entry) for entry in near(n)]
@@ -262,7 +257,7 @@
         cost_estimate=price(n),
         compiler_params=mib(ATTEND_MIB),
         name="attend",
-    )(cache_length, positions, queries, keys, values)
+    )(cache_length, positions[None], queries, keys, values)
     skip = len(blocks(n))
     tables, kept = result[skip : skip + 2], result[skip + 2 :]
     blocks_of = [found(result, n)]

time: 77.3 us -> 76.7 us (level)
  transfers between devices with their start and end apart: 20 -> 20, of which waited for: 10 -> 10; matrix products, arithmetic and copies ran while one was open for 0% -> 0% of each run, Pallas kernels for 18% -> 17%
where the time goes in v5:
time: 76.7 us; the launch traced here: 76.5 us
  waiting for transfers between devices  28.7 us (37%)
  starting transfers between devices  26.3 us (34%)
  Pallas kernels  18.2 us (24%)
  local copies, waits for them, and re-layouts  2.11 us (3%)
  between operations  0.87 us (1%)
    ppermute x20, waiting for transfers between devices, swap(): return lax.ppermute(values, axis, [(i, i ^ distance) for i in range(size)])  28.7 us
    ppermute x20, starting transfers between devices, swap(): return lax.ppermute(values, axis, [(i, i ^ distance) for i in range(size)])  26.3 us
    pallas_call x2, Pallas kernels, attend(): pl.pallas_call(functools.partial(attend_near_kernel, call, share, per_cop...  4.8 us
    pallas_call x1, Pallas kernels, sweep_all(): pl.pallas_call(functools.partial(sweep_kernel, (n_tm, time_each, rows, mo...  4.27 us
    pallas_call x1, Pallas kernels, attend(): pl.pallas_call(functools.partial(attend_kernel, calls, share, per_copy, r...  3.84 us
    unnamed x24, local copies, waits for them, and re-layouts  2.11 us
    pallas_call x1, Pallas kernels, project(): pl.pallas_call(functools.partial(project_kernel, cuts, later, row_cuts),...  1.6 us
  transfers between devices with their start and end apart: 20, of which 10 were waited for; matrix products, arithmetic and copies ran while one was open for 0% of the time, Pallas kernels for 17%

profile of v5, /device:TPU:0, one launch (start us, length us, event | category | flops | bytes accessed | tf_op | source)
XLA Modules:
  0.0 76.5 jit_solution(12654112185810174089)
XLA Ops:
  0.0 3.0 %collective-permute-start.9 = (bf16[2048,384]{1,0:T(8,128)(2,1)}, bf16[2048,384]{1,0:T(8,128)(2,1)S(1)}, u32[]{:S(2)}, u32[]{:S(2)}) collective-permute-start(bf16[2048,384]{1,0:T(8,128)(2,1)} %refs_1_.1), channel_id=1, source_target_pairs={{0,8},{4,12},{8,0},{12,4},{1,9},{5,13},{9,1},{13,5},{2,10},{6,14},... | collective-permute-start | bytes 4718600 | tf_op jit(solution)/shard_map/ppermute | solution.py:19
  3.6 1.2 %copy-done.4 = bf16[128,2048]{1,0:T(8,128)(2,1)S(1)} copy-done((bf16[128,2048]{1,0:T(8,128)(2,1)S(1)}, bf16[128,2048]{1,0:T(8,128)(2,1)}, u32[]{:S(2)}) %copy-start.4) | copy-done | bytes 524312
  5.7 3.8 %attend.1 = (bf16[136,512]{1,0:T(8,128)(2,1)S(1)}, f32[128,128]{1,0:T(8,128)S(1)}, f32[128,128]{1,0:T(8,128)S(1)}, bf16[2,128,512]{2,1,0:T(8,128)(2,1)S(1)}, bf1...) custom-call(s32[1]{0:T(128)S(6)} %copy.15.refs_0_, ...), custom_call_target="tpu_custom_call" | custom-call | flops 268435456 | bytes 2097152 | tf_op jit(solution)/shard_map/attend/pallas_call | solution.py:250
  9.6 3.2 %attend_near.3 = (bf16[136,512]{1,0:T(8,128)(2,1)S(1)}, bf16[136,512]{1,0:T(8,128)(2,1)S(1)}) custom-call(s32[1]{0:T(128)S(6)} %copy.15.refs_0_, f32[128,128]{1,0:T(8,128)S(1)} %get-tuple-element.40.refs_1_, f32[128,128]{1,0:T(8,128)S(1)} %get-tuple-element.41.refs_2_, bf16[2,128,512]{2,1,0:T(8,128)(2,1)S(1)} %get-tuple-element.45.refs_3_, ...), custom_call_target="tpu_custom_call" | custom-call | flops 536870912 | bytes 4194304 | tf_op jit(solution)/shard_map/attend_near/pallas_call | solution.py:266
  12.7 1.6 %collective-permute-start.3 = (bf16[136,512]{1,0:T(8,128)(2,1)S(1)}, bf16[136,512]{1,0:T(8,128)(2,1)S(1)}, u32[]{:S(2)}, u32[]{:S(2)}) collective-permute-start(bf16[136,512]{1,0:T(8,128)(2,1)S(1)} %get-tuple-element.48), channel_id=1, source_target_pairs={{0,1},{1,0},{2,3},{3,2},{4,5},{5,4},{6,7},{7,6},{8,9},{9,8},{10,11... | collective-permute-start | bytes 417800 | tf_op jit(solution)/shard_map/ppermute | solution.py:19
  14.3 2.6 %collective-permute-start.4 = (bf16[136,512]{1,0:T(8,128)(2,1)S(1)}, bf16[136,512]{1,0:T(8,128)(2,1)S(1)}, u32[]{:S(2)}, u32[]{:S(2)}) collective-permute-start(bf16[136,512]{1,0:T(8,128)(2,1)S(1)} %get-tuple-element.49), channel_id=1, source_target_pairs={{0,2},{1,3},{2,0},{3,1},{4,6},{5,7},{6,4},{7,5},{8,10},{9,11},{10,... | collective-permute-start | bytes 417800 | tf_op jit(solution)/shard_map/ppermute | solution.py:19
  17.1 1.6 %attend_near.2.refs_0_ = bf16[136,512]{1,0:T(8,128)(2,1)S(1)} custom-call(s32[1]{0:T(128)S(6)} %copy.15.refs_0_, f32[128,128]{1,0:T(8,128)S(1)} %get-tuple-element.40.refs_1_, f32[128,128]{1,0:T(8,128)S(1)} %get-tuple-element.41.refs_2_, bf16[1,128,512]{2,1,0:T(8,128)(2,1)S(1)} %get-tuple-element.42.refs_3_, ...), custom_call_target="tpu_custom_call" | custom-call | flops 268435456 | bytes 2097152 | tf_op jit(solution)/shard_map/attend_near/pallas_call | solution.py:266
  19.6 8.0 %collective-permute-done.4.refs_2_ = bf16[136,512]{1,0:T(8,128)(2,1)S(1)} collective-permute-done((bf16[136,512]{1,0:T(8,128)(2,1)S(1)}, bf16[136,512]{1,0:T(8,128)(2,1)S(1)}, u32[]{:S(2)}, u32[]{:S(2)}) %collective-permute-start.4) | collective-permute-done | bytes 139296 | tf_op jit(solution)/shard_map/ppermute | solution.py:19
  28.1 2.1 %collective-permute-start.6 = (bf16[128,512]{1,0:T(8,128)(2,1)S(1)}, bf16[128,512]{1,0:T(8,128)(2,1)S(1)}, u32[]{:S(2)}, u32[]{:S(2)}) collective-permute-start(bf16[128,512]{1,0:T(8,128)(2,1)S(1)} %merge.1.refs_0_), channel_id=1, source_target_pairs={{0,1},{1,0},{2,3},{3,2},{4,5},{5,4},{6,7},{7,6},{8,9},{9,8},{10,11... | collective-permute-start | bytes 393224 | tf_op jit(solution)/shard_map/ppermute | solution.py:19
  31.3 1.4 %collective-permute-start.8 = (bf16[128,512]{1,0:T(8,128)(2,1)S(1)}, bf16[128,512]{1,0:T(8,128)(2,1)S(1)}, u32[]{:S(2)}, u32[]{:S(2)}) collective-permute-start(bf16[128,512]{1,0:T(8,128)(2,1)S(1)} %merge.1.refs_0_), channel_id=1, source_target_pairs={{0,3},{1,2},{2,1},{3,0},{4,7},{5,6},{6,5},{7,4},{8,11},{9,10},{10,... | collective-permute-start | bytes 393224 | tf_op jit(solution)/shard_map/ppermute | solution.py:19
  32.7 1.9 %collective-permute-done.6.refs_1_ = bf16[128,512]{1,0:T(8,128)(2,1)S(1)} collective-permute-done((bf16[128,512]{1,0:T(8,128)(2,1)S(1)}, bf16[128,512]{1,0:T(8,128)(2,1)S(1)}, u32[]{:S(2)}, u32[]{:S(2)}) %collective-permute-start.6) | collective-permute-done | bytes 131104 | tf_op jit(solution)/shard_map/ppermute | solution.py:19
  34.6 1.6 %project.1 = (f32[128,2048]{1,0:T(8,128)S(1)}, bf16[2,512,2048]{2,1,0:T(8,128)(2,1)S(1)}) custom-call(bf16[128,512]{1,0:T(8,128)(2,1)S(1)} %merge.1.refs_0_, bf16[128,512]{1,0:T(8,128)(2,1)S(1)} %collective-permute-done.6.refs_1_, bf16[2048,2048]{1,0:T(8,128)(2,1)S(1)} %bitcast.6), custom_call_target="tpu_custom_call" | custom-call | flops 536870912 | bytes 8388608 | tf_op jit(solution)/shard_map/project/pallas_call | solution.py:342
  36.2 5.7 %collective-permute-done.7.refs_0_ = bf16[128,512]{1,0:T(8,128)(2,1)S(1)} collective-permute-done((bf16[128,512]{1,0:T(8,128)(2,1)S(1)}, bf16[128,512]{1,0:T(8,128)(2,1)S(1)}, u32[]{:S(2)}, u32[]{:S(2)}) %collective-permute-start.7) | collective-permute-done | bytes 131104 | tf_op jit(solution)/shard_map/ppermute | solution.py:19
  43.3 2.0 %collective-permute-start = (bf16[16,1152]{1,0:T(8,128)(2,1)S(1)}, bf16[16,1152]{1,0:T(8,128)(2,1)S(1)}, u32[]{:S(2)}, u32[]{:S(2)}) collective-permute-start(bf16[16,1152]{1,0:T(8,128)(2,1)S(1)} %get-tuple-element.37), channel_id=1, source_target_pairs={{0,1},{1,0},{2,3},{3,2},{4,5},{5,4},{6,7},{7,6},{8,9},{9,8},{10,11... | collective-permute-start | bytes 110600 | tf_op jit(solution)/shard_map/ppermute | solution.py:19
  47.0 1.2 %collective-permute-done.10.got_ref = bf16[2,32,2048]{2,1,0:T(8,128)(2,1)S(1)} collective-permute-done((bf16[2,32,2048]{2,1,0:T(8,128)(2,1)S(1)}, bf16[2,32,2048]{2,1,0:T(8,128)(2,1)S(1)}, u32[]{:S(2)}, u32[]{:S(2)}) %collective-permute-start.10) | collective-permute-done | bytes 262176 | tf_op jit(solution)/shard_map/ppermute | solution.py:19
  48.7 1.4 %collective-permute-start.2 = (bf16[16,1152]{1,0:T(8,128)(2,1)S(1)}, bf16[16,1152]{1,0:T(8,128)(2,1)S(1)}, u32[]{:S(2)}, u32[]{:S(2)}) collective-permute-start(bf16[16,1152]{1,0:T(8,128)(2,1)S(1)} %get-tuple-element.39), channel_id=1, source_target_pairs={{0,3},{1,2},{2,1},{3,0},{4,7},{5,6},{6,5},{7,4},{8,11},{9,10},{10,... | collective-permute-start | bytes 110600 | tf_op jit(solution)/shard_map/ppermute | solution.py:19
  50.2 3.6 %collective-permute-done.11.refs_0_ = bf16[32,2048]{1,0:T(8,128)(2,1)S(1)} collective-permute-done((bf16[32,2048]{1,0:T(8,128)(2,1)S(1)}, bf16[32,2048]{1,0:T(8,128)(2,1)S(1)}, u32[]{:S(2)}, u32[]{:S(2)}) %collective-permute-start.11) | collective-permute-done | bytes 131104 | tf_op jit(solution)/shard_map/ppermute | solution.py:19
  54.9 2.0 %collective-permute-start.14 = (bf16[8,1664]{1,0:T(8,128)(2,1)S(1)}, bf16[8,1664]{1,0:T(8,128)(2,1)S(1)}, u32[]{:S(2)}, u32[]{:S(2)}) collective-permute-start(bf16[8,1664]{1,0:T(8,128)(2,1)S(1)} %get-tuple-element.60), channel_id=1, source_target_pairs={{0,1},{1,0},{2,3},{3,2},{4,5},{5,4},{6,7},{7,6},{8,9},{9,8},{10,11... | collective-permute-start | bytes 79880 | tf_op jit(solution)/shard_map/ppermute | solution.py:19
  57.0 2.4 %collective-permute-start.16 = (bf16[8,1664]{1,0:T(8,128)(2,1)S(1)}, bf16[8,1664]{1,0:T(8,128)(2,1)S(1)}, u32[]{:S(2)}, u32[]{:S(2)}) collective-permute-start(bf16[8,1664]{1,0:T(8,128)(2,1)S(1)} %get-tuple-element.62), channel_id=1, source_target_pairs={{0,3},{1,2},{2,1},{3,0},{4,7},{5,6},{6,5},{7,4},{8,11},{9,10},{10,... | collective-permute-start | bytes 79880 | tf_op jit(solution)/shard_map/ppermute | solution.py:19
  59.5 2.2 %collective-permute-done.15.refs_6_ = bf16[8,1664]{1,0:T(8,128)(2,1)S(1)} collective-permute-done((bf16[8,1664]{1,0:T(8,128)(2,1)S(1)}, bf16[8,1664]{1,0:T(8,128)(2,1)S(1)}, u32[]{:S(2)}, u32[]{:S(2)}) %collective-permute-start.15) | collective-permute-done | bytes 26656 | tf_op jit(solution)/shard_map/ppermute | solution.py:19
  62.6 4.3 %sweeps.1 = (bf16[16,1152]{1,0:T(8,128)(2,1)S(1)}, bf16[16,1152]{1,0:T(8,128)(2,1)S(1)}, bf16[16,1152]{1,0:T(8,128)(2,1)S(1)}, bf16[16,1152]{1,0:T(8,128)(2,1)S(1)}) custom-call(f32[16]{0:T(128)S(1)} %pad_maximum_fusion.1.steps, f32[4,8,1152]{2,1,0:T(8,128)S(1)} %bitcast.7, f32[8,1536]{1,0:T(8,128)S(1)} %pad_maximum_fusion.embed_ref, ...), custom_call_target="tpu_custom_call" | custom-call | flops 1132462080 | bytes 7077888 | tf_op jit(solution)/shard_map/sweeps/pallas_call | solution.py:536
  67.0 3.0 %collective-permute-start.18 = (bf16[16,1152]{1,0:T(8,128)(2,1)S(1)}, bf16[16,1152]{1,0:T(8,128)(2,1)S(1)}, u32[]{:S(2)}, u32[]{:S(2)}) collective-permute-start(bf16[16,1152]{1,0:T(8,128)(2,1)S(1)} %get-tuple-element.65), channel_id=1, source_target_pairs={{0,2},{1,3},{2,0},{3,1},{4,6},{5,7},{6,4},{7,5},{8,10},{9,11},{10,... | collective-permute-start | bytes 110600 | tf_op jit(solution)/shard_map/ppermute | solution.py:19
  70.0 1.4 %collective-permute-start.19 = (bf16[16,1152]{1,0:T(8,128)(2,1)S(1)}, bf16[16,1152]{1,0:T(8,128)(2,1)S(1)}, u32[]{:S(2)}, u32[]{:S(2)}) collective-permute-start(bf16[16,1152]{1,0:T(8,128)(2,1)S(1)} %get-tuple-element.66), channel_id=1, source_target_pairs={{0,3},{1,2},{2,1},{3,0},{4,7},{5,6},{6,5},{7,4},{8,11},{9,10},{10,... | collective-permute-start | bytes 110600 | tf_op jit(solution)/shard_map/ppermute | solution.py:19
  72.3 3.4 %collective-permute-done.19.refs_3_ = bf16[16,1152]{1,0:T(8,128)(2,1)S(1)} collective-permute-done((bf16[16,1152]{1,0:T(8,128)(2,1)S(1)}, bf16[16,1152]{1,0:T(8,128)(2,1)S(1)}, u32[]{:S(2)}, u32[]{:S(2)}) %collective-permute-start.19) | collective-permute-done | bytes 36896 | tf_op jit(solution)/shard_map/ppermute | solution.py:19
  (58 shorter events, 11.1 us)
Async XLA Ops:
  0.0 42.8 %collective-permute-start.9 = (bf16[2048,384]{1,0:T(8,128)(2,1)}, bf16[2048,384]{1,0:T(8,128)(2,1)S(1)}, u32[]{:S(2)}, u32[]{:S(2)}) collective-permute-start(bf16[2048,384]{1,0:T(8,128)(2,1)} %refs_1_.1), channel_id=1, source_target_pairs={{0,8},{4,12},{8,0},{12,4},{1,9},{5,13},{9,1},{13,5},{2,10},{6,14},... | collective-permute-start | bytes 4718600 | tf_op jit(solution)/shard_map/ppermute | solution.py:19
  3.6 31.0 %slice-start = ((s8[8388608]{0:T(1024)(128)(4,1)}), s8[4194304]{0:T(1024)(128)(4,1)S(1)}, s32[]{:S(2)}) async-start(s8[8388608]{0:T(1024)(128)(4,1)} %bitcast.5), calls=%async_computation | async-start | bytes 8388608
  5.7 28.9 %slice-start.1 = ((s8[8388608]{0:T(1024)(128)(4,1)}), s8[4194304]{0:T(1024)(128)(4,1)S(1)}, s32[]{:S(2)}) async-start(s8[8388608]{0:T(1024)(128)(4,1)} %bitcast.5), calls=%async_computation.1 | async-start | bytes 8388608
  9.5 23.2 %copy-start.2 = (bf16[2048,384]{1,0:T(8,128)(2,1)S(1)}, bf16[2048,384]{1,0:T(8,128)(2,1)}, u32[]{:S(2)}) copy-start(bf16[2048,384]{1,0:T(8,128)(2,1)} %refs_1_.1) | copy-start | bytes 4718596
  12.7 6.9 %collective-permute-start.3 = (bf16[136,512]{1,0:T(8,128)(2,1)S(1)}, bf16[136,512]{1,0:T(8,128)(2,1)S(1)}, u32[]{:S(2)}, u32[]{:S(2)}) collective-permute-start(bf16[136,512]{1,0:T(8,128)(2,1)S(1)} %get-tuple-element.48), channel_id=1, source_target_pairs={{0,1},{1,0},{2,3},{3,2},{4,5},{5,4},{6,7},{7,6},{8,9},{9,8},{10,11... | collective-permute-start | bytes 417800 | tf_op jit(solution)/shard_map/ppermute | solution.py:19
  14.3 13.3 %collective-permute-start.4 = (bf16[136,512]{1,0:T(8,128)(2,1)S(1)}, bf16[136,512]{1,0:T(8,128)(2,1)S(1)}, u32[]{:S(2)}, u32[]{:S(2)}) collective-permute-start(bf16[136,512]{1,0:T(8,128)(2,1)S(1)} %get-tuple-element.49), channel_id=1, source_target_pairs={{0,2},{1,3},{2,0},{3,1},{4,6},{5,7},{6,4},{7,5},{8,10},{9,11},{10,... | collective-permute-start | bytes 417800 | tf_op jit(solution)/shard_map/ppermute | solution.py:19
  16.9 10.7 %collective-permute-start.5 = (bf16[136,512]{1,0:T(8,128)(2,1)S(1)}, bf16[136,512]{1,0:T(8,128)(2,1)S(1)}, u32[]{:S(2)}, u32[]{:S(2)}) collective-permute-start(bf16[136,512]{1,0:T(8,128)(2,1)S(1)} %get-tuple-element.50), channel_id=1, source_target_pairs={{0,3},{1,2},{2,1},{3,0},{4,7},{5,6},{6,5},{7,4},{8,11},{9,10},{10,... | collective-permute-start | bytes 417800 | tf_op jit(solution)/shard_map/ppermute | solution.py:19
  28.1 6.5 %collective-permute-start.6 = (bf16[128,512]{1,0:T(8,128)(2,1)S(1)}, bf16[128,512]{1,0:T(8,128)(2,1)S(1)}, u32[]{:S(2)}, u32[]{:S(2)}) collective-permute-start(bf16[128,512]{1,0:T(8,128)(2,1)S(1)} %merge.1.refs_0_), channel_id=1, source_target_pairs={{0,1},{1,0},{2,3},{3,2},{4,5},{5,4},{6,7},{7,6},{8,9},{9,8},{10,11... | collective-permute-start | bytes 393224 | tf_op jit(solution)/shard_map/ppermute | solution.py:19
  30.2 11.7 %collective-permute-start.7 = (bf16[128,512]{1,0:T(8,128)(2,1)S(1)}, bf16[128,512]{1,0:T(8,128)(2,1)S(1)}, u32[]{:S(2)}, u32[]{:S(2)}) collective-permute-start(bf16[128,512]{1,0:T(8,128)(2,1)S(1)} %merge.1.refs_0_), channel_id=1, source_target_pairs={{0,2},{1,3},{2,0},{3,1},{4,6},{5,7},{6,4},{7,5},{8,10},{9,11},{10,... | collective-permute-start | bytes 393224 | tf_op jit(solution)/shard_map/ppermute | solution.py:19
  31.3 10.6 %collective-permute-start.8 = (bf16[128,512]{1,0:T(8,128)(2,1)S(1)}, bf16[128,512]{1,0:T(8,128)(2,1)S(1)}, u32[]{:S(2)}, u32[]{:S(2)}) collective-permute-start(bf16[128,512]{1,0:T(8,128)(2,1)S(1)} %merge.1.refs_0_), channel_id=1, source_target_pairs={{0,3},{1,2},{2,1},{3,0},{4,7},{5,6},{6,5},{7,4},{8,11},{9,10},{10,... | collective-permute-start | bytes 393224 | tf_op jit(solution)/shard_map/ppermute | solution.py:19
  32.7 16.1 %collective-permute-start.12 = (bf16[2048,384]{1,0:T(8,128)(2,1)S(1)}, bf16[2048,384]{1,0:T(8,128)(2,1)S(1)}, u32[]{:S(2)}, u32[]{:S(2)}) collective-permute-start(bf16[2048,384]{1,0:T(8,128)(2,1)S(1)} %copy-done.2), channel_id=1, source_target_pairs={{0,4},{4,0},{8,12},{12,8},{1,5},{5,1},{9,13},{13,9},{2,6},{6,2},{1... | collective-permute-start | bytes 4718600 | tf_op jit(solution)/shard_map/ppermute | solution.py:19
  36.2 17.6 %copy-start.5 = (bf16[128,2048]{1,0:T(8,128)(2,1)S(1)}, bf16[128,2048]{1,0:T(8,128)(2,1)}, u32[]{:S(2)}) copy-start(bf16[128,2048]{1,0:T(8,128)(2,1)} %param.17) | copy-start | bytes 1572868
  42.9 11.0 %collective-permute-start.13 = (bf16[2048,384]{1,0:T(8,128)(2,1)S(1)}, bf16[2048,384]{1,0:T(8,128)(2,1)S(1)}, u32[]{:S(2)}, u32[]{:S(2)}) collective-permute-start(bf16[2048,384]{1,0:T(8,128)(2,1)S(1)} %collective-permute-done.9.refs_3_), channel_id=1, source_target_pairs={{0,4},{4,0},{8,12},{12,8},{1,5},{5,1},{9,13},{13,9},{2,6},{6,2},{1... | collective-permute-start | bytes 4718600 | tf_op jit(solution)/shard_map/ppermute | solution.py:19
  43.3 13.6 %collective-permute-start = (bf16[16,1152]{1,0:T(8,128)(2,1)S(1)}, bf16[16,1152]{1,0:T(8,128)(2,1)S(1)}, u32[]{:S(2)}, u32[]{:S(2)}) collective-permute-start(bf16[16,1152]{1,0:T(8,128)(2,1)S(1)} %get-tuple-element.37), channel_id=1, source_target_pairs={{0,1},{1,0},{2,3},{3,2},{4,5},{5,4},{6,7},{7,6},{8,9},{9,8},{10,11... | collective-permute-start | bytes 110600 | tf_op jit(solution)/shard_map/ppermute | solution.py:19
  45.3 14.1 %collective-permute-start.1 = (bf16[16,1152]{1,0:T(8,128)(2,1)S(1)}, bf16[16,1152]{1,0:T(8,128)(2,1)S(1)}, u32[]{:S(2)}, u32[]{:S(2)}) collective-permute-start(bf16[16,1152]{1,0:T(8,128)(2,1)S(1)} %get-tuple-element.38), channel_id=1, source_target_pairs={{0,2},{1,3},{2,0},{3,1},{4,6},{5,7},{6,4},{7,5},{8,10},{9,11},{10,... | collective-permute-start | bytes 110600 | tf_op jit(solution)/shard_map/ppermute | solution.py:19
  46.6 1.5 %collective-permute-start.10 = (bf16[2,32,2048]{2,1,0:T(8,128)(2,1)S(1)}, bf16[2,32,2048]{2,1,0:T(8,128)(2,1)S(1)}, u32[]{:S(2)}, u32[]{:S(2)}) collective-permute-start(bf16[2,32,2048]{2,1,0:T(8,128)(2,1)S(1)} %get-tuple-element.55), channel_id=1, source_target_pairs={{0,4},{4,0},{8,12},{12,8},{1,5},{5,1},{9,13},{13,9},{2,6},{6,2},{1... | collective-permute-start | bytes 786440 | tf_op jit(solution)/shard_map/ppermute | solution.py:19
  48.2 5.7 %collective-permute-start.11 = (bf16[32,2048]{1,0:T(8,128)(2,1)S(1)}, bf16[32,2048]{1,0:T(8,128)(2,1)S(1)}, u32[]{:S(2)}, u32[]{:S(2)}) collective-permute-start(bf16[32,2048]{1,0:T(8,128)(2,1)S(1)} %get-tuple-element.57), channel_id=1, source_target_pairs={{0,8},{4,12},{8,0},{12,4},{1,9},{5,13},{9,1},{13,5},{2,10},{6,14},... | collective-permute-start | bytes 393224 | tf_op jit(solution)/shard_map/ppermute | solution.py:19
  48.7 10.7 %collective-permute-start.2 = (bf16[16,1152]{1,0:T(8,128)(2,1)S(1)}, bf16[16,1152]{1,0:T(8,128)(2,1)S(1)}, u32[]{:S(2)}, u32[]{:S(2)}) collective-permute-start(bf16[16,1152]{1,0:T(8,128)(2,1)S(1)} %get-tuple-element.39), channel_id=1, source_target_pairs={{0,3},{1,2},{2,1},{3,0},{4,7},{5,6},{6,5},{7,4},{8,11},{9,10},{10,... | collective-permute-start | bytes 110600 | tf_op jit(solution)/shard_map/ppermute | solution.py:19
  54.9 4.5 %collective-permute-start.14 = (bf16[8,1664]{1,0:T(8,128)(2,1)S(1)}, bf16[8,1664]{1,0:T(8,128)(2,1)S(1)}, u32[]{:S(2)}, u32[]{:S(2)}) collective-permute-start(bf16[8,1664]{1,0:T(8,128)(2,1)S(1)} %get-tuple-element.60), channel_id=1, source_target_pairs={{0,1},{1,0},{2,3},{3,2},{4,5},{5,4},{6,7},{7,6},{8,9},{9,8},{10,11... | collective-permute-start | bytes 79880 | tf_op jit(solution)/shard_map/ppermute | solution.py:19
  56.9 4.7 %collective-permute-start.15 = (bf16[8,1664]{1,0:T(8,128)(2,1)S(1)}, bf16[8,1664]{1,0:T(8,128)(2,1)S(1)}, u32[]{:S(2)}, u32[]{:S(2)}) collective-permute-start(bf16[8,1664]{1,0:T(8,128)(2,1)S(1)} %get-tuple-element.61), channel_id=1, source_target_pairs={{0,2},{1,3},{2,0},{3,1},{4,6},{5,7},{6,4},{7,5},{8,10},{9,11},{10,... | collective-permute-start | bytes 79880 | tf_op jit(solution)/shard_map/ppermute | solution.py:19
  57.0 5.6 %collective-permute-start.16 = (bf16[8,1664]{1,0:T(8,128)(2,1)S(1)}, bf16[8,1664]{1,0:T(8,128)(2,1)S(1)}, u32[]{:S(2)}, u32[]{:S(2)}) collective-permute-start(bf16[8,1664]{1,0:T(8,128)(2,1)S(1)} %get-tuple-element.62), channel_id=1, source_target_pairs={{0,3},{1,2},{2,1},{3,0},{4,7},{5,6},{6,5},{7,4},{8,11},{9,10},{10,... | collective-permute-start | bytes 79880 | tf_op jit(solution)/shard_map/ppermute | solution.py:19
  66.9 4.5 %collective-permute-start.17 = (bf16[16,1152]{1,0:T(8,128)(2,1)S(1)}, bf16[16,1152]{1,0:T(8,128)(2,1)S(1)}, u32[]{:S(2)}, u32[]{:S(2)}) collective-permute-start(bf16[16,1152]{1,0:T(8,128)(2,1)S(1)} %get-tuple-element.64), channel_id=1, source_target_pairs={{0,1},{1,0},{2,3},{3,2},{4,5},{5,4},{6,7},{7,6},{8,9},{9,8},{10,11... | collective-permute-start | bytes 110600 | tf_op jit(solution)/shard_map/ppermute | solution.py:19
  67.0 5.3 %collective-permute-start.18 = (bf16[16,1152]{1,0:T(8,128)(2,1)S(1)}, bf16[16,1152]{1,0:T(8,128)(2,1)S(1)}, u32[]{:S(2)}, u32[]{:S(2)}) collective-permute-start(bf16[16,1152]{1,0:T(8,128)(2,1)S(1)} %get-tuple-element.65), channel_id=1, source_target_pairs={{0,2},{1,3},{2,0},{3,1},{4,6},{5,7},{6,4},{7,5},{8,10},{9,11},{10,... | collective-permute-start | bytes 110600 | tf_op jit(solution)/shard_map/ppermute | solution.py:19
  70.0 5.8 %collective-permute-start.19 = (bf16[16,1152]{1,0:T(8,128)(2,1)S(1)}, bf16[16,1152]{1,0:T(8,128)(2,1)S(1)}, u32[]{:S(2)}, u32[]{:S(2)}) collective-permute-start(bf16[16,1152]{1,0:T(8,128)(2,1)S(1)} %get-tuple-element.66), channel_id=1, source_target_pairs={{0,3},{1,2},{2,1},{3,0},{4,7},{5,6},{6,5},{7,4},{8,11},{9,10},{10,... | collective-permute-start | bytes 110600 | tf_op jit(solution)/shard_map/ppermute | solution.py:19
  (8 other events, 63.0 us)

commit v6 on v5

--- a/solution.py
+++ b/solution.py
@@ -473,7 +473,25 @@
     return [pick(result, t ^ s) for s in range(n_tm)]
 
 
-def sweep_kernel(sizes, steps, start_ref, embed_ref, in_ref, head_ref, *refs):
+def opening_kernel(start_ref, in_ref, out_ref):
+    start = start_ref[lax.axis_index("tm")].astype(jnp.bfloat16)
+    out_ref[...] = jnp.dot(start, in_ref[...], preferred_element_type=jnp.float32)
+
+
+def opening_product(start, in_weight):
+    rows, width = start.shape[1], in_weight.shape[1]
+    return pl.pallas_call(
+        opening_kernel,
+        in_specs=[VMEM] * 2,
+        out_specs=VMEM,
+        out_shape=jax.ShapeDtypeStruct((rows, width), jnp.float32),
+        cost_estimate=cost(2 * rows * in_weight.size, 0, in_weight),
+        compiler_params=mib(8),
+        name="opening",
+    )(start, in_weight)
+
+
+def sweep_kernel(sizes, steps, start_ref, embed_ref, in_ref, head_ref, opening_ref, *refs):
     n_tm, time_each, rows, model = sizes
     noise_refs, refs = refs[:n_tm], refs[n_tm:]
     parts, refs = refs[:n_tm], refs[n_tm:]
@@ -491,7 +509,7 @@
 
     noise = [steps[times + i] * held[block(i)] for i in range(times - 1)]
     width = in_ref.shape[1]
-    opening = jnp.dot(start.astype(jnp.bfloat16), in_ref[...], preferred_element_type=jnp.float32)
+    opening = opening_ref[...]
     total = sum(p[...].astype(jnp.float32) for p in parts)
     squares = total[:, width : width + 1]
     for p in range(1, PIECES):
@@ -533,9 +551,10 @@
 def sweep_all(parts, noise, embedding, steps, start, in_weight, head_out, time_each, model):
     n_tm, rows, chan = start.shape
     block = (time_each * rows, chan)
+    opening = opening_product(start, in_weight)
     return pl.pallas_call(
         functools.partial(sweep_kernel, (n_tm, time_each, rows, model)),
-        in_specs=[SMEM] + [VMEM] * (4 + 2 * n_tm),
+        in_specs=[SMEM] + [VMEM] * (5 + 2 * n_tm),
         out_specs=[VMEM] * n_tm,
         out_shape=[jax.ShapeDtypeStruct(block, jnp.bfloat16)] * n_tm,
         scratch_shapes=[pltpu.VMEM((n_tm, *block), jnp.float32)],
@@ -544,7 +563,7 @@
         ),
         compiler_params=mib(16),
         name="sweeps",
-    )(steps, start, embedding, in_weight, head_out, *noise, *parts)
+    )(steps, start, embedding, in_weight, head_out, opening, *noise, *parts)
 
 
 def noise_kernel(time_each, noise_ref, *outs):

time: 76.7 us -> 76.4 us (level)
  transfers between devices with their start and end apart: 20 -> 20, of which waited for: 10 -> 10; matrix products, arithmetic and copies ran while one was open for 0% -> 0% of each run, Pallas kernels for 17% -> 18%
where the time goes in v6:
time: 76.4 us; the launch traced here: 76.2 us
  waiting for transfers between devices  28.1 us (37%)
  starting transfers between devices  26.3 us (34%)
  Pallas kernels  18.5 us (24%)
  local copies, waits for them, and re-layouts  2.11 us (3%)
  between operations  0.87 us (1%)
    ppermute x20, waiting for transfers between devices, swap(): return lax.ppermute(values, axis, [(i, i ^ distance) for i in range(size)])  28.1 us
    ppermute x20, starting transfers between devices, swap(): return lax.ppermute(values, axis, [(i, i ^ distance) for i in range(size)])  26.3 us
    pallas_call x2, Pallas kernels, attend(): pl.pallas_call(functools.partial(attend_near_kernel, call, share, per_cop...  4.8 us
    pallas_call x1, Pallas kernels, sweep_all(): pl.pallas_call(functools.partial(sweep_kernel, (n_tm, time_each, rows, mo...  3.93 us
    pallas_call x1, Pallas kernels, attend(): pl.pallas_call(functools.partial(attend_kernel, calls, share, per_copy, r...  3.84 us
    unnamed x24, local copies, waits for them, and re-layouts  2.11 us
    pallas_call x1, Pallas kernels, project(): pl.pallas_call(functools.partial(project_kernel, cuts, later, row_cuts),...  1.6 us
  transfers between devices with their start and end apart: 20, of which 10 were waited for; matrix products, arithmetic and copies ran while one was open for 0% of the time, Pallas kernels for 18%

profile of v6, /device:TPU:0, one launch (start us, length us, event | category | flops | bytes accessed | tf_op | source)
XLA Modules:
  0.0 76.2 jit_solution(3066615529286453877)
XLA Ops:
  0.0 3.0 %collective-permute-start.9 = (bf16[2048,384]{1,0:T(8,128)(2,1)}, bf16[2048,384]{1,0:T(8,128)(2,1)S(1)}, u32[]{:S(2)}, u32[]{:S(2)}) collective-permute-start(bf16[2048,384]{1,0:T(8,128)(2,1)} %refs_1_.1), channel_id=1, source_target_pairs={{0,8},{4,12},{8,0},{12,4},{1,9},{5,13},{9,1},{13,5},{2,10},{6,14},... | collective-permute-start | bytes 4718600 | tf_op jit(solution)/shard_map/ppermute | solution.py:19
  3.6 1.2 %copy-done.4 = bf16[128,2048]{1,0:T(8,128)(2,1)S(1)} copy-done((bf16[128,2048]{1,0:T(8,128)(2,1)S(1)}, bf16[128,2048]{1,0:T(8,128)(2,1)}, u32[]{:S(2)}) %copy-start.4) | copy-done | bytes 524312
  5.7 3.8 %attend.1 = (bf16[136,512]{1,0:T(8,128)(2,1)S(1)}, f32[128,128]{1,0:T(8,128)S(1)}, f32[128,128]{1,0:T(8,128)S(1)}, bf16[2,128,512]{2,1,0:T(8,128)(2,1)S(1)}, bf1...) custom-call(s32[1]{0:T(128)S(6)} %copy.15.refs_0_, ...), custom_call_target="tpu_custom_call" | custom-call | flops 268435456 | bytes 2097152 | tf_op jit(solution)/shard_map/attend/pallas_call | solution.py:250
  9.6 3.2 %attend_near.3 = (bf16[136,512]{1,0:T(8,128)(2,1)S(1)}, bf16[136,512]{1,0:T(8,128)(2,1)S(1)}) custom-call(s32[1]{0:T(128)S(6)} %copy.15.refs_0_, f32[128,128]{1,0:T(8,128)S(1)} %get-tuple-element.40.refs_1_, f32[128,128]{1,0:T(8,128)S(1)} %get-tuple-element.41.refs_2_, bf16[2,128,512]{2,1,0:T(8,128)(2,1)S(1)} %get-tuple-element.45.refs_3_, ...), custom_call_target="tpu_custom_call" | custom-call | flops 536870912 | bytes 4194304 | tf_op jit(solution)/shard_map/attend_near/pallas_call | solution.py:266
  12.7 1.6 %collective-permute-start.3 = (bf16[136,512]{1,0:T(8,128)(2,1)S(1)}, bf16[136,512]{1,0:T(8,128)(2,1)S(1)}, u32[]{:S(2)}, u32[]{:S(2)}) collective-permute-start(bf16[136,512]{1,0:T(8,128)(2,1)S(1)} %get-tuple-element.48), channel_id=1, source_target_pairs={{0,1},{1,0},{2,3},{3,2},{4,5},{5,4},{6,7},{7,6},{8,9},{9,8},{10,11... | collective-permute-start | bytes 417800 | tf_op jit(solution)/shard_map/ppermute | solution.py:19
  14.3 2.6 %collective-permute-start.4 = (bf16[136,512]{1,0:T(8,128)(2,1)S(1)}, bf16[136,512]{1,0:T(8,128)(2,1)S(1)}, u32[]{:S(2)}, u32[]{:S(2)}) collective-permute-start(bf16[136,512]{1,0:T(8,128)(2,1)S(1)} %get-tuple-element.49), channel_id=1, source_target_pairs={{0,2},{1,3},{2,0},{3,1},{4,6},{5,7},{6,4},{7,5},{8,10},{9,11},{10,... | collective-permute-start | bytes 417800 | tf_op jit(solution)/shard_map/ppermute | solution.py:19
  17.1 1.6 %attend_near.2.refs_0_ = bf16[136,512]{1,0:T(8,128)(2,1)S(1)} custom-call(s32[1]{0:T(128)S(6)} %copy.15.refs_0_, f32[128,128]{1,0:T(8,128)S(1)} %get-tuple-element.40.refs_1_, f32[128,128]{1,0:T(8,128)S(1)} %get-tuple-element.41.refs_2_, bf16[1,128,512]{2,1,0:T(8,128)(2,1)S(1)} %get-tuple-element.42.refs_3_, ...), custom_call_target="tpu_custom_call" | custom-call | flops 268435456 | bytes 2097152 | tf_op jit(solution)/shard_map/attend_near/pallas_call | solution.py:266
  19.6 8.0 %collective-permute-done.4.refs_2_ = bf16[136,512]{1,0:T(8,128)(2,1)S(1)} collective-permute-done((bf16[136,512]{1,0:T(8,128)(2,1)S(1)}, bf16[136,512]{1,0:T(8,128)(2,1)S(1)}, u32[]{:S(2)}, u32[]{:S(2)}) %collective-permute-start.4) | collective-permute-done | bytes 139296 | tf_op jit(solution)/shard_map/ppermute | solution.py:19
  28.1 2.1 %collective-permute-start.6 = (bf16[128,512]{1,0:T(8,128)(2,1)S(1)}, bf16[128,512]{1,0:T(8,128)(2,1)S(1)}, u32[]{:S(2)}, u32[]{:S(2)}) collective-permute-start(bf16[128,512]{1,0:T(8,128)(2,1)S(1)} %merge.1.refs_0_), channel_id=1, source_target_pairs={{0,1},{1,0},{2,3},{3,2},{4,5},{5,4},{6,7},{7,6},{8,9},{9,8},{10,11... | collective-permute-start | bytes 393224 | tf_op jit(solution)/shard_map/ppermute | solution.py:19
  31.3 1.4 %collective-permute-start.8 = (bf16[128,512]{1,0:T(8,128)(2,1)S(1)}, bf16[128,512]{1,0:T(8,128)(2,1)S(1)}, u32[]{:S(2)}, u32[]{:S(2)}) collective-permute-start(bf16[128,512]{1,0:T(8,128)(2,1)S(1)} %merge.1.refs_0_), channel_id=1, source_target_pairs={{0,3},{1,2},{2,1},{3,0},{4,7},{5,6},{6,5},{7,4},{8,11},{9,10},{10,... | collective-permute-start | bytes 393224 | tf_op jit(solution)/shard_map/ppermute | solution.py:19
  32.7 1.9 %collective-permute-done.6.refs_1_ = bf16[128,512]{1,0:T(8,128)(2,1)S(1)} collective-permute-done((bf16[128,512]{1,0:T(8,128)(2,1)S(1)}, bf16[128,512]{1,0:T(8,128)(2,1)S(1)}, u32[]{:S(2)}, u32[]{:S(2)}) %collective-permute-start.6) | collective-permute-done | bytes 131104 | tf_op jit(solution)/shard_map/ppermute | solution.py:19
  34.6 1.6 %project.1 = (f32[128,2048]{1,0:T(8,128)S(1)}, bf16[2,512,2048]{2,1,0:T(8,128)(2,1)S(1)}) custom-call(bf16[128,512]{1,0:T(8,128)(2,1)S(1)} %merge.1.refs_0_, bf16[128,512]{1,0:T(8,128)(2,1)S(1)} %collective-permute-done.6.refs_1_, bf16[2048,2048]{1,0:T(8,128)(2,1)S(1)} %bitcast.6), custom_call_target="tpu_custom_call" | custom-call | flops 536870912 | bytes 8388608 | tf_op jit(solution)/shard_map/project/pallas_call | solution.py:342
  36.2 5.7 %collective-permute-done.7.refs_0_ = bf16[128,512]{1,0:T(8,128)(2,1)S(1)} collective-permute-done((bf16[128,512]{1,0:T(8,128)(2,1)S(1)}, bf16[128,512]{1,0:T(8,128)(2,1)S(1)}, u32[]{:S(2)}, u32[]{:S(2)}) %collective-permute-start.7) | collective-permute-done | bytes 131104 | tf_op jit(solution)/shard_map/ppermute | solution.py:19
  43.3 2.0 %collective-permute-start = (bf16[16,1152]{1,0:T(8,128)(2,1)S(1)}, bf16[16,1152]{1,0:T(8,128)(2,1)S(1)}, u32[]{:S(2)}, u32[]{:S(2)}) collective-permute-start(bf16[16,1152]{1,0:T(8,128)(2,1)S(1)} %get-tuple-element.37), channel_id=1, source_target_pairs={{0,1},{1,0},{2,3},{3,2},{4,5},{5,4},{6,7},{7,6},{8,9},{9,8},{10,11... | collective-permute-start | bytes 110600 | tf_op jit(solution)/shard_map/ppermute | solution.py:19
  47.0 1.2 %collective-permute-done.10.got_ref = bf16[2,32,2048]{2,1,0:T(8,128)(2,1)S(1)} collective-permute-done((bf16[2,32,2048]{2,1,0:T(8,128)(2,1)S(1)}, bf16[2,32,2048]{2,1,0:T(8,128)(2,1)S(1)}, u32[]{:S(2)}, u32[]{:S(2)}) %collective-permute-start.10) | collective-permute-done | bytes 262176 | tf_op jit(solution)/shard_map/ppermute | solution.py:19
  48.8 1.4 %collective-permute-start.2 = (bf16[16,1152]{1,0:T(8,128)(2,1)S(1)}, bf16[16,1152]{1,0:T(8,128)(2,1)S(1)}, u32[]{:S(2)}, u32[]{:S(2)}) collective-permute-start(bf16[16,1152]{1,0:T(8,128)(2,1)S(1)} %get-tuple-element.39), channel_id=1, source_target_pairs={{0,3},{1,2},{2,1},{3,0},{4,7},{5,6},{6,5},{7,4},{8,11},{9,10},{10,... | collective-permute-start | bytes 110600 | tf_op jit(solution)/shard_map/ppermute | solution.py:19
  50.2 3.6 %collective-permute-done.11.refs_0_ = bf16[32,2048]{1,0:T(8,128)(2,1)S(1)} collective-permute-done((bf16[32,2048]{1,0:T(8,128)(2,1)S(1)}, bf16[32,2048]{1,0:T(8,128)(2,1)S(1)}, u32[]{:S(2)}, u32[]{:S(2)}) %collective-permute-start.11) | collective-permute-done | bytes 131104 | tf_op jit(solution)/shard_map/ppermute | solution.py:19
  55.0 2.0 %collective-permute-start.14 = (bf16[8,1664]{1,0:T(8,128)(2,1)S(1)}, bf16[8,1664]{1,0:T(8,128)(2,1)S(1)}, u32[]{:S(2)}, u32[]{:S(2)}) collective-permute-start(bf16[8,1664]{1,0:T(8,128)(2,1)S(1)} %get-tuple-element.60), channel_id=1, source_target_pairs={{0,1},{1,0},{2,3},{3,2},{4,5},{5,4},{6,7},{7,6},{8,9},{9,8},{10,11... | collective-permute-start | bytes 79880 | tf_op jit(solution)/shard_map/ppermute | solution.py:19
  57.0 2.4 %collective-permute-start.16 = (bf16[8,1664]{1,0:T(8,128)(2,1)S(1)}, bf16[8,1664]{1,0:T(8,128)(2,1)S(1)}, u32[]{:S(2)}, u32[]{:S(2)}) collective-permute-start(bf16[8,1664]{1,0:T(8,128)(2,1)S(1)} %get-tuple-element.62), channel_id=1, source_target_pairs={{0,3},{1,2},{2,1},{3,0},{4,7},{5,6},{6,5},{7,4},{8,11},{9,10},{10,... | collective-permute-start | bytes 79880 | tf_op jit(solution)/shard_map/ppermute | solution.py:19
  60.1 1.6 %collective-permute-done.15.refs_6_ = bf16[8,1664]{1,0:T(8,128)(2,1)S(1)} collective-permute-done((bf16[8,1664]{1,0:T(8,128)(2,1)S(1)}, bf16[8,1664]{1,0:T(8,128)(2,1)S(1)}, u32[]{:S(2)}, u32[]{:S(2)}) %collective-permute-start.15) | collective-permute-done | bytes 26656 | tf_op jit(solution)/shard_map/ppermute | solution.py:19
  62.6 3.9 %sweeps.1 = (bf16[16,1152]{1,0:T(8,128)(2,1)S(1)}, bf16[16,1152]{1,0:T(8,128)(2,1)S(1)}, bf16[16,1152]{1,0:T(8,128)(2,1)S(1)}, bf16[16,1152]{1,0:T(8,128)(2,1)S(1)}) custom-call(f32[16]{0:T(128)S(1)} %pad_maximum_fusion.1.steps, f32[4,8,1152]{2,1,0:T(8,128)S(1)} %bitcast.8, f32[8,1536]{1,0:T(8,128)S(1)} %pad_maximum_fusion.embed_ref, ...), custom_call_target="tpu_custom_call" | custom-call | flops 1132462080 | bytes 7077888 | tf_op jit(solution)/shard_map/sweeps/pallas_call | solution.py:555
  66.6 3.0 %collective-permute-start.18 = (bf16[16,1152]{1,0:T(8,128)(2,1)S(1)}, bf16[16,1152]{1,0:T(8,128)(2,1)S(1)}, u32[]{:S(2)}, u32[]{:S(2)}) collective-permute-start(bf16[16,1152]{1,0:T(8,128)(2,1)S(1)} %get-tuple-element.65), channel_id=1, source_target_pairs={{0,2},{1,3},{2,0},{3,1},{4,6},{5,7},{6,4},{7,5},{8,10},{9,11},{10,... | collective-permute-start | bytes 110600 | tf_op jit(solution)/shard_map/ppermute | solution.py:19
  69.6 1.4 %collective-permute-start.19 = (bf16[16,1152]{1,0:T(8,128)(2,1)S(1)}, bf16[16,1152]{1,0:T(8,128)(2,1)S(1)}, u32[]{:S(2)}, u32[]{:S(2)}) collective-permute-start(bf16[16,1152]{1,0:T(8,128)(2,1)S(1)} %get-tuple-element.66), channel_id=1, source_target_pairs={{0,3},{1,2},{2,1},{3,0},{4,7},{5,6},{6,5},{7,4},{8,11},{9,10},{10,... | collective-permute-start | bytes 110600 | tf_op jit(solution)/shard_map/ppermute | solution.py:19
  72.0 3.4 %collective-permute-done.19.refs_3_ = bf16[16,1152]{1,0:T(8,128)(2,1)S(1)} collective-permute-done((bf16[16,1152]{1,0:T(8,128)(2,1)S(1)}, bf16[16,1152]{1,0:T(8,128)(2,1)S(1)}, u32[]{:S(2)}, u32[]{:S(2)}) %collective-permute-start.19) | collective-permute-done | bytes 36896 | tf_op jit(solution)/shard_map/ppermute | solution.py:19
  (59 shorter events, 11.7 us)
Async XLA Ops:
  0.0 42.8 %collective-permute-start.9 = (bf16[2048,384]{1,0:T(8,128)(2,1)}, bf16[2048,384]{1,0:T(8,128)(2,1)S(1)}, u32[]{:S(2)}, u32[]{:S(2)}) collective-permute-start(bf16[2048,384]{1,0:T(8,128)(2,1)} %refs_1_.1), channel_id=1, source_target_pairs={{0,8},{4,12},{8,0},{12,4},{1,9},{5,13},{9,1},{13,5},{2,10},{6,14},... | collective-permute-start | bytes 4718600 | tf_op jit(solution)/shard_map/ppermute | solution.py:19
  3.6 31.0 %slice-start = ((s8[8388608]{0:T(1024)(128)(4,1)}), s8[4194304]{0:T(1024)(128)(4,1)S(1)}, s32[]{:S(2)}) async-start(s8[8388608]{0:T(1024)(128)(4,1)} %bitcast.5), calls=%async_computation | async-start | bytes 8388608
  5.7 28.9 %slice-start.1 = ((s8[8388608]{0:T(1024)(128)(4,1)}), s8[4194304]{0:T(1024)(128)(4,1)S(1)}, s32[]{:S(2)}) async-start(s8[8388608]{0:T(1024)(128)(4,1)} %bitcast.5), calls=%async_computation.1 | async-start | bytes 8388608
  9.5 23.2 %copy-start.2 = (bf16[2048,384]{1,0:T(8,128)(2,1)S(1)}, bf16[2048,384]{1,0:T(8,128)(2,1)}, u32[]{:S(2)}) copy-start(bf16[2048,384]{1,0:T(8,128)(2,1)} %refs_1_.1) | copy-start | bytes 4718596
  12.7 6.9 %collective-permute-start.3 = (bf16[136,512]{1,0:T(8,128)(2,1)S(1)}, bf16[136,512]{1,0:T(8,128)(2,1)S(1)}, u32[]{:S(2)}, u32[]{:S(2)}) collective-permute-start(bf16[136,512]{1,0:T(8,128)(2,1)S(1)} %get-tuple-element.48), channel_id=1, source_target_pairs={{0,1},{1,0},{2,3},{3,2},{4,5},{5,4},{6,7},{7,6},{8,9},{9,8},{10,11... | collective-permute-start | bytes 417800 | tf_op jit(solution)/shard_map/ppermute | solution.py:19
  14.3 13.3 %collective-permute-start.4 = (bf16[136,512]{1,0:T(8,128)(2,1)S(1)}, bf16[136,512]{1,0:T(8,128)(2,1)S(1)}, u32[]{:S(2)}, u32[]{:S(2)}) collective-permute-start(bf16[136,512]{1,0:T(8,128)(2,1)S(1)} %get-tuple-element.49), channel_id=1, source_target_pairs={{0,2},{1,3},{2,0},{3,1},{4,6},{5,7},{6,4},{7,5},{8,10},{9,11},{10,... | collective-permute-start | bytes 417800 | tf_op jit(solution)/shard_map/ppermute | solution.py:19
  16.9 10.7 %collective-permute-start.5 = (bf16[136,512]{1,0:T(8,128)(2,1)S(1)}, bf16[136,512]{1,0:T(8,128)(2,1)S(1)}, u32[]{:S(2)}, u32[]{:S(2)}) collective-permute-start(bf16[136,512]{1,0:T(8,128)(2,1)S(1)} %get-tuple-element.50), channel_id=1, source_target_pairs={{0,3},{1,2},{2,1},{3,0},{4,7},{5,6},{6,5},{7,4},{8,11},{9,10},{10,... | collective-permute-start | bytes 417800 | tf_op jit(solution)/shard_map/ppermute | solution.py:19
  28.1 6.5 %collective-permute-start.6 = (bf16[128,512]{1,0:T(8,128)(2,1)S(1)}, bf16[128,512]{1,0:T(8,128)(2,1)S(1)}, u32[]{:S(2)}, u32[]{:S(2)}) collective-permute-start(bf16[128,512]{1,0:T(8,128)(2,1)S(1)} %merge.1.refs_0_), channel_id=1, source_target_pairs={{0,1},{1,0},{2,3},{3,2},{4,5},{5,4},{6,7},{7,6},{8,9},{9,8},{10,11... | collective-permute-start | bytes 393224 | tf_op jit(solution)/shard_map/ppermute | solution.py:19
  30.2 11.7 %collective-permute-start.7 = (bf16[128,512]{1,0:T(8,128)(2,1)S(1)}, bf16[128,512]{1,0:T(8,128)(2,1)S(1)}, u32[]{:S(2)}, u32[]{:S(2)}) collective-permute-start(bf16[128,512]{1,0:T(8,128)(2,1)S(1)} %merge.1.refs_0_), channel_id=1, source_target_pairs={{0,2},{1,3},{2,0},{3,1},{4,6},{5,7},{6,4},{7,5},{8,10},{9,11},{10,... | collective-permute-start | bytes 393224 | tf_op jit(solution)/shard_map/ppermute | solution.py:19
  31.3 10.6 %collective-permute-start.8 = (bf16[128,512]{1,0:T(8,128)(2,1)S(1)}, bf16[128,512]{1,0:T(8,128)(2,1)S(1)}, u32[]{:S(2)}, u32[]{:S(2)}) collective-permute-start(bf16[128,512]{1,0:T(8,128)(2,1)S(1)} %merge.1.refs_0_), channel_id=1, source_target_pairs={{0,3},{1,2},{2,1},{3,0},{4,7},{5,6},{6,5},{7,4},{8,11},{9,10},{10,... | collective-permute-start | bytes 393224 | tf_op jit(solution)/shard_map/ppermute | solution.py:19
  32.7 16.1 %collective-permute-start.12 = (bf16[2048,384]{1,0:T(8,128)(2,1)S(1)}, bf16[2048,384]{1,0:T(8,128)(2,1)S(1)}, u32[]{:S(2)}, u32[]{:S(2)}) collective-permute-start(bf16[2048,384]{1,0:T(8,128)(2,1)S(1)} %copy-done.2), channel_id=1, source_target_pairs={{0,4},{4,0},{8,12},{12,8},{1,5},{5,1},{9,13},{13,9},{2,6},{6,2},{1... | collective-permute-start | bytes 4718600 | tf_op jit(solution)/shard_map/ppermute | solution.py:19
  36.2 17.6 %copy-start.5 = (bf16[128,2048]{1,0:T(8,128)(2,1)S(1)}, bf16[128,2048]{1,0:T(8,128)(2,1)}, u32[]{:S(2)}) copy-start(bf16[128,2048]{1,0:T(8,128)(2,1)} %param.17) | copy-start | bytes 1572868
  42.9 11.0 %collective-permute-start.13 = (bf16[2048,384]{1,0:T(8,128)(2,1)S(1)}, bf16[2048,384]{1,0:T(8,128)(2,1)S(1)}, u32[]{:S(2)}, u32[]{:S(2)}) collective-permute-start(bf16[2048,384]{1,0:T(8,128)(2,1)S(1)} %collective-permute-done.9.refs_3_), channel_id=1, source_target_pairs={{0,4},{4,0},{8,12},{12,8},{1,5},{5,1},{9,13},{13,9},{2,6},{6,2},{1... | collective-permute-start | bytes 4718600 | tf_op jit(solution)/shard_map/ppermute | solution.py:19
  43.3 13.6 %collective-permute-start = (bf16[16,1152]{1,0:T(8,128)(2,1)S(1)}, bf16[16,1152]{1,0:T(8,128)(2,1)S(1)}, u32[]{:S(2)}, u32[]{:S(2)}) collective-permute-start(bf16[16,1152]{1,0:T(8,128)(2,1)S(1)} %get-tuple-element.37), channel_id=1, source_target_pairs={{0,1},{1,0},{2,3},{3,2},{4,5},{5,4},{6,7},{7,6},{8,9},{9,8},{10,11... | collective-permute-start | bytes 110600 | tf_op jit(solution)/shard_map/ppermute | solution.py:19
  45.3 14.7 %collective-permute-start.1 = (bf16[16,1152]{1,0:T(8,128)(2,1)S(1)}, bf16[16,1152]{1,0:T(8,128)(2,1)S(1)}, u32[]{:S(2)}, u32[]{:S(2)}) collective-permute-start(bf16[16,1152]{1,0:T(8,128)(2,1)S(1)} %get-tuple-element.38), channel_id=1, source_target_pairs={{0,2},{1,3},{2,0},{3,1},{4,6},{5,7},{6,4},{7,5},{8,10},{9,11},{10,... | collective-permute-start | bytes 110600 | tf_op jit(solution)/shard_map/ppermute | solution.py:19
  46.6 1.5 %collective-permute-start.10 = (bf16[2,32,2048]{2,1,0:T(8,128)(2,1)S(1)}, bf16[2,32,2048]{2,1,0:T(8,128)(2,1)S(1)}, u32[]{:S(2)}, u32[]{:S(2)}) collective-permute-start(bf16[2,32,2048]{2,1,0:T(8,128)(2,1)S(1)} %get-tuple-element.55), channel_id=1, source_target_pairs={{0,4},{4,0},{8,12},{12,8},{1,5},{5,1},{9,13},{13,9},{2,6},{6,2},{1... | collective-permute-start | bytes 786440 | tf_op jit(solution)/shard_map/ppermute | solution.py:19
  48.2 5.7 %collective-permute-start.11 = (bf16[32,2048]{1,0:T(8,128)(2,1)S(1)}, bf16[32,2048]{1,0:T(8,128)(2,1)S(1)}, u32[]{:S(2)}, u32[]{:S(2)}) collective-permute-start(bf16[32,2048]{1,0:T(8,128)(2,1)S(1)} %get-tuple-element.57), channel_id=1, source_target_pairs={{0,8},{4,12},{8,0},{12,4},{1,9},{5,13},{9,1},{13,5},{2,10},{6,14},... | collective-permute-start | bytes 393224 | tf_op jit(solution)/shard_map/ppermute | solution.py:19
  48.8 11.3 %collective-permute-start.2 = (bf16[16,1152]{1,0:T(8,128)(2,1)S(1)}, bf16[16,1152]{1,0:T(8,128)(2,1)S(1)}, u32[]{:S(2)}, u32[]{:S(2)}) collective-permute-start(bf16[16,1152]{1,0:T(8,128)(2,1)S(1)} %get-tuple-element.39), channel_id=1, source_target_pairs={{0,3},{1,2},{2,1},{3,0},{4,7},{5,6},{6,5},{7,4},{8,11},{9,10},{10,... | collective-permute-start | bytes 110600 | tf_op jit(solution)/shard_map/ppermute | solution.py:19
  55.0 5.1 %collective-permute-start.14 = (bf16[8,1664]{1,0:T(8,128)(2,1)S(1)}, bf16[8,1664]{1,0:T(8,128)(2,1)S(1)}, u32[]{:S(2)}, u32[]{:S(2)}) collective-permute-start(bf16[8,1664]{1,0:T(8,128)(2,1)S(1)} %get-tuple-element.60), channel_id=1, source_target_pairs={{0,1},{1,0},{2,3},{3,2},{4,5},{5,4},{6,7},{7,6},{8,9},{9,8},{10,11... | collective-permute-start | bytes 79880 | tf_op jit(solution)/shard_map/ppermute | solution.py:19
  56.9 4.7 %collective-permute-start.15 = (bf16[8,1664]{1,0:T(8,128)(2,1)S(1)}, bf16[8,1664]{1,0:T(8,128)(2,1)S(1)}, u32[]{:S(2)}, u32[]{:S(2)}) collective-permute-start(bf16[8,1664]{1,0:T(8,128)(2,1)S(1)} %get-tuple-element.61), channel_id=1, source_target_pairs={{0,2},{1,3},{2,0},{3,1},{4,6},{5,7},{6,4},{7,5},{8,10},{9,11},{10,... | collective-permute-start | bytes 79880 | tf_op jit(solution)/shard_map/ppermute | solution.py:19
  57.0 5.6 %collective-permute-start.16 = (bf16[8,1664]{1,0:T(8,128)(2,1)S(1)}, bf16[8,1664]{1,0:T(8,128)(2,1)S(1)}, u32[]{:S(2)}, u32[]{:S(2)}) collective-permute-start(bf16[8,1664]{1,0:T(8,128)(2,1)S(1)} %get-tuple-element.62), channel_id=1, source_target_pairs={{0,3},{1,2},{2,1},{3,0},{4,7},{5,6},{6,5},{7,4},{8,11},{9,10},{10,... | collective-permute-start | bytes 79880 | tf_op jit(solution)/shard_map/ppermute | solution.py:19
  66.6 4.5 %collective-permute-start.17 = (bf16[16,1152]{1,0:T(8,128)(2,1)S(1)}, bf16[16,1152]{1,0:T(8,128)(2,1)S(1)}, u32[]{:S(2)}, u32[]{:S(2)}) collective-permute-start(bf16[16,1152]{1,0:T(8,128)(2,1)S(1)} %get-tuple-element.64), channel_id=1, source_target_pairs={{0,1},{1,0},{2,3},{3,2},{4,5},{5,4},{6,7},{7,6},{8,9},{9,8},{10,11... | collective-permute-start | bytes 110600 | tf_op jit(solution)/shard_map/ppermute | solution.py:19
  66.6 5.3 %collective-permute-start.18 = (bf16[16,1152]{1,0:T(8,128)(2,1)S(1)}, bf16[16,1152]{1,0:T(8,128)(2,1)S(1)}, u32[]{:S(2)}, u32[]{:S(2)}) collective-permute-start(bf16[16,1152]{1,0:T(8,128)(2,1)S(1)} %get-tuple-element.65), channel_id=1, source_target_pairs={{0,2},{1,3},{2,0},{3,1},{4,6},{5,7},{6,4},{7,5},{8,10},{9,11},{10,... | collective-permute-start | bytes 110600 | tf_op jit(solution)/shard_map/ppermute | solution.py:19
  69.6 5.8 %collective-permute-start.19 = (bf16[16,1152]{1,0:T(8,128)(2,1)S(1)}, bf16[16,1152]{1,0:T(8,128)(2,1)S(1)}, u32[]{:S(2)}, u32[]{:S(2)}) collective-permute-start(bf16[16,1152]{1,0:T(8,128)(2,1)S(1)} %get-tuple-element.66), channel_id=1, source_target_pairs={{0,3},{1,2},{2,1},{3,0},{4,7},{5,6},{6,5},{7,4},{8,11},{9,10},{10,... | collective-permute-start | bytes 110600 | tf_op jit(solution)/shard_map/ppermute | solution.py:19
  (8 other events, 55.6 us)

commit v7 on v6

--- a/solution.py
+++ b/solution.py
@@ -43,7 +43,8 @@
 SMEM = pl.BlockSpec(memory_space=pltpu.SMEM)
 HBM = pl.BlockSpec(memory_space=pltpu.HBM)
 PIECES = 3
-ATTEND_MIB = 44
+FIRST_MIB = 50
+NEXT_MIB = 46
 
 
 def pieces_of(value):
@@ -195,23 +196,70 @@
         copy.wait()
 
 
-def attend_near_kernel(groups, share, per_copy, joined, *refs):
+def attend_near_kernel(groups, fresh, later, share, per_copy, row_cuts, joined, *refs):
     length_ref, cos_ref, sin_ref, q_ref, k_ref, v_ref = refs[:6]
-    n = len(groups)
-    outs, stats = refs[6 : 6 + n], [] if joined else refs[6 + n :]
+    refs = refs[6:]
+    hbm, refs = (refs[:3], refs[3:]) if fresh or later else ([], refs)
+    n = len(groups) + len(fresh)
+    outs, refs = refs[:n], refs[n:]
+    stats, refs = ([], refs) if joined else (refs[:n], refs[n:])
+    kept, refs = (refs[:3], refs[3:]) if later else ([], refs)
+    parts = share // per_copy
+    copies, waiting = [], {}
+    if hbm:
+        sem = refs[-1]
+        own = lax.axis_index("tm") // row_cuts
+        for to, call in ((refs[:3] if fresh else [], fresh), (kept, later)):
+            for g, a in enumerate(call):
+                first = pl.multiple_of((own ^ a) * share * HD, HD)
+                for part in range(parts):
+                    slot = g * parts + part
+                    column = pl.multiple_of(first + part * per_copy * HD, HD)
+                    wanted = [(hbm[0].at[:, pl.ds(first, share * HD)], to[0].at[g])] * (part == 0)
+                    for from_ref, to_ref in zip(hbm[1:], to[1:]):
+                        wanted.append(
+                            (from_ref.at[:, pl.ds(column, per_copy * HD)], to_ref.at[slot])
+                        )
+                    started = []
+                    for pair in wanted:
+                        copies.append(pltpu.make_async_copy(*pair, sem.at[len(copies)]))
+                        copies[-1].start()
+                        started.append(copies[-1])
+                    if call is fresh:
+                        waiting[len(groups) * parts + slot] = started
+    late = copies[sum(len(started) for started in waiting.values()) :]
+    near_slots = len(groups) * parts
+
+    def arrive(slot):
+        for copy in waiting.pop(slot, []):
+            copy.wait()
+
+    def query(g, at):
+        arrive(g * parts)
+        return q_ref[g, :, at] if g < len(groups) else refs[0][g - len(groups), :, at]
+
+    def reader(near_ref, index):
+        def read(slot, at):
+            arrive(slot)
+            return near_ref[slot, :, at] if slot < near_slots else refs[index][slot - near_slots, :, at]
+
+        return read
+
     attend_heads(
-        groups,
+        (*groups, *fresh),
         share,
         per_copy,
         valid_keys(length_ref, k_ref.shape[1]),
-        lambda g, at: q_ref[g, :, at],
-        lambda slot, at: k_ref[slot, :, at],
-        lambda slot, at: v_ref[slot, :, at],
+        query,
+        reader(k_ref, 1),
+        reader(v_ref, 2),
         cos_ref,
         sin_ref,
         outs,
         stats,
     )
+    for copy in late:
+        copy.wait()
 
 
 def attend(queries, keys, values, positions, cache_length, calls, share, row_cuts):
@@ -242,37 +290,61 @@
     def found(result, n):
         return list(zip(result[:n], [None] * n if joined else result[n : 2 * n]))
 
+    split = [(call[:1], call[1:]) for call in calls[1:]]
     n = len(calls[0])
+    nearby = split[0][0] if split else []
     out_shape = blocks(n) + [table] * 2
-    for call in calls[1:]:
-        out_shape = out_shape + [jax.ShapeDtypeStruct(*entry) for entry in near(len(call))]
-    count = sum(len(call) for call in calls) * (1 + 2 * share // per_copy)
+    if nearby:
+        out_shape = out_shape + [jax.ShapeDtypeStruct(*entry) for entry in near(len(nearby))]
+    count = (n + len(nearby)) * (1 + 2 * share // per_copy)
     result = pl.pallas_call(
-        functools.partial(attend_kernel, calls, share, per_copy, row_cuts, joined),
+        functools.partial(
+            attend_kernel,
+            [calls[0], nearby] if nearby else [calls[0]],
+            share,
+            per_copy,
+            row_cuts,
+            joined,
+        ),
         in_specs=[SMEM, VMEM] + [HBM] * 3,
         out_specs=[VMEM] * len(out_shape),
         out_shape=out_shape,
         scratch_shapes=[pltpu.VMEM(*entry) for entry in near(n)]
         + [pltpu.SemaphoreType.DMA((count,))],
         cost_estimate=price(n),
-        compiler_params=mib(ATTEND_MIB),
+        compiler_params=mib(FIRST_MIB),
         name="attend",
     )(cache_length, positions[None], queries, keys, values)
     skip = len(blocks(n))
     tables, kept = result[skip : skip + 2], result[skip + 2 :]
     blocks_of = [found(result, n)]
-    for c, call in enumerate(calls[1:]):
-        n = len(call)
+    for c, (groups, fresh) in enumerate(split):
+        later = split[c + 1][0] if c + 1 < len(split) else []
+        n = len(groups) + len(fresh)
+        moving = bool(fresh or later)
+        out_shape = blocks(n)
+        scratch = []
+        if later:
+            out_shape = out_shape + [jax.ShapeDtypeStruct(*entry) for entry in near(len(later))]
+        if fresh:
+            scratch = [pltpu.VMEM(*entry) for entry in near(len(fresh))]
+        if moving:
+            count = (len(fresh) + len(later)) * (1 + 2 * share // per_copy)
+            scratch = scratch + [pltpu.SemaphoreType.DMA((count,))]
         result = pl.pallas_call(
-            functools.partial(attend_near_kernel, call, share, per_copy, joined),
-            in_specs=[SMEM] + [VMEM] * 5,
-            out_specs=[VMEM] * len(blocks(n)),
-            out_shape=blocks(n),
+            functools.partial(
+                attend_near_kernel, groups, fresh, later, share, per_copy, row_cuts, joined
+            ),
+            in_specs=[SMEM] + [VMEM] * 5 + [HBM] * 3 * moving,
+            out_specs=[VMEM] * len(out_shape),
+            out_shape=out_shape,
+            scratch_shapes=scratch,
             cost_estimate=price(n),
-            compiler_params=mib(16),
+            compiler_params=mib(NEXT_MIB if moving else 16),
             name="attend_near",
-        )(cache_length, *tables, *kept[3 * c : 3 * c + 3])
+        )(cache_length, *tables, *kept, *([queries, keys, values] if moving else []))
         blocks_of.append(found(result, n))
+        kept = result[len(blocks(n)) :]
     return blocks_of
 
 
@@ -317,7 +389,16 @@
     )(*outs, *stats)
 
 
-def project_kernel(cuts, later, row_cuts, *refs):
+def core_order(part, chips):
+    core = lax.axis_index("heads") % 2
+    rows = part.shape[0] // (2 * chips)
+    firsts = [
+        pl.multiple_of((2 * chip + c) * rows, rows) for c in (core, 1 - core) for chip in range(chips)
+    ]
+    return jnp.concatenate([part[pl.ds(first, rows), :] for first in firsts], axis=0)
+
+
+def project_kernel(cuts, later, row_cuts, chips, *refs):
     parts, refs = refs[: len(cuts)], refs[len(cuts) :]
     w_hbm, total_ref, kept_ref, w_buf, sem = refs
     own = lax.axis_index("tm") // row_cuts
@@ -330,17 +411,19 @@
         copies[i].start()
     for i, part in enumerate(parts):
         copies[i].wait()
-        product = jnp.dot(part[...], w_buf[i], preferred_element_type=jnp.float32)
+        product = jnp.dot(
+            core_order(part, chips), w_buf[i], preferred_element_type=jnp.float32
+        )
         total_ref[...] = product + total_ref[...] if i else product
     for copy in copies[len(cuts) :]:
         copy.wait()
 
 
-def project(parts, cuts, later, weight, row_cuts):
+def project(parts, cuts, later, weight, row_cuts, chips):
     rows, depth = parts[0].shape
     columns = weight.shape[1]
     return pl.pallas_call(
-        functools.partial(project_kernel, cuts, later, row_cuts),
+        functools.partial(project_kernel, cuts, later, row_cuts, chips),
         in_specs=[VMEM] * len(parts) + [HBM],
         out_specs=[VMEM, VMEM],
         out_shape=[
@@ -358,18 +441,17 @@
 
 
 def project_rest_kernel(count, total_ref, kept_ref, *refs):
-    parts, (keep_ref, send_ref, whole_ref) = refs[:count], refs[count:]
+    parts, (keep_ref, send_ref) = refs[:count], refs[count:]
+    chips, rows = keep_ref.shape[:2]
     value = total_ref[...]
     for i, part in enumerate(parts):
-        value = value + jnp.dot(part[...], kept_ref[i], preferred_element_type=jnp.float32)
-    chips, rows = keep_ref.shape[:2]
-    core = lax.axis_index("heads") % 2
+        value = value + jnp.dot(
+            core_order(part, chips), kept_ref[i], preferred_element_type=jnp.float32
+        )
     for chip in range(chips):
-        for c in range(2):
-            first = (2 * chip + c) * rows
-            whole_ref[c, chip] = value[first : first + rows]
-    keep_ref[...] = whole_ref[core]
-    send_ref[...] = whole_ref[1 - core].astype(jnp.bfloat16)
+        keep_ref[chip] = value[chip * rows : (chip + 1) * rows]
+        other = (chips + chip) * rows
+        send_ref[chip] = value[other : other + rows].astype(jnp.bfloat16)
 
 
 def project_rest(total, kept, parts, chips):
@@ -383,7 +465,6 @@
             jax.ShapeDtypeStruct(block, jnp.float32),
             jax.ShapeDtypeStruct(block, jnp.bfloat16),
         ],
-        scratch_shapes=[pltpu.VMEM((2, *block), jnp.float32)],
         cost_estimate=cost(2 * rows * columns * kept.shape[0] * kept.shape[1], 0, kept),
         compiler_params=mib(16),
         name="project_rest",
@@ -687,7 +768,7 @@
         by_cut.append(part)
     half = max(1, head_cuts // 2)
     cuts = list(range(head_cuts))
-    total, kept = project(by_cut[:half], cuts[:half], cuts[half:], out_weight, row_cuts)
+    total, kept = project(by_cut[:half], cuts[:half], cuts[half:], out_weight, row_cuts, chips)
     keep, send = project_rest(total, kept, by_cut[half:], chips)
 
     far, send = lax.optimization_barrier((far, send))

time: 76.4 us -> 78.7 us (1.030)
  local copies, waits for them, and re-layouts: 2.11 us -> 4.63 us
    unnamed x24 -> x34, local copies, waits for them, and re-layouts: 2.11 us -> 4.63 us
  transfers between devices with their start and end apart: 20 -> 20, of which waited for: 10 -> 10; matrix products, arithmetic and copies ran while one was open for 0% -> 0% of each run, Pallas kernels for 18% -> 17%
where the time goes in v7:
time: 78.7 us; the launch traced here: 78.5 us
  waiting for transfers between devices  28.1 us (36%)
  starting transfers between devices  26.4 us (34%)
  Pallas kernels  18.1 us (23%)
  local copies, waits for them, and re-layouts  4.63 us (6%)
  between operations  0.87 us (1%)
    ppermute x20, waiting for transfers between devices, swap(): return lax.ppermute(values, axis, [(i, i ^ distance) for i in range(size)])  28.1 us
    ppermute x20, starting transfers between devices, swap(): return lax.ppermute(values, axis, [(i, i ^ distance) for i in range(size)])  26.4 us
    pallas_call x2, Pallas kernels, attend(): pl.pallas_call(functools.partial(attend_near_kernel, groups, fresh, later...  5.21 us
    unnamed x34, local copies, waits for them, and re-layouts  4.63 us
    pallas_call x1, Pallas kernels, sweep_all(): pl.pallas_call(functools.partial(sweep_kernel, (n_tm, time_each, rows, mo...  3.93 us
    pallas_call x1, Pallas kernels, attend(): pl.pallas_call(functools.partial(attend_kernel, [calls[0], nearby] if nea...  3.29 us
    pallas_call x1, Pallas kernels, project(): pl.pallas_call(functools.partial(project_kernel, cuts, later, row_cuts, c...  1.58 us
  transfers between devices with their start and end apart: 20, of which 10 were waited for; matrix products, arithmetic and copies ran while one was open for 0% of the time, Pallas kernels for 17%

profile of v7, /device:TPU:0, one launch (start us, length us, event | category | flops | bytes accessed | tf_op | source)
XLA Modules:
  0.0 78.5 jit_solution(13555181334259807189)
XLA Ops:
  0.0 3.0 %collective-permute-start.9 = (bf16[2048,384]{1,0:T(8,128)(2,1)}, bf16[2048,384]{1,0:T(8,128)(2,1)S(1)}, u32[]{:S(2)}, u32[]{:S(2)}) collective-permute-start(bf16[2048,384]{1,0:T(8,128)(2,1)} %refs_1_.1), channel_id=1, source_target_pairs={{0,8},{4,12},{8,0},{12,4},{1,9},{5,13},{9,1},{13,5},{2,10},{6,14},... | collective-permute-start | bytes 4718600 | tf_op jit(solution)/shard_map/ppermute | solution.py:19
  5.3 3.3 %attend.1 = (bf16[136,512]{1,0:T(8,128)(2,1)S(1)}, f32[128,128]{1,0:T(8,128)S(1)}, f32[128,128]{1,0:T(8,128)S(1)}, bf16[1,128,512]{2,1,0:T(8,128)(2,1)S(1)}, bf1...) custom-call(s32[1]{0:T(128)S(6)} %copy.15.refs_0_, s32[1,128]{1,0:T(1,128)S(1)} %bitcast.13, ...), custom_call_target="tpu_custom_call" | custom-call | flops 268435456 | bytes 2097152 | tf_op jit(solution)/shard_map/attend/pallas_call | solution.py:300
  10.3 1.2 %copy-done.7 = bf16[2,1024,256]{2,1,0:T(8,128)(2,1)S(1)} copy-done((bf16[2,1024,256]{2,1,0:T(8,128)(2,1)S(1)}, bf16[2,1024,256]{2,1,0:T(8,128)(2,1)}, u32[]{:S(2)}) %copy-start.7) | copy-done | bytes 1048600
  11.5 3.6 %attend_near.2 = (bf16[136,512]{1,0:T(8,128)(2,1)S(1)}, bf16[136,512]{1,0:T(8,128)(2,1)S(1)}, bf16[1,128,512]{2,1,0:T(8,128)(2,1)S(1)}, bf16[2,1024,256]{2,1,0:T(8,128)(2,1)S(1)}, bf16[2,1024,256]{2,1,0:T(8,128)(2,1)S(1)}) custom-call(s32[1]{0:T(128)S(6)} %copy.15.refs_0_, f32[128,128]{1,0:T(8,128)S(1)} %get-tuple-element.40.refs_1_, ...), custom_call_target="tpu_custom_call" | custom-call | flops 536870912 | bytes 4194304 | tf_op jit(solution)/shard_map/attend_near/pallas_call | solution.py:334
  15.1 1.7 %collective-permute-start.3 = (bf16[136,512]{1,0:T(8,128)(2,1)S(1)}, bf16[136,512]{1,0:T(8,128)(2,1)S(1)}, u32[]{:S(2)}, u32[]{:S(2)}) collective-permute-start(bf16[136,512]{1,0:T(8,128)(2,1)S(1)} %get-tuple-element.48), channel_id=1, source_target_pairs={{0,1},{1,0},{2,3},{3,2},{4,5},{5,4},{6,7},{7,6},{8,9},{9,8},{10,11... | collective-permute-start | bytes 417800 | tf_op jit(solution)/shard_map/ppermute | solution.py:19
  16.8 2.6 %collective-permute-start.4 = (bf16[136,512]{1,0:T(8,128)(2,1)S(1)}, bf16[136,512]{1,0:T(8,128)(2,1)S(1)}, u32[]{:S(2)}, u32[]{:S(2)}) collective-permute-start(bf16[136,512]{1,0:T(8,128)(2,1)S(1)} %get-tuple-element.49), channel_id=1, source_target_pairs={{0,2},{1,3},{2,0},{3,1},{4,6},{5,7},{6,4},{7,5},{8,10},{9,11},{10,... | collective-permute-start | bytes 417800 | tf_op jit(solution)/shard_map/ppermute | solution.py:19
  19.6 1.6 %attend_near.3.refs_0_ = bf16[136,512]{1,0:T(8,128)(2,1)S(1)} custom-call(s32[1]{0:T(128)S(6)} %copy.15.refs_0_, f32[128,128]{1,0:T(8,128)S(1)} %get-tuple-element.40.refs_1_, f32[128,128]{1,0:T(8,128)S(1)} %get-tuple-element.41.refs_2_, bf16[1,128,512]{2,1,0:T(8,128)(2,1)S(1)} %get-tuple-element.45.refs_3_, ...), custom_call_target="tpu_custom_call" | custom-call | flops 268435456 | bytes 2097152 | tf_op jit(solution)/shard_map/attend_near/pallas_call | solution.py:334
  22.0 8.0 %collective-permute-done.4.refs_2_ = bf16[136,512]{1,0:T(8,128)(2,1)S(1)} collective-permute-done((bf16[136,512]{1,0:T(8,128)(2,1)S(1)}, bf16[136,512]{1,0:T(8,128)(2,1)S(1)}, u32[]{:S(2)}, u32[]{:S(2)}) %collective-permute-start.4) | collective-permute-done | bytes 139296 | tf_op jit(solution)/shard_map/ppermute | solution.py:19
  30.5 2.1 %collective-permute-start.6 = (bf16[128,512]{1,0:T(8,128)(2,1)S(1)}, bf16[128,512]{1,0:T(8,128)(2,1)S(1)}, u32[]{:S(2)}, u32[]{:S(2)}) collective-permute-start(bf16[128,512]{1,0:T(8,128)(2,1)S(1)} %merge.1.refs_0_), channel_id=1, source_target_pairs={{0,1},{1,0},{2,3},{3,2},{4,5},{5,4},{6,7},{7,6},{8,9},{9,8},{10,11... | collective-permute-start | bytes 393224 | tf_op jit(solution)/shard_map/ppermute | solution.py:19
  33.7 1.4 %collective-permute-start.8 = (bf16[128,512]{1,0:T(8,128)(2,1)S(1)}, bf16[128,512]{1,0:T(8,128)(2,1)S(1)}, u32[]{:S(2)}, u32[]{:S(2)}) collective-permute-start(bf16[128,512]{1,0:T(8,128)(2,1)S(1)} %merge.1.refs_0_), channel_id=1, source_target_pairs={{0,3},{1,2},{2,1},{3,0},{4,7},{5,6},{6,5},{7,4},{8,11},{9,10},{10,... | collective-permute-start | bytes 393224 | tf_op jit(solution)/shard_map/ppermute | solution.py:19
  35.1 1.9 %collective-permute-done.6.refs_1_ = bf16[128,512]{1,0:T(8,128)(2,1)S(1)} collective-permute-done((bf16[128,512]{1,0:T(8,128)(2,1)S(1)}, bf16[128,512]{1,0:T(8,128)(2,1)S(1)}, u32[]{:S(2)}, u32[]{:S(2)}) %collective-permute-start.6) | collective-permute-done | bytes 131104 | tf_op jit(solution)/shard_map/ppermute | solution.py:19
  37.0 1.6 %project.1 = (f32[128,2048]{1,0:T(8,128)S(1)}, bf16[2,512,2048]{2,1,0:T(8,128)(2,1)S(1)}) custom-call(bf16[128,512]{1,0:T(8,128)(2,1)S(1)} %merge.1.refs_0_, bf16[128,512]{1,0:T(8,128)(2,1)S(1)} %collective-permute-done.6.refs_1_, bf16[2048,2048]{1,0:T(8,128)(2,1)S(1)} %bitcast.6), custom_call_target="tpu_custom_call" | custom-call | flops 536870912 | bytes 8388608 | tf_op jit(solution)/shard_map/project/pallas_call | solution.py:425
  38.6 5.7 %collective-permute-done.7.refs_0_ = bf16[128,512]{1,0:T(8,128)(2,1)S(1)} collective-permute-done((bf16[128,512]{1,0:T(8,128)(2,1)S(1)}, bf16[128,512]{1,0:T(8,128)(2,1)S(1)}, u32[]{:S(2)}, u32[]{:S(2)}) %collective-permute-start.7) | collective-permute-done | bytes 131104 | tf_op jit(solution)/shard_map/ppermute | solution.py:19
  45.6 2.0 %collective-permute-start = (bf16[16,1152]{1,0:T(8,128)(2,1)S(1)}, bf16[16,1152]{1,0:T(8,128)(2,1)S(1)}, u32[]{:S(2)}, u32[]{:S(2)}) collective-permute-start(bf16[16,1152]{1,0:T(8,128)(2,1)S(1)} %get-tuple-element.37), channel_id=1, source_target_pairs={{0,1},{1,0},{2,3},{3,2},{4,5},{5,4},{6,7},{7,6},{8,9},{9,8},{10,11... | collective-permute-start | bytes 110600 | tf_op jit(solution)/shard_map/ppermute | solution.py:19
  49.3 1.2 %collective-permute-done.10.got_ref = bf16[2,32,2048]{2,1,0:T(8,128)(2,1)S(1)} collective-permute-done((bf16[2,32,2048]{2,1,0:T(8,128)(2,1)S(1)}, bf16[2,32,2048]{2,1,0:T(8,128)(2,1)S(1)}, u32[]{:S(2)}, u32[]{:S(2)}) %collective-permute-start.10) | collective-permute-done | bytes 262176 | tf_op jit(solution)/shard_map/ppermute | solution.py:19
  51.1 1.4 %collective-permute-start.2 = (bf16[16,1152]{1,0:T(8,128)(2,1)S(1)}, bf16[16,1152]{1,0:T(8,128)(2,1)S(1)}, u32[]{:S(2)}, u32[]{:S(2)}) collective-permute-start(bf16[16,1152]{1,0:T(8,128)(2,1)S(1)} %get-tuple-element.39), channel_id=1, source_target_pairs={{0,3},{1,2},{2,1},{3,0},{4,7},{5,6},{6,5},{7,4},{8,11},{9,10},{10,... | collective-permute-start | bytes 110600 | tf_op jit(solution)/shard_map/ppermute | solution.py:19
  52.5 3.6 %collective-permute-done.11.refs_0_ = bf16[32,2048]{1,0:T(8,128)(2,1)S(1)} collective-permute-done((bf16[32,2048]{1,0:T(8,128)(2,1)S(1)}, bf16[32,2048]{1,0:T(8,128)(2,1)S(1)}, u32[]{:S(2)}, u32[]{:S(2)}) %collective-permute-start.11) | collective-permute-done | bytes 131104 | tf_op jit(solution)/shard_map/ppermute | solution.py:19
  57.2 2.0 %collective-permute-start.14 = (bf16[8,1664]{1,0:T(8,128)(2,1)S(1)}, bf16[8,1664]{1,0:T(8,128)(2,1)S(1)}, u32[]{:S(2)}, u32[]{:S(2)}) collective-permute-start(bf16[8,1664]{1,0:T(8,128)(2,1)S(1)} %get-tuple-element.60), channel_id=1, source_target_pairs={{0,1},{1,0},{2,3},{3,2},{4,5},{5,4},{6,7},{7,6},{8,9},{9,8},{10,11... | collective-permute-start | bytes 79880 | tf_op jit(solution)/shard_map/ppermute | solution.py:19
  59.3 2.4 %collective-permute-start.16 = (bf16[8,1664]{1,0:T(8,128)(2,1)S(1)}, bf16[8,1664]{1,0:T(8,128)(2,1)S(1)}, u32[]{:S(2)}, u32[]{:S(2)}) collective-permute-start(bf16[8,1664]{1,0:T(8,128)(2,1)S(1)} %get-tuple-element.62), channel_id=1, source_target_pairs={{0,3},{1,2},{2,1},{3,0},{4,7},{5,6},{6,5},{7,4},{8,11},{9,10},{10,... | collective-permute-start | bytes 79880 | tf_op jit(solution)/shard_map/ppermute | solution.py:19
  62.4 1.6 %collective-permute-done.15.refs_6_ = bf16[8,1664]{1,0:T(8,128)(2,1)S(1)} collective-permute-done((bf16[8,1664]{1,0:T(8,128)(2,1)S(1)}, bf16[8,1664]{1,0:T(8,128)(2,1)S(1)}, u32[]{:S(2)}, u32[]{:S(2)}) %collective-permute-start.15) | collective-permute-done | bytes 26656 | tf_op jit(solution)/shard_map/ppermute | solution.py:19
  64.9 3.9 %sweeps.1 = (bf16[16,1152]{1,0:T(8,128)(2,1)S(1)}, bf16[16,1152]{1,0:T(8,128)(2,1)S(1)}, bf16[16,1152]{1,0:T(8,128)(2,1)S(1)}, bf16[16,1152]{1,0:T(8,128)(2,1)S(1)}) custom-call(f32[16]{0:T(128)S(1)} %pad_maximum_fusion.1.steps, f32[4,8,1152]{2,1,0:T(8,128)S(1)} %bitcast.8, f32[8,1536]{1,0:T(8,128)S(1)} %pad_maximum_fusion.embed_ref, ...), custom_call_target="tpu_custom_call" | custom-call | flops 1132462080 | bytes 7077888 | tf_op jit(solution)/shard_map/sweeps/pallas_call | solution.py:636
  68.9 3.0 %collective-permute-start.18 = (bf16[16,1152]{1,0:T(8,128)(2,1)S(1)}, bf16[16,1152]{1,0:T(8,128)(2,1)S(1)}, u32[]{:S(2)}, u32[]{:S(2)}) collective-permute-start(bf16[16,1152]{1,0:T(8,128)(2,1)S(1)} %get-tuple-element.65), channel_id=1, source_target_pairs={{0,2},{1,3},{2,0},{3,1},{4,6},{5,7},{6,4},{7,5},{8,10},{9,11},{10,... | collective-permute-start | bytes 110600 | tf_op jit(solution)/shard_map/ppermute | solution.py:19
  71.9 1.4 %collective-permute-start.19 = (bf16[16,1152]{1,0:T(8,128)(2,1)S(1)}, bf16[16,1152]{1,0:T(8,128)(2,1)S(1)}, u32[]{:S(2)}, u32[]{:S(2)}) collective-permute-start(bf16[16,1152]{1,0:T(8,128)(2,1)S(1)} %get-tuple-element.66), channel_id=1, source_target_pairs={{0,3},{1,2},{2,1},{3,0},{4,7},{5,6},{6,5},{7,4},{8,11},{9,10},{10,... | collective-permute-start | bytes 110600 | tf_op jit(solution)/shard_map/ppermute | solution.py:19
  74.3 3.4 %collective-permute-done.19.refs_3_ = bf16[16,1152]{1,0:T(8,128)(2,1)S(1)} collective-permute-done((bf16[16,1152]{1,0:T(8,128)(2,1)S(1)}, bf16[16,1152]{1,0:T(8,128)(2,1)S(1)}, u32[]{:S(2)}, u32[]{:S(2)}) %collective-permute-start.19) | collective-permute-done | bytes 36896 | tf_op jit(solution)/shard_map/ppermute | solution.py:19
  (69 shorter events, 14.0 us)
Async XLA Ops:
  0.0 45.1 %collective-permute-start.9 = (bf16[2048,384]{1,0:T(8,128)(2,1)}, bf16[2048,384]{1,0:T(8,128)(2,1)S(1)}, u32[]{:S(2)}, u32[]{:S(2)}) collective-permute-start(bf16[2048,384]{1,0:T(8,128)(2,1)} %refs_1_.1), channel_id=1, source_target_pairs={{0,8},{4,12},{8,0},{12,4},{1,9},{5,13},{9,1},{13,5},{2,10},{6,14},... | collective-permute-start | bytes 4718600 | tf_op jit(solution)/shard_map/ppermute | solution.py:19
  5.3 31.7 %slice-start = ((s8[8388608]{0:T(1024)(128)(4,1)}), s8[4194304]{0:T(1024)(128)(4,1)S(1)}, s32[]{:S(2)}) async-start(s8[8388608]{0:T(1024)(128)(4,1)} %bitcast.5), calls=%async_computation | async-start | bytes 8388608
  11.5 23.6 %copy-start.4 = (bf16[2048,384]{1,0:T(8,128)(2,1)S(1)}, bf16[2048,384]{1,0:T(8,128)(2,1)}, u32[]{:S(2)}) copy-start(bf16[2048,384]{1,0:T(8,128)(2,1)} %refs_1_.1) | copy-start | bytes 4718596
  11.5 25.5 %slice-start.1 = ((s8[8388608]{0:T(1024)(128)(4,1)}), s8[4194304]{0:T(1024)(128)(4,1)S(1)}, s32[]{:S(2)}) async-start(s8[8388608]{0:T(1024)(128)(4,1)} %bitcast.5), calls=%async_computation.1 | async-start | bytes 8388608
  15.1 6.9 %collective-permute-start.3 = (bf16[136,512]{1,0:T(8,128)(2,1)S(1)}, bf16[136,512]{1,0:T(8,128)(2,1)S(1)}, u32[]{:S(2)}, u32[]{:S(2)}) collective-permute-start(bf16[136,512]{1,0:T(8,128)(2,1)S(1)} %get-tuple-element.48), channel_id=1, source_target_pairs={{0,1},{1,0},{2,3},{3,2},{4,5},{5,4},{6,7},{7,6},{8,9},{9,8},{10,11... | collective-permute-start | bytes 417800 | tf_op jit(solution)/shard_map/ppermute | solution.py:19
  16.8 13.3 %collective-permute-start.4 = (bf16[136,512]{1,0:T(8,128)(2,1)S(1)}, bf16[136,512]{1,0:T(8,128)(2,1)S(1)}, u32[]{:S(2)}, u32[]{:S(2)}) collective-permute-start(bf16[136,512]{1,0:T(8,128)(2,1)S(1)} %get-tuple-element.49), channel_id=1, source_target_pairs={{0,2},{1,3},{2,0},{3,1},{4,6},{5,7},{6,4},{7,5},{8,10},{9,11},{10,... | collective-permute-start | bytes 417800 | tf_op jit(solution)/shard_map/ppermute | solution.py:19
  19.3 10.7 %collective-permute-start.5 = (bf16[136,512]{1,0:T(8,128)(2,1)S(1)}, bf16[136,512]{1,0:T(8,128)(2,1)S(1)}, u32[]{:S(2)}, u32[]{:S(2)}) collective-permute-start(bf16[136,512]{1,0:T(8,128)(2,1)S(1)} %copy-done.13), channel_id=1, source_target_pairs={{0,3},{1,2},{2,1},{3,0},{4,7},{5,6},{6,5},{7,4},{8,11},{9,10},{10,... | collective-permute-start | bytes 417800 | tf_op jit(solution)/shard_map/ppermute | solution.py:19
  30.5 6.5 %collective-permute-start.6 = (bf16[128,512]{1,0:T(8,128)(2,1)S(1)}, bf16[128,512]{1,0:T(8,128)(2,1)S(1)}, u32[]{:S(2)}, u32[]{:S(2)}) collective-permute-start(bf16[128,512]{1,0:T(8,128)(2,1)S(1)} %merge.1.refs_0_), channel_id=1, source_target_pairs={{0,1},{1,0},{2,3},{3,2},{4,5},{5,4},{6,7},{7,6},{8,9},{9,8},{10,11... | collective-permute-start | bytes 393224 | tf_op jit(solution)/shard_map/ppermute | solution.py:19
  32.7 11.7 %collective-permute-start.7 = (bf16[128,512]{1,0:T(8,128)(2,1)S(1)}, bf16[128,512]{1,0:T(8,128)(2,1)S(1)}, u32[]{:S(2)}, u32[]{:S(2)}) collective-permute-start(bf16[128,512]{1,0:T(8,128)(2,1)S(1)} %merge.1.refs_0_), channel_id=1, source_target_pairs={{0,2},{1,3},{2,0},{3,1},{4,6},{5,7},{6,4},{7,5},{8,10},{9,11},{10,... | collective-permute-start | bytes 393224 | tf_op jit(solution)/shard_map/ppermute | solution.py:19
  33.7 10.6 %collective-permute-start.8 = (bf16[128,512]{1,0:T(8,128)(2,1)S(1)}, bf16[128,512]{1,0:T(8,128)(2,1)S(1)}, u32[]{:S(2)}, u32[]{:S(2)}) collective-permute-start(bf16[128,512]{1,0:T(8,128)(2,1)S(1)} %merge.1.refs_0_), channel_id=1, source_target_pairs={{0,3},{1,2},{2,1},{3,0},{4,7},{5,6},{6,5},{7,4},{8,11},{9,10},{10,... | collective-permute-start | bytes 393224 | tf_op jit(solution)/shard_map/ppermute | solution.py:19
  35.1 16.0 %collective-permute-start.12 = (bf16[2048,384]{1,0:T(8,128)(2,1)S(1)}, bf16[2048,384]{1,0:T(8,128)(2,1)S(1)}, u32[]{:S(2)}, u32[]{:S(2)}) collective-permute-start(bf16[2048,384]{1,0:T(8,128)(2,1)S(1)} %copy-done.4), channel_id=1, source_target_pairs={{0,4},{4,0},{8,12},{12,8},{1,5},{5,1},{9,13},{13,9},{2,6},{6,2},{1... | collective-permute-start | bytes 4718600 | tf_op jit(solution)/shard_map/ppermute | solution.py:19
  38.6 17.5 %copy-start.8 = (bf16[128,2048]{1,0:T(8,128)(2,1)S(1)}, bf16[128,2048]{1,0:T(8,128)(2,1)}, u32[]{:S(2)}) copy-start(bf16[128,2048]{1,0:T(8,128)(2,1)} %param.17) | copy-start | bytes 1572868
  45.1 11.0 %collective-permute-start.13 = (bf16[2048,384]{1,0:T(8,128)(2,1)S(1)}, bf16[2048,384]{1,0:T(8,128)(2,1)S(1)}, u32[]{:S(2)}, u32[]{:S(2)}) collective-permute-start(bf16[2048,384]{1,0:T(8,128)(2,1)S(1)} %collective-permute-done.9.refs_3_), channel_id=1, source_target_pairs={{0,4},{4,0},{8,12},{12,8},{1,5},{5,1},{9,13},{13,9},{2,6},{6,2},{1... | collective-permute-start | bytes 4718600 | tf_op jit(solution)/shard_map/ppermute | solution.py:19
  45.6 13.7 %collective-permute-start = (bf16[16,1152]{1,0:T(8,128)(2,1)S(1)}, bf16[16,1152]{1,0:T(8,128)(2,1)S(1)}, u32[]{:S(2)}, u32[]{:S(2)}) collective-permute-start(bf16[16,1152]{1,0:T(8,128)(2,1)S(1)} %get-tuple-element.37), channel_id=1, source_target_pairs={{0,1},{1,0},{2,3},{3,2},{4,5},{5,4},{6,7},{7,6},{8,9},{9,8},{10,11... | collective-permute-start | bytes 110600 | tf_op jit(solution)/shard_map/ppermute | solution.py:19
  47.6 14.7 %collective-permute-start.1 = (bf16[16,1152]{1,0:T(8,128)(2,1)S(1)}, bf16[16,1152]{1,0:T(8,128)(2,1)S(1)}, u32[]{:S(2)}, u32[]{:S(2)}) collective-permute-start(bf16[16,1152]{1,0:T(8,128)(2,1)S(1)} %get-tuple-element.38), channel_id=1, source_target_pairs={{0,2},{1,3},{2,0},{3,1},{4,6},{5,7},{6,4},{7,5},{8,10},{9,11},{10,... | collective-permute-start | bytes 110600 | tf_op jit(solution)/shard_map/ppermute | solution.py:19
  48.9 1.5 %collective-permute-start.10 = (bf16[2,32,2048]{2,1,0:T(8,128)(2,1)S(1)}, bf16[2,32,2048]{2,1,0:T(8,128)(2,1)S(1)}, u32[]{:S(2)}, u32[]{:S(2)}) collective-permute-start(bf16[2,32,2048]{2,1,0:T(8,128)(2,1)S(1)} %get-tuple-element.55), channel_id=1, source_target_pairs={{0,4},{4,0},{8,12},{12,8},{1,5},{5,1},{9,13},{13,9},{2,6},{6,2},{1... | collective-permute-start | bytes 786440 | tf_op jit(solution)/shard_map/ppermute | solution.py:19
  50.5 5.7 %collective-permute-start.11 = (bf16[32,2048]{1,0:T(8,128)(2,1)S(1)}, bf16[32,2048]{1,0:T(8,128)(2,1)S(1)}, u32[]{:S(2)}, u32[]{:S(2)}) collective-permute-start(bf16[32,2048]{1,0:T(8,128)(2,1)S(1)} %get-tuple-element.57), channel_id=1, source_target_pairs={{0,8},{4,12},{8,0},{12,4},{1,9},{5,13},{9,1},{13,5},{2,10},{6,14},... | collective-permute-start | bytes 393224 | tf_op jit(solution)/shard_map/ppermute | solution.py:19
  51.1 11.3 %collective-permute-start.2 = (bf16[16,1152]{1,0:T(8,128)(2,1)S(1)}, bf16[16,1152]{1,0:T(8,128)(2,1)S(1)}, u32[]{:S(2)}, u32[]{:S(2)}) collective-permute-start(bf16[16,1152]{1,0:T(8,128)(2,1)S(1)} %get-tuple-element.39), channel_id=1, source_target_pairs={{0,3},{1,2},{2,1},{3,0},{4,7},{5,6},{6,5},{7,4},{8,11},{9,10},{10,... | collective-permute-start | bytes 110600 | tf_op jit(solution)/shard_map/ppermute | solution.py:19
  57.2 5.1 %collective-permute-start.14 = (bf16[8,1664]{1,0:T(8,128)(2,1)S(1)}, bf16[8,1664]{1,0:T(8,128)(2,1)S(1)}, u32[]{:S(2)}, u32[]{:S(2)}) collective-permute-start(bf16[8,1664]{1,0:T(8,128)(2,1)S(1)} %get-tuple-element.60), channel_id=1, source_target_pairs={{0,1},{1,0},{2,3},{3,2},{4,5},{5,4},{6,7},{7,6},{8,9},{9,8},{10,11... | collective-permute-start | bytes 79880 | tf_op jit(solution)/shard_map/ppermute | solution.py:19
  59.2 4.7 %collective-permute-start.15 = (bf16[8,1664]{1,0:T(8,128)(2,1)S(1)}, bf16[8,1664]{1,0:T(8,128)(2,1)S(1)}, u32[]{:S(2)}, u32[]{:S(2)}) collective-permute-start(bf16[8,1664]{1,0:T(8,128)(2,1)S(1)} %get-tuple-element.61), channel_id=1, source_target_pairs={{0,2},{1,3},{2,0},{3,1},{4,6},{5,7},{6,4},{7,5},{8,10},{9,11},{10,... | collective-permute-start | bytes 79880 | tf_op jit(solution)/shard_map/ppermute | solution.py:19
  59.3 5.6 %collective-permute-start.16 = (bf16[8,1664]{1,0:T(8,128)(2,1)S(1)}, bf16[8,1664]{1,0:T(8,128)(2,1)S(1)}, u32[]{:S(2)}, u32[]{:S(2)}) collective-permute-start(bf16[8,1664]{1,0:T(8,128)(2,1)S(1)} %get-tuple-element.62), channel_id=1, source_target_pairs={{0,3},{1,2},{2,1},{3,0},{4,7},{5,6},{6,5},{7,4},{8,11},{9,10},{10,... | collective-permute-start | bytes 79880 | tf_op jit(solution)/shard_map/ppermute | solution.py:19
  68.9 4.5 %collective-permute-start.17 = (bf16[16,1152]{1,0:T(8,128)(2,1)S(1)}, bf16[16,1152]{1,0:T(8,128)(2,1)S(1)}, u32[]{:S(2)}, u32[]{:S(2)}) collective-permute-start(bf16[16,1152]{1,0:T(8,128)(2,1)S(1)} %get-tuple-element.64), channel_id=1, source_target_pairs={{0,1},{1,0},{2,3},{3,2},{4,5},{5,4},{6,7},{7,6},{8,9},{9,8},{10,11... | collective-permute-start | bytes 110600 | tf_op jit(solution)/shard_map/ppermute | solution.py:19
  68.9 5.3 %collective-permute-start.18 = (bf16[16,1152]{1,0:T(8,128)(2,1)S(1)}, bf16[16,1152]{1,0:T(8,128)(2,1)S(1)}, u32[]{:S(2)}, u32[]{:S(2)}) collective-permute-start(bf16[16,1152]{1,0:T(8,128)(2,1)S(1)} %get-tuple-element.65), channel_id=1, source_target_pairs={{0,2},{1,3},{2,0},{3,1},{4,6},{5,7},{6,4},{7,5},{8,10},{9,11},{10,... | collective-permute-start | bytes 110600 | tf_op jit(solution)/shard_map/ppermute | solution.py:19
  71.9 5.8 %collective-permute-start.19 = (bf16[16,1152]{1,0:T(8,128)(2,1)S(1)}, bf16[16,1152]{1,0:T(8,128)(2,1)S(1)}, u32[]{:S(2)}, u32[]{:S(2)}) collective-permute-start(bf16[16,1152]{1,0:T(8,128)(2,1)S(1)} %get-tuple-element.66), channel_id=1, source_target_pairs={{0,3},{1,2},{2,1},{3,0},{4,7},{5,6},{6,5},{7,4},{8,11},{9,10},{10,... | collective-permute-start | bytes 110600 | tf_op jit(solution)/shard_map/ppermute | solution.py:19
  (13 other events, 70.6 us)
